TPU v7x, 8 devices: a whole 2x2x1 slice. The times are simulated.
8 devices in a mesh: exam: 1 (over z), cols: 2 (over y), rows: 4 (over x, core).
Axes of the slice: x: 2, y: 2, z: 1, core: 2. Of those that a mesh axis runs over, the one named last changes fastest.
Arguments:
- kspace: float32 [2, 8, 16384], P(None, None, ('exam', 'rows', 'cols'))
- wts_y: float32 [4, 16384], P(None, ('exam', 'rows', 'cols'))
- wts_x: float32 [4, 16384], P(None, ('exam', 'rows', 'cols'))
- idx_y: int32 [16384], P(('exam', 'rows', 'cols'))
- idx_x: int32 [16384], P(('exam', 'rows', 'cols'))
- coil_maps: float32 [2, 8, 368, 368], P(None, ('exam', 'cols'), None, 'rows')
- deapod: float32 [368], replicated
Outputs:
- output: float32 [2, 368, 368], P(None, ('exam', 'cols'), 'rows')
All inputs are finite; a program needn't handle non-finite values.
Results may differ from a plain program's by a relative error of at most 0.001.
Values are sent between devices in bfloat16 or wider.
A program may use at most 1 GiB of HBM per device.

v0:
```python
import math
import jax
import jax.numpy as jnp
from jax import lax
from jax.sharding import PartitionSpec as P


def dft_matrix(n_img, n_grid):
    freq_idx = jnp.arange(n_grid) - n_grid // 2
    pos_idx = jnp.arange(n_img) - n_img // 2
    phase_int = (freq_idx[:, None] * pos_idx[None, :]) % n_grid
    phase_ang = phase_int.astype(jnp.float32) * (2.0 * math.pi / n_grid)
    dft_norm = 1.0 / math.sqrt(n_grid)
    cos_t = jnp.cos(phase_ang) * dft_norm
    sin_t = jnp.sin(phase_ang) * dft_norm
    upper_half = jnp.stack([cos_t, sin_t], axis=1)
    lower_half = jnp.stack([-sin_t, cos_t], axis=1)
    return jnp.stack([upper_half, lower_half], axis=0).astype(jnp.bfloat16)


def tap_matrix(tap_off, weights):
    tap_ids = jnp.arange(weights.shape[0]).reshape((-1,) + (1,) * tap_off.ndim)
    return jnp.sum(jnp.where(tap_off[None] == tap_ids, weights[..., None, :], 0.0), axis=0)


def spread_block(kspace, wts_y, wts_x, row_loc, col_loc, row_len, col_len):
    n_coils = kspace.shape[1]
    kern_width = wts_y.shape[0]
    n_slots = kspace.shape[2]
    tile_len = math.gcd(n_slots, 256)
    n_steps = n_slots // tile_len
    tile_data = (
        jnp.moveaxis(kspace.reshape(2, n_coils, n_steps, tile_len), 2, 0),
        jnp.moveaxis(wts_y.reshape(kern_width, n_steps, tile_len), 1, 0),
        jnp.moveaxis(wts_x.reshape(kern_width, n_steps, tile_len), 1, 0),
        row_loc.reshape(n_steps, tile_len),
        col_loc.reshape(n_steps, tile_len),
    )
    row_pos = jnp.arange(row_len)[:, None]
    col_pos = jnp.arange(col_len)[:, None]

    def add_tile(acc_buf, tile_in):
        samp_t, wy_t, wx_t, ry_t, rx_t = tile_in
        row_mat = tap_matrix(row_pos - ry_t[None, :], wy_t)
        col_mat = tap_matrix(col_pos - rx_t[None, :], wx_t)
        scaled = samp_t[:, :, None, :] * row_mat
        return acc_buf + jnp.einsum('sclm,km->sclk', scaled, col_mat, precision=lax.Precision.HIGHEST, preferred_element_type=jnp.float32), None

    start_buf = jnp.zeros((2, n_coils, row_len, col_len), jnp.float32)
    spread_buf, _ = lax.scan(add_tile, start_buf, tile_data)
    return spread_buf


def fold_ghosts(spread_buf, axis, axis_name, n_dev, half_w, core_len):
    lead_band, head_band, body_band, tail_band, trail_band = jnp.split(spread_buf, [half_w, 2 * half_w, core_len, core_len + half_w], axis=axis)
    to_prev = [(k, (k - 1) % n_dev) for k in range(n_dev)]
    to_next = [(k, (k + 1) % n_dev) for k in range(n_dev)]
    from_next = lax.ppermute(lead_band, axis_name, to_prev)
    from_prev = lax.ppermute(trail_band, axis_name, to_next)
    return jnp.concatenate([head_band + from_prev, body_band, tail_band + from_next], axis=axis)


def solution(mesh):
    n_rows = mesh.shape['rows']
    n_cols = mesh.shape['cols']
    sample_spec = ('exam', 'rows', 'cols')

    def local_fn(kspace, wts_y, wts_x, idx_y, idx_x, coil_maps, deapod):
        kern_width = wts_y.shape[0]
        half_w = kern_width // 2
        n_img = deapod.shape[0]
        n_grid = 2 * n_img
        row_blk = n_grid // n_rows
        col_blk = n_grid // n_cols
        row_id = lax.axis_index('rows')
        col_id = lax.axis_index('cols')
        spread_buf = spread_block(kspace, wts_y, wts_x, idx_y - row_id * row_blk, idx_x - col_id * col_blk, row_blk + kern_width, col_blk + kern_width)
        spread_buf = fold_ghosts(spread_buf, 2, 'rows', n_rows, half_w, row_blk)
        spread_buf = fold_ghosts(spread_buf, 3, 'cols', n_cols, half_w, col_blk)
        k_grid = lax.all_to_all(spread_buf.astype(jnp.bfloat16), 'cols', 1, 3, tiled=True)
        dft_mat = dft_matrix(n_img, n_grid)
        half_img = jnp.einsum('scuv,svtq->tcuq', k_grid, dft_mat, preferred_element_type=jnp.float32).astype(jnp.bfloat16)
        half_img = lax.all_to_all(half_img, 'rows', 3, 2, tiled=True)
        coil_img = jnp.einsum('tcuq,tuop->ocpq', half_img, dft_mat, preferred_element_type=jnp.float32)
        part_re = jnp.sum(coil_maps[0] * coil_img[0] + coil_maps[1] * coil_img[1], axis=0)
        part_im = jnp.sum(coil_maps[0] * coil_img[1] - coil_maps[1] * coil_img[0], axis=0)
        combined = lax.psum_scatter(jnp.stack([part_re, part_im]), 'cols', scatter_dimension=1, tiled=True)
        d_rows = deapod.reshape(n_cols, n_img // n_cols)[col_id]
        d_cols = deapod.reshape(n_rows, n_img // n_rows)[row_id]
        return combined * (d_rows[:, None] * d_cols[None, :])

    return jax.shard_map(
        local_fn,
        mesh=mesh,
        in_specs=(P(None, None, sample_spec), P(None, sample_spec), P(None, sample_spec), P(sample_spec), P(sample_spec), P(None, ('exam', 'cols'), None, 'rows'), P()),
        out_specs=P(None, ('exam', 'cols'), 'rows'),
        check_vma=False,
    )
```

profile of v0, /device:TPU:0, one launch (start us, length us, event | category | flops | bytes accessed | tf_op | source)
XLA Modules:
  0.0 249.5 jit_solution(8755154398662131029)
XLA Ops:
  6.5 0.7 broadcast_subtract_fusion
  7.2 0.7 broadcast_subtract_fusion.1
  7.9 0.9 copy.94
  8.9 84.7 %while.11 = (s32[]{:T(128)}, f32[2,8,188,372]{3,2,1,0:T(8,128)}, f32[8,2,8,256]{3,0,2,1:T(8,128)S(1)}, s32[8,256]{1,0:T(8,128)S(1)}, f32[8,4,256]{2,1,0:T(4,128)...) while((s32[]{:T(128)}, f32[2,8,188,372]{3,2,1,0:T(8,128)}, ...), condition=%wide.region_3.4_spmd.clone, body=%wide.region_0.3_spmd.clone.sunk | while | flops 3442222592 | bytes 11358323 | solution.py:50
  9.0 0.7 dynamic-slice_bitcast_fusion.4
  9.7 1.0 select_reduce_fusion.5
  11.3 6.8 %select_add_fusion.2 = f32[2,8,188,372]{3,2,1,0:T(8,128)} fusion(f32[2,8,188,372]{3,2,1,0:T(8,128)} %get-tuple-element.199, pred[]{:T(512)S(6)} %compare.3, f32[188,256]{1,0:T(8,128)S(1)} %select_reduce_fusion.4, f32[2,8,256]{2,1,0:T(8,128)S(1)} %bitcast.95, f32[372,256]{1,0:T(8,128)S(1)} %select_reduce_fusion.5), kind=kOutput, calls=%fused_computation.2.clone.1 | convolution fusion | flops 3440502272 | bytes 9541633 | tf_op jit(solution)/shard_map/while/body/eval_jaxpr/sclm,km->sclk/dot_general | solution.py:47
  18.1 0.7 dynamic-slice_bitcast_fusion.4
  18.8 1.0 select_reduce_fusion.5
  19.9 0.5 select_reduce_fusion.4
  20.5 8.4 %select_add_fusion.2 = f32[2,8,188,372]{3,2,1,0:T(8,128)} fusion(f32[2,8,188,372]{3,2,1,0:T(8,128)} %get-tuple-element.199, pred[]{:T(512)S(6)} %compare.3, f32[188,256]{1,0:T(8,128)S(1)} %select_reduce_fusion.4, f32[2,8,256]{2,1,0:T(8,128)S(1)} %bitcast.95, f32[372,256]{1,0:T(8,128)S(1)} %select_reduce_fusion.5), kind=kOutput, calls=%fused_computation.2.clone.1 | convolution fusion | flops 3440502272 | bytes 9541633 | tf_op jit(solution)/shard_map/while/body/eval_jaxpr/sclm,km->sclk/dot_general | solution.py:47
  28.9 0.7 dynamic-slice_bitcast_fusion.4
  29.6 1.0 select_reduce_fusion.5
  31.2 8.4 %select_add_fusion.2 = f32[2,8,188,372]{3,2,1,0:T(8,128)} fusion(f32[2,8,188,372]{3,2,1,0:T(8,128)} %get-tuple-element.199, pred[]{:T(512)S(6)} %compare.3, f32[188,256]{1,0:T(8,128)S(1)} %select_reduce_fusion.4, f32[2,8,256]{2,1,0:T(8,128)S(1)} %bitcast.95, f32[372,256]{1,0:T(8,128)S(1)} %select_reduce_fusion.5), kind=kOutput, calls=%fused_computation.2.clone.1 | convolution fusion | flops 3440502272 | bytes 9541633 | tf_op jit(solution)/shard_map/while/body/eval_jaxpr/sclm,km->sclk/dot_general | solution.py:47
  39.7 0.7 dynamic-slice_bitcast_fusion.4
  40.4 1.0 select_reduce_fusion.5
  42.0 8.4 %select_add_fusion.2 = f32[2,8,188,372]{3,2,1,0:T(8,128)} fusion(f32[2,8,188,372]{3,2,1,0:T(8,128)} %get-tuple-element.199, pred[]{:T(512)S(6)} %compare.3, f32[188,256]{1,0:T(8,128)S(1)} %select_reduce_fusion.4, f32[2,8,256]{2,1,0:T(8,128)S(1)} %bitcast.95, f32[372,256]{1,0:T(8,128)S(1)} %select_reduce_fusion.5), kind=kOutput, calls=%fused_computation.2.clone.1 | convolution fusion | flops 3440502272 | bytes 9541633 | tf_op jit(solution)/shard_map/while/body/eval_jaxpr/sclm,km->sclk/dot_general | solution.py:47
  50.5 0.7 dynamic-slice_bitcast_fusion.4
  51.2 1.0 select_reduce_fusion.5
  52.8 8.4 %select_add_fusion.2 = f32[2,8,188,372]{3,2,1,0:T(8,128)} fusion(f32[2,8,188,372]{3,2,1,0:T(8,128)} %get-tuple-element.199, pred[]{:T(512)S(6)} %compare.3, f32[188,256]{1,0:T(8,128)S(1)} %select_reduce_fusion.4, f32[2,8,256]{2,1,0:T(8,128)S(1)} %bitcast.95, f32[372,256]{1,0:T(8,128)S(1)} %select_reduce_fusion.5), kind=kOutput, calls=%fused_computation.2.clone.1 | convolution fusion | flops 3440502272 | bytes 9541633 | tf_op jit(solution)/shard_map/while/body/eval_jaxpr/sclm,km->sclk/dot_general | solution.py:47
  61.3 0.7 dynamic-slice_bitcast_fusion.4
  62.0 1.0 select_reduce_fusion.5
  63.6 8.4 %select_add_fusion.2 = f32[2,8,188,372]{3,2,1,0:T(8,128)} fusion(f32[2,8,188,372]{3,2,1,0:T(8,128)} %get-tuple-element.199, pred[]{:T(512)S(6)} %compare.3, f32[188,256]{1,0:T(8,128)S(1)} %select_reduce_fusion.4, f32[2,8,256]{2,1,0:T(8,128)S(1)} %bitcast.95, f32[372,256]{1,0:T(8,128)S(1)} %select_reduce_fusion.5), kind=kOutput, calls=%fused_computation.2.clone.1 | convolution fusion | flops 3440502272 | bytes 9541633 | tf_op jit(solution)/shard_map/while/body/eval_jaxpr/sclm,km->sclk/dot_general | solution.py:47
  72.1 0.7 dynamic-slice_bitcast_fusion.4
  72.8 1.0 select_reduce_fusion.5
  74.4 8.4 %select_add_fusion.2 = f32[2,8,188,372]{3,2,1,0:T(8,128)} fusion(f32[2,8,188,372]{3,2,1,0:T(8,128)} %get-tuple-element.199, pred[]{:T(512)S(6)} %compare.3, f32[188,256]{1,0:T(8,128)S(1)} %select_reduce_fusion.4, f32[2,8,256]{2,1,0:T(8,128)S(1)} %bitcast.95, f32[372,256]{1,0:T(8,128)S(1)} %select_reduce_fusion.5), kind=kOutput, calls=%fused_computation.2.clone.1 | convolution fusion | flops 3440502272 | bytes 9541633 | tf_op jit(solution)/shard_map/while/body/eval_jaxpr/sclm,km->sclk/dot_general | solution.py:47
  82.9 0.7 dynamic-slice_bitcast_fusion.4
  83.6 1.0 select_reduce_fusion.5
  85.2 8.4 %select_add_fusion.2 = f32[2,8,188,372]{3,2,1,0:T(8,128)} fusion(f32[2,8,188,372]{3,2,1,0:T(8,128)} %get-tuple-element.199, pred[]{:T(512)S(6)} %compare.3, f32[188,256]{1,0:T(8,128)S(1)} %select_reduce_fusion.4, f32[2,8,256]{2,1,0:T(8,128)S(1)} %bitcast.95, f32[372,256]{1,0:T(8,128)S(1)} %select_reduce_fusion.5), kind=kOutput, calls=%fused_computation.2.clone.1 | convolution fusion | flops 3440502272 | bytes 9541633 | tf_op jit(solution)/shard_map/while/body/eval_jaxpr/sclm,km->sclk/dot_general | solution.py:47
  93.6 5.0 %copy.56 = f32[2,8,188,372]{3,1,2,0:T(8,128)S(1)} copy(f32[2,8,188,372]{3,2,1,0:T(8,128)} %get-tuple-element.52) | data formatting | bytes 8951808 | tf_op jit(solution)/shard_map/while | solution.py:50
  98.6 0.9 collective-permute-start
  99.5 3.7 %collective-permute-done = f32[2,8,2,372]{3,1,2,0:T(8,128)S(1)} collective-permute-done((f32[2,8,2,372]{3,1,2,0:T(8,128)S(1)}, f32[2,8,2,372]{3,1,2,0:T(8,128)S(1)}, u32[]{:S(2)}, u32[]{:S(2)}) %collective-permute-start) | collective-permute-done | bytes 47648 | tf_op jit(solution)/shard_map/ppermute | solution.py:59
  103.5 6.6 %copy.58 = f32[2,8,188,372]{2,1,3,0:T(8,128)} copy(f32[2,8,188,372]{3,2,1,0:T(8,128)} %get-tuple-element.52) | data formatting | bytes 8951808 | tf_op jit(solution)/shard_map/while | solution.py:50
  110.1 7.0 %split.43 = f32[2,8,180,372]{2,1,3,0:T(8,128)} slice(f32[2,8,188,372]{2,1,3,0:T(8,128)} %copy.58), slice={[0:2], [0:8], [4:184], [0:372]} | slice | bytes 8570880 | tf_op jit(solution)/shard_map/split | solution.py:55
  117.1 2.6 %copy.61 = f32[2,8,2,372]{2,1,3,0:T(8,128)} copy(f32[2,8,2,372]{3,1,2,0:T(8,128)S(1)} %get-tuple-element.129) | data formatting | bytes 95232 | tf_op jit(solution)/shard_map/add | solution.py:60
  119.7 0.8 slice_add_fusion
  120.5 2.6 %copy.62 = f32[2,8,2,372]{2,1,3,0:T(8,128)} copy(f32[2,8,2,372]{3,1,2,0:T(8,128)S(1)} %slice_add_fusion) | data formatting | bytes 95232 | tf_op jit(solution)/shard_map/add | solution.py:60
  123.1 9.7 %pad_maximum_fusion = f32[2,8,184,372]{2,1,3,0:T(8,128)} fusion(f32[2,8,2,372]{2,1,3,0:T(8,128)} %copy.62, f32[2,8,180,372]{2,1,3,0:T(8,128)} %split.43, f32[2,8,2,372]{2,1,3,0:T(8,128)} %copy.61), kind=kLoop, calls=%fused_computation.20 | loop fusion | flops 2190336 | bytes 8761344 | tf_op jit(solution)/shard_map/concatenate | solution.py:60
  132.8 0.8 split.47
  133.5 2.1 collective-permute-start.2
  135.7 3.0 %split.55 = bf16[2,8,184,364]{2,1,3,0:T(8,128)(2,1)S(1)} slice(f32[2,8,184,372]{2,1,3,0:T(8,128)} %pad_maximum_fusion), slice={[0:2], [0:8], [0:184], [4:368]} | slice | bytes 4286464 | tf_op jit(solution)/shard_map/split | solution.py:55
  138.8 0.8 fusion.23
  139.6 3.1 %collective-permute-done.3 = f32[2,8,184,2]{2,1,3,0:T(8,128)S(1)} collective-permute-done((f32[2,8,184,2]{2,1,3,0:T(8,128)S(1)}, f32[2,8,184,2]{2,1,3,0:T(8,128)S(1)}, u32[]{:S(2)}, u32[]{:S(2)}) %collective-permute-start.3) | collective-permute-done | bytes 23584 | tf_op jit(solution)/shard_map/ppermute | solution.py:58
  142.8 0.6 pad_maximum_fusion.1
  143.3 3.3 %copy.63 = bf16[2,8,184,368]{3,2,0,1:T(8,128)(2,1)} copy(bf16[2,8,184,368]{2,1,3,0:T(8,128)(2,1)S(1)} %pad_maximum_fusion.1) | data formatting | bytes 4333568 | tf_op jit(solution)/shard_map/concatenate | solution.py:60
  146.7 3.8 %all-to-all-start = ((bf16[2,8,184,368]{3,2,0,1:T(8,128)(2,1)}), bf16[2,8,184,368]{3,2,0,1:T(8,128)(2,1)S(1)}, u32[]{:S(2)}, u32[]{:S(2)}) async-start(bf16[2,8,184,368]{3,2,0,1:T(8,128)(2,1)} %copy.63), calls=%async_computation | async-start | bytes 4521984 | tf_op jit(solution)/shard_map/all_to_all | solution.py:80
  150.5 5.4 %fusion.21 = (bf16[736,1,368]{2,0,1:T(8,128)(2,1)S(1)}, bf16[736,1,368]{2,0,1:T(8,128)(2,1)S(1)}, bf16[736,1,368]{2,0,1:T(8,128)(2,1)S(1)}) fusion(s32[368]{0:T(512)S(1)} %iota_add_fusion.1, s32[736]{0:T(1024)S(1)} %iota_add_fusion), kind=kLoop, calls=%fused_computation.44 | loop fusion | flops 4062720 | bytes 1629504 | tf_op jit(solution)/shard_map/convert.11
  155.9 1.5 maximum_bitcast_fusion.7
  157.4 18.9 %all-to-all-done = bf16[2,8,184,368]{3,2,0,1:T(8,128)(2,1)S(1)} async-done(((bf16[2,8,184,368]{3,2,0,1:T(8,128)(2,1)}), bf16[2,8,184,368]{3,2,0,1:T(8,128)(2,1)S(1)}, u32[]{:S(2)}, u32[]{:S(2)}) %all-to-all-start) | async-done | bytes 2166816 | tf_op jit(solution)/shard_map/all_to_all | solution.py:80
  176.3 3.7 %copy.92 = bf16[2,2,4,184,368]{4,1,3,0,2:T(2,128)(2,1)} copy(bf16[2,2,4,184,368]{4,3,0,2,1:T(8,128)(2,1)S(1)} %bitcast.91) | data formatting | bytes 4333568 | tf_op jit(solution)/shard_map/all_to_all | solution.py:80
  180.0 4.9 %reshape.293 = bf16[2,4,184,736,1]{3,2,0,1,4:T(8,128)(2,1)S(1)} reshape(bf16[2,4,184,2,368]{4,3,2,0,1:T(2,128)(2,1)} %bitcast.92) | data formatting | bytes 4333568 | tf_op jit(solution)/shard_map/all_to_all | solution.py:80
  184.9 4.2 %fusion.13 = bf16[2,4,184,368]{3,2,1,0:T(8,128)(2,1)} fusion(bf16[2,4,184,736,1]{3,2,0,1,4:T(8,128)(2,1)S(1)} %reshape.293, bf16[1,736,2,368]{3,1,0,2:T(8,128)(2,1)} %get-tuple-element.134, bf16[1,736,2,368]{3,1,0,2:T(8,128)(2,1)S(1)} %get-tuple-element.133), kind=kOutput, calls=%fused_computation.30 | convolution fusion | flops 1599628288 | bytes 5416960 | tf_op jit(solution)/shard_map/scuv,svtq->tcuq/dot_general | solution.py:82
  189.2 3.9 %copy.65 = bf16[2,4,184,368]{2,1,0,3:T(4,128)(2,1)} copy(bf16[2,4,184,368]{3,2,1,0:T(8,128)(2,1)} %fusion.13) | data formatting | bytes 2166784 | tf_op jit(solution)/shard_map/convert_element_type | solution.py:82
  193.0 3.6 %all-to-all-start.1 = ((bf16[2,4,184,368]{2,1,0,3:T(4,128)(2,1)}), bf16[2,4,184,368]{2,1,0,3:T(4,128)(2,1)S(1)}, u32[]{:S(2)}, u32[]{:S(2)}) async-start(bf16[2,4,184,368]{2,1,0,3:T(4,128)(2,1)} %copy.65), calls=%async_computation.1 | async-start | bytes 3014656 | tf_op jit(solution)/shard_map/all_to_all | solution.py:83
  196.8 1.2 fusion.26
  198.0 17.7 %all-to-all-done.1 = bf16[2,4,184,368]{2,1,0,3:T(4,128)(2,1)S(1)} async-done(((bf16[2,4,184,368]{2,1,0,3:T(4,128)(2,1)}), bf16[2,4,184,368]{2,1,0,3:T(4,128)(2,1)S(1)}, u32[]{:S(2)}, u32[]{:S(2)}) %all-to-all-start.1) | async-done | bytes 1083424 | tf_op jit(solution)/shard_map/all_to_all | solution.py:83
  215.7 1.2 copy.93
  216.9 1.4 all_to_all.33
  218.2 2.8 %fusion.12 = f32[2,4,368,92]{2,3,1,0:T(8,128)S(1)} fusion(bf16[1,736,2,368]{3,1,0,2:T(8,128)(2,1)} %get-tuple-element.134, bf16[1,736,2,368]{3,1,0,2:T(8,128)(2,1)} %copy-done.6, bf16[2,4,736,92]{2,3,1,0:T(8,128)(2,1)S(1)} %all_to_all.33), kind=kOutput, calls=%fused_computation.29 | convolution fusion | flops 801710080 | bytes 4333568 | tf_op jit(solution)/shard_map/tcuq,tuop->ocpq/dot_general | solution.py:84
  221.3 0.9 copy.69
  222.3 0.6 dynamic-slice
  223.6 17.4 %all-reduce.3.cloned.1.call-done = f32[2,368,92]{2,0,1:T(2,128)} async-done(((f32[2,368,92]{2,0,1:T(2,128)}), f32[2,368,92]{2,0,1:T(2,128)}) %all-reduce.3.cloned.1.call-update) | async-done | bytes 270864
  241.0 1.0 dynamic-slice_multiply_fusion
  242.0 0.7 copy.70
  (92 shorter events, 5.3 us)
Async XLA Ops:
  98.6 4.6 %copy-start.2 = (f32[2,8,188,372]{3,1,2,0:T(8,128)}, f32[2,8,188,372]{3,1,2,0:T(8,128)S(1)}, u32[]{:S(2)}) copy-start(f32[2,8,188,372]{3,1,2,0:T(8,128)S(1)} %copy.56) | copy-start | bytes 13427716
  98.6 4.6 %collective-permute-start = (f32[2,8,2,372]{3,1,2,0:T(8,128)S(1)}, f32[2,8,2,372]{3,1,2,0:T(8,128)S(1)}, u32[]{:S(2)}, u32[]{:S(2)}) collective-permute-start(f32[2,8,2,372]{3,1,2,0:T(8,128)S(1)} %split.42), channel_id=1, source_target_pairs={{0,1},{1,2},{2,3},{3,0},{4,5},{5,6},{6,7},{7,4}} | collective-permute-start | bytes 142856 | tf_op jit(solution)/shard_map/ppermute | solution.py:59
  103.2 16.4 %collective-permute-start.1 = (f32[2,8,2,372]{3,1,2,0:T(8,128)S(1)}, f32[2,8,2,372]{3,1,2,0:T(8,128)S(1)}, u32[]{:S(2)}, u32[]{:S(2)}) collective-permute-start(f32[2,8,2,372]{3,1,2,0:T(8,128)S(1)} %get-tuple-element.130), channel_id=1, source_target_pairs={{0,3},{1,0},{2,1},{3,2},{4,7},{5,4},{6,5},{7,6}} | collective-permute-start | bytes 142856 | tf_op jit(solution)/shard_map/ppermute | solution.py:58
  120.5 15.2 %slice-start = ((s8[6094848]{0:T(1024)(128)(4,1)}), s8[1900544]{0:T(1024)(128)(4,1)S(1)}, s32[]{:S(2)}) async-start(s8[6094848]{0:T(1024)(128)(4,1)} %bitcast.89), calls=%async_computation.3 | async-start | bytes 3801088
  123.1 12.6 %slice-start.1 = ((s8[6094848]{0:T(1024)(128)(4,1)}), s8[4194304]{0:T(1024)(128)(4,1)S(1)}, s32[]{:S(2)}) async-start(s8[6094848]{0:T(1024)(128)(4,1)} %bitcast.89), calls=%async_computation.4 | async-start | bytes 8388608
  123.1 12.6 %copy-start = (f32[2,8,2,372]{2,1,3,0:T(8,128)S(1)}, f32[2,8,2,372]{2,1,3,0:T(8,128)}, u32[]{:S(2)}) copy-start(f32[2,8,2,372]{2,1,3,0:T(8,128)} %copy.61) | copy-start | bytes 142852
  123.1 12.6 %copy-start.1 = (f32[2,8,2,372]{2,1,3,0:T(8,128)S(1)}, f32[2,8,2,372]{2,1,3,0:T(8,128)}, u32[]{:S(2)}) copy-start(f32[2,8,2,372]{2,1,3,0:T(8,128)} %copy.62) | copy-start | bytes 142852
  133.5 5.3 %collective-permute-start.2 = (f32[2,8,184,2]{2,1,3,0:T(8,128)S(1)}, f32[2,8,184,2]{2,1,3,0:T(8,128)S(1)}, u32[]{:S(2)}, u32[]{:S(2)}) collective-permute-start(f32[2,8,184,2]{2,1,3,0:T(8,128)S(1)} %split.47), channel_id=1, source_target_pairs={{0,4},{4,0},{1,5},{5,1},{2,6},{6,2},{3,7},{7,3}} | collective-permute-start | bytes 70664 | tf_op jit(solution)/shard_map/ppermute | solution.py:59
  138.7 3.9 %collective-permute-start.3 = (f32[2,8,184,2]{2,1,3,0:T(8,128)S(1)}, f32[2,8,184,2]{2,1,3,0:T(8,128)S(1)}, u32[]{:S(2)}, u32[]{:S(2)}) collective-permute-start(f32[2,8,184,2]{2,1,3,0:T(8,128)S(1)} %pad_maximum_fusion.3), channel_id=1, source_target_pairs={{0,4},{4,0},{1,5},{5,1},{2,6},{6,2},{3,7},{7,3}} | collective-permute-start | bytes 70664 | tf_op jit(solution)/shard_map/ppermute | solution.py:58
  146.7 29.7 %all-to-all-start = ((bf16[2,8,184,368]{3,2,0,1:T(8,128)(2,1)}), bf16[2,8,184,368]{3,2,0,1:T(8,128)(2,1)S(1)}, u32[]{:S(2)}, u32[]{:S(2)}) async-start(bf16[2,8,184,368]{3,2,0,1:T(8,128)(2,1)} %copy.63), calls=%async_computation | async-start | bytes 4521984 | tf_op jit(solution)/shard_map/all_to_all | solution.py:80
  157.4 27.5 %copy-start.6 = (bf16[1,736,2,368]{3,1,0,2:T(8,128)(2,1)}, bf16[1,736,2,368]{3,1,0,2:T(8,128)(2,1)S(1)}, u32[]{:S(2)}) copy-start(bf16[1,736,2,368]{3,1,0,2:T(8,128)(2,1)S(1)} %get-tuple-element.133) | copy-start | bytes 3250180
  189.2 7.5 %copy-start.7 = (f32[368]{0:T(512)S(1)}, f32[368]{0:T(512)}, u32[]{:S(2)}) copy-start(f32[368]{0:T(512)} %param.15) | copy-start | bytes 4420
  189.2 7.7 %copy-start.5 = (f32[2,4,368,92]{2,1,3,0:T(4,128)S(1)}, f32[2,4,368,92]{2,1,3,0:T(4,128)}, u32[]{:S(2)}) copy-start(f32[2,4,368,92]{2,1,3,0:T(4,128)} %param.14) | copy-start | bytes 3250180
  193.0 22.7 %all-to-all-start.1 = ((bf16[2,4,184,368]{2,1,0,3:T(4,128)(2,1)}), bf16[2,4,184,368]{2,1,0,3:T(4,128)(2,1)S(1)}, u32[]{:S(2)}, u32[]{:S(2)}) async-start(bf16[2,4,184,368]{2,1,0,3:T(4,128)(2,1)} %copy.65), calls=%async_computation.1 | async-start | bytes 3014656 | tf_op jit(solution)/shard_map/all_to_all | solution.py:83
  196.6 44.4 %all-reduce.3.cloned.1.call-start = ((), (), s32[]{:S(2)}) async-start(), calls=%async_computation.2 | async-start | bytes 753664
  218.2 2.8 %copy-start.3 = (f32[1,4,368,92]{2,1,3,0:T(4,128)S(1)}, f32[1,4,368,92]{2,1,3,0:T(4,128)}, u32[]{:S(2)}) copy-start(f32[1,4,368,92]{2,1,3,0:T(4,128)} %get-tuple-element.131) | copy-start | bytes 1625092
  218.2 2.8 %copy-start.4 = (f32[1,4,368,92]{2,1,3,0:T(4,128)S(1)}, f32[1,4,368,92]{2,1,3,0:T(4,128)}, u32[]{:S(2)}) copy-start(f32[1,4,368,92]{2,1,3,0:T(4,128)} %get-tuple-element.132) | copy-start | bytes 1625092
  221.0 1.2 copy-start.8
Sparse Core Ops, SparseCore 0:
  222.4 18.5 all-reduce.2
where the time goes:
time: 251 us; the launch traced here: 250 us
  matrix products  72.7 us (29%)
  waiting for transfers between devices  60.8 us (24%)
  local copies, waits for them, and re-layouts  56.3 us (22%)
  other arithmetic  34.4 us (14%)
  between operations  14.3 us (6%)
  starting transfers between devices  10.7 us (4%)
    dot_general x8, matrix products, add_tile(): jnp.einsum('sclm,km->sclk', scaled, col_mat, precision=lax.Precision.HIGH...  65.7 us
    all_to_all x1, waiting for transfers between devices, local_fn(): lax.all_to_all(spread_buf.astype(jnp.bfloat16), 'cols', 1, 3, tiled=True)  18.9 us
    all_to_all x1, waiting for transfers between devices, local_fn(): half_img = lax.all_to_all(half_img, 'rows', 3, 2, tiled=True)  17.7 us
    unnamed x2, waiting for transfers between devices  17.4 us
    reduce_sum x16, other arithmetic, tap_matrix(): jnp.sum(jnp.where(tap_off[None] == tap_ids, weights[..., None, :], 0.0),...  12.3 us
    while x2, local copies, waits for them, and re-layouts, spread_block(): spread_buf, _ = lax.scan(add_tile, start_buf, tile_data)  11.6 us
    split x4, local copies, waits for them, and re-layouts, fold_ghosts(): jnp.split(spread_buf, [half_w, 2 * half_w, core_len, core_len + half_w],...  10.7 us
    concatenate x2, other arithmetic, fold_ghosts(): jnp.concatenate([head_band + from_prev, body_band, tail_band + from_next]...  10.3 us
  transfers between devices with their start and end apart: 7, of which 5 were waited for; matrix products, arithmetic and copies ran while one was open for 12% of the time, Pallas kernels for 0%

commit v1 on v0

v1 whole, which is shorter than its diff:
```python
import functools
import math

import jax
import jax.numpy as jnp
import numpy as np
from jax import lax
from jax.experimental import pallas as pl
from jax.experimental.pallas import tpu as pltpu
from jax.sharding import PartitionSpec as P

F32, BF16 = jnp.float32, jnp.bfloat16
MESH = pl.DeviceIdType.MESH

N_IMG = 368
N_GRID = 736
ROW_BLK = 184
Q_BLK, Q_PAD = 92, 96
P_BLK, P_PAD = 184, 192
N_CH = 8
TILE_U, STRIDE_U, N_SRC = 16, 13, 15
N_TGT = 12
VR = 752
KV = 768
N_CHUNK = 6
N_COPY = 4
CHUNK_TILES = [(1 + 2 * j, 2 + 2 * j) for j in range(5)] + [(0, 11)]


def dft_constants():
    scale = 1.0 / math.sqrt(N_GRID)
    phase = ((np.arange(N_GRID)[:, None] - N_GRID // 2) * (np.arange(N_IMG)[None, :] - N_IMG // 2)) % N_GRID
    ang = phase.astype(np.float64) * (2.0 * math.pi / N_GRID)
    parts = (np.cos(ang) * scale, np.sin(ang) * scale)
    e1 = np.zeros((4, 2, Q_PAD, KV))
    for dest in range(4):
        for cs in range(2):
            e1[dest, cs, :Q_BLK, 6:6 + N_GRID] = parts[cs][:, dest * Q_BLK:(dest + 1) * Q_BLK].T
    e2 = np.zeros((N_CHUNK, 4, 2, TILE_U, 2, 2, P_PAD))
    for j in range(N_CHUNK):
        for src in range(4):
            for tl in range(2):
                base = TILE_U * CHUNK_TILES[j][tl]
                rows = min(TILE_U, ROW_BLK - base)
                u0 = src * ROW_BLK + base
                for cs in range(2):
                    for k in range(2):
                        e2[j, src, tl, :rows, cs, k, :P_BLK] = parts[cs][u0:u0 + rows, k * P_BLK:(k + 1) * P_BLK]
    return (jnp.asarray(e1.reshape(8 * Q_PAD, KV).astype(np.float32)).astype(BF16),
            jnp.asarray(e2.reshape(N_CHUNK * 128, 4 * P_PAD).astype(np.float32)).astype(BF16))


def exchange_kernel(y_ref, wy_ref, wx_ref, iy_ref, ix_ref, y8_ref, wyo_ref, wxo_ref, addr_ref, roff_ref,
                    ysend, asend, rsend, send_sem, recv_sem):
    k = lax.axis_index('cols')
    r = lax.axis_index('rows')
    other = 1 - k
    barrier = pltpu.get_barrier_semaphore()
    pl.semaphore_signal(barrier, inc=1, device_id={'cols': other}, device_id_type=MESH)
    n = y_ref.shape[2]
    y_re, y_im = y_ref[0], y_ref[1]
    low = jnp.concatenate([y_re[0:4], y_im[0:4]], axis=0)
    high = jnp.concatenate([y_re[4:8], y_im[4:8]], axis=0)
    first = k == 0
    y8_ref[:, 0:n] = jnp.where(first, low, high)
    ysend[...] = jnp.where(first, high, low)
    wyo_ref[:, 0:n] = wy_ref[...]
    wxo_ref[0] = wx_ref[...]
    row = iy_ref[...] - r * ROW_BLK
    tile = jnp.zeros_like(row)
    for t in range(1, N_SRC):
        tile = tile + jnp.where(row >= STRIDE_U * t, 1, 0)
    addr = tile * VR + ix_ref[...]
    roff = row - STRIDE_U * tile
    addr_ref[0:16, :] = addr
    roff_ref[0:16, :] = roff
    asend[...] = addr
    rsend[...] = roff
    pl.semaphore_wait(barrier, 1)
    pairs = [(ysend, y8_ref.at[:, n:2 * n]), (wy_ref, wyo_ref.at[:, n:2 * n]), (wx_ref, wxo_ref.at[1]),
             (asend, addr_ref.at[16:32]), (rsend, roff_ref.at[16:32])]
    copies = []
    for i, (src, dst) in enumerate(pairs):
        copies.append(pltpu.make_async_remote_copy(src_ref=src, dst_ref=dst, send_sem=send_sem.at[i], recv_sem=recv_sem.at[i],
                                                   device_id={'cols': other}, device_id_type=MESH))
        copies[-1].start()
    for c in copies:
        c.wait()


def split3(x):
    hi = x.astype(BF16).astype(F32)
    rest = x - hi
    mid = rest.astype(BF16).astype(F32)
    return [hi, mid, rest - mid]


def spread_kernel(addr_ref, y_ref, wy_ref, wx_ref, roff_ref, g_ref, f0_ref, f11_ref, gp_ref, gn_ref, *scr):
    accs = scr[:N_COPY]
    q_scr, raw0 = scr[N_COPY:]
    n = y_ref.shape[1]

    def zero(i, _):
        for a in accs:
            a[pl.ds(pl.multiple_of(i * VR, 8), VR), :] = jnp.zeros((VR, 128), F32)
        return 0
    lax.fori_loop(0, N_SRC, zero, 0)

    r = lax.broadcasted_iota(jnp.int32, (80, 256), 0)
    l = lax.broadcasted_iota(jnp.int32, (80, 256), 1)
    ry = (r < 24) & (l < 128) & ((r & 7) == (l >> 4))
    rw = (r >= 24) & (r < 72) & (l >= 128) & (((r - 24) & 15) == (l & 15))
    expand = jnp.where(ry | rw, 1.0, 0.0).astype(BF16)
    rr = lax.broadcasted_iota(jnp.int32, (16, 512), 0)

    def prep(i, _):
        ds = pl.ds(pl.multiple_of(i * 512, 512), 512)
        y = y_ref[:, ds]
        wy = wy_ref[:, ds]
        ro = jnp.concatenate([roff_ref[pl.ds(4 * i + s, 1), :] for s in range(4)], axis=1)
        d = rr - ro
        w16 = jnp.zeros((16, 512), F32)
        for a in range(4):
            w16 = jnp.where(d == a, wy[a:a + 1], w16)
        lhs = jnp.concatenate(split3(y) + split3(w16) + [jnp.zeros((8, 512), F32)], axis=0).astype(BF16)
        o = lax.dot_general(lhs, expand, (((0,), (0,)), ((), ())), preferred_element_type=F32)
        q_scr[ds, :] = o[:, :128] * o[:, 128:]
        return 0
    lax.fori_loop(0, n // 512, prep, 0)

    sub = lax.broadcasted_iota(jnp.int32, (8, 128), 0)
    top = sub < 4
    half = n // 2

    def block(i, _):
        ds = pl.ds(pl.multiple_of(i * 128, 128), 128)
        wx = jnp.concatenate([wx_ref[0, :, ds], wx_ref[1, :, ds]], axis=0)
        for j in range(128):
            col = jnp.broadcast_to(wx[:, j:j + 1], (8, 128))
            for h in range(2):
                acc = accs[(2 * j + h) % N_COPY]
                base = addr_ref[i + 16 * h, j] + (4 if h == 0 else 0)
                row = jnp.broadcast_to(q_scr[pl.ds(pl.multiple_of(i * 128, 128) + (j + half * h), 1), :], (8, 128))
                s = pl.ds(base, 8)
                c = jnp.where(top, col, 0.0) if h == 0 else jnp.where(top, 0.0, col)
                acc[s, :] = acc[s, :] + c * row
        return 0
    lax.fori_loop(0, half // 128, block, 0)

    for t in range(N_SRC):
        sa, sb = pl.ds(t * VR, 8), pl.ds(t * VR + 736, 8)
        a = accs[0][sa, :]
        b = accs[0][sb, :]
        for acc in accs[1:]:
            a = a + acc[sa, :]
            b = b + acc[sb, :]
            acc[sa, :] = jnp.zeros((8, 128), F32)
            acc[sb, :] = jnp.zeros((8, 128), F32)
        accs[0][sa, :] = a + jnp.where(sub == 6, b, 0.0)
        accs[0][sb, :] = b + jnp.where((sub == 4) | (sub == 5), a, 0.0)

    lane16 = lax.broadcasted_iota(jnp.int32, (16, 128), 1) & 15

    def retile(i, _):
        off = pl.multiple_of(i * 16, 16)
        tiles = []
        for t in range(N_SRC):
            s = pl.ds(t * VR + off, 16)
            v = accs[0][s, :]
            for acc in accs[1:]:
                v = v + acc[s, :]
            tiles.append(v)
        raw0[pl.ds(off, 16), :] = tiles[0]
        for m in range(N_TGT):
            out = None
            for t in range(N_SRC):
                delta = STRIDE_U * t - TILE_U * m - 2
                lo, hi = max(0, delta), min(15, 15 + delta)
                if lo > hi:
                    continue
                v = tiles[t] if delta % 128 == 0 else pltpu.roll(tiles[t], delta % 128, 1)
                if lo > 0 or hi < 15:
                    v = jnp.where((lane16 >= lo) & (lane16 <= hi), v, 0.0)
                out = v if out is None else out + v
            if m == 0:
                f0_ref[pl.ds(off, 16), :] = out
            elif m == N_TGT - 1:
                f11_ref[pl.ds(off, 16), :] = out
            else:
                g_ref[pl.ds(off, 16), (m - 1) * 128:m * 128] = out.astype(BF16)
        return 0
    lax.fori_loop(0, VR // 16, retile, 0)
    g_ref[VR:KV, :] = jnp.zeros((KV - VR, g_ref.shape[1]), BF16)
    for ref in (raw0, f0_ref, f11_ref):
        ref[VR:KV, :] = jnp.zeros((KV - VR, 128), F32)

    la = lax.broadcasted_iota(jnp.int32, (96, 128), 1) & 15
    gp = jnp.zeros((96, 128), F32)
    for c in range(8):
        v = raw0[96 * c:96 * c + 96, :]
        v = pltpu.roll(v, 2 * c, 1) if c else v
        gp = jnp.where((la == 2 * c) | (la == 2 * c + 1), v, gp)
    gp_ref[...] = gp
    lb = lax.broadcasted_iota(jnp.int32, (48, 128), 1) & 15
    gn = jnp.zeros((48, 128), F32)
    for c in range(16):
        v = f11_ref[48 * c:48 * c + 48, :]
        v = pltpu.roll(v, (c - 8) % 128, 1) if c != 8 else v
        gn = jnp.where(lb == c, v, gn)
    gn_ref[...] = gn


def transform_kernel(g_ref, f0_ref, f11_ref, gp_ref, gn_ref, e1_ref, e2_ref, s_ref, out_ref,
                     edge, msg, recv, gpr, gnr, e2f, st, img, psend, precv,
                     msend_sem, mrecv_sem, gsend_sem, grecv_sem, psend_sem, precv_sem):
    k = lax.axis_index('cols')
    r = lax.axis_index('rows')
    chip, core = r // 2, r % 2
    dests = [2 * (1 - chip) + core, 2 * (1 - chip) + (1 - core), 2 * chip + (1 - core)]
    nxt, prv = lax.rem(r + 1, 4), lax.rem(r + 3, 4)
    barrier = pltpu.get_barrier_semaphore()
    for d in dests:
        pl.semaphore_signal(barrier, inc=1, device_id={'rows': d}, device_id_type=MESH)
    pl.semaphore_signal(barrier, inc=1, device_id={'cols': 1 - k}, device_id_type=MESH)

    lane = lax.broadcasted_iota(jnp.int32, (Q_PAD, 256), 1) & 127

    def first_dft(j, g):
        ab = jnp.dot(e1_ref[...], g, preferred_element_type=F32)
        for d in range(4):
            a = ab[192 * d:192 * d + 96]
            b = ab[192 * d + 96:192 * d + 192]
            b = jnp.concatenate([pltpu.roll(b[:, :128], 64, 1), pltpu.roll(b[:, 128:], 64, 1)], axis=1)
            msg[j, d] = jnp.where(lane < 64, a - b, a + b).astype(BF16)

    def message(j, i):
        d = dests[i]
        return pltpu.make_async_remote_copy(src_ref=msg.at[j, d], dst_ref=recv.at[j, r], send_sem=msend_sem.at[j, i],
                                            recv_sem=mrecv_sem.at[j, r], device_id={'rows': d}, device_id_type=MESH)

    def arrival(j, i):
        d = dests[i]
        return pltpu.make_async_remote_copy(src_ref=msg.at[j, d], dst_ref=recv.at[j, d], send_sem=msend_sem.at[j, i],
                                            recv_sem=mrecv_sem.at[j, d], device_id={'rows': d}, device_id_type=MESH)

    def post(j):
        for i in range(3):
            message(j, i).start()
        recv[j, r] = msg[j, r]

    first_dft(0, g_ref[:, 0:256])
    pl.semaphore_wait(barrier, 4)
    to_prv = pltpu.make_async_remote_copy(src_ref=gp_ref, dst_ref=gpr, send_sem=gsend_sem.at[0], recv_sem=grecv_sem.at[0],
                                          device_id={'rows': prv}, device_id_type=MESH)
    to_nxt = pltpu.make_async_remote_copy(src_ref=gn_ref, dst_ref=gnr, send_sem=gsend_sem.at[1], recv_sem=grecv_sem.at[1],
                                          device_id={'rows': nxt}, device_id_type=MESH)
    to_prv.start()
    to_nxt.start()
    post(0)

    def middle(j, _):
        first_dft(j, g_ref[:, pl.ds(pl.multiple_of(j * 256, 256), 256)])
        post(j)
        return 0
    lax.fori_loop(1, 5, middle, 0)

    to_prv.wait()
    to_nxt.wait()
    la = lax.broadcasted_iota(jnp.int32, (96, 128), 1) & 15
    lb = lax.broadcasted_iota(jnp.int32, (48, 128), 1) & 15
    gp, gn = gpr[...], gnr[...]
    for c in range(8):
        s = slice(96 * c, 96 * c + 96)
        add = jnp.where((la == 6) | (la == 7), pltpu.roll(gp, (6 - 2 * c) % 128, 1) if c != 3 else gp, 0.0)
        edge[s, 128:256] = (f11_ref[s, :] + add).astype(BF16)
    for c in range(16):
        s = slice(48 * c, 48 * c + 48)
        add = jnp.where(lb == 0, pltpu.roll(gn, (-c) % 128, 1) if c else gn, 0.0)
        edge[s, 0:128] = (f0_ref[s, :] + add).astype(BF16)
    first_dft(5, edge[...])
    post(5)

    for j in range(N_CHUNK):
        v = e2_ref[128 * j:128 * j + 128, :]
        e2f[j, 0:128, :] = v
        e2f[j, 128:256, 0:384] = -v[:, 384:768]
        e2f[j, 128:256, 384:768] = v[:, 0:384]
    st[...] = jnp.zeros_like(st)
    for s in range(2):
        for c in range(4):
            for h in range(2):
                st[s, c, 0:Q_BLK, P_PAD * h:P_PAD * h + P_BLK] = s_ref[s, c, P_BLK * h:P_BLK * h + P_BLK, :].T

    grp = lax.broadcasted_iota(jnp.int32, (Q_PAD, 128), 1) >> 4

    def regroup(j):
        v = [recv[j, s // 2, :, 128 * (s % 2):128 * (s % 2) + 128].astype(F32) for s in range(8)]
        for b in range(3):
            bit = 1 << b
            m = (grp & bit) == 0
            for s in range(8):
                if s & bit:
                    continue
                x, y = v[s], v[s | bit]
                v[s] = jnp.where(m, x, pltpu.roll(y, 16 * bit, 1))
                v[s | bit] = jnp.where(m, pltpu.roll(x, 128 - 16 * bit, 1), y)
        return [x.astype(BF16) for x in v]

    def second_dft(j):
        for i in range(3):
            arrival(j, i).wait_recv()
        v = regroup(j)
        lhs = jnp.concatenate([jnp.concatenate([v[c], v[4 + c]], axis=1) for c in range(4)], axis=0)
        return jnp.dot(lhs, e2f[j], preferred_element_type=F32)

    img[...] = second_dft(0)

    def accumulate(j, _):
        img[...] += second_dft(j)
        return 0
    lax.fori_loop(1, N_CHUNK, accumulate, 0)

    x_re = jnp.zeros((Q_PAD, 384), F32)
    x_im = jnp.zeros((Q_PAD, 384), F32)
    for c in range(4):
        i_re = img[96 * c:96 * c + 96, 0:384]
        i_im = img[96 * c:96 * c + 96, 384:768]
        x_re = x_re + st[0, c] * i_re + st[1, c] * i_im
        x_im = x_im + st[0, c] * i_im - st[1, c] * i_re
    lo = jnp.concatenate([x_re[:, 0:192], x_im[:, 0:192]], axis=1)
    hi = jnp.concatenate([x_re[:, 192:384], x_im[:, 192:384]], axis=1)
    first = k == 0
    psend[...] = jnp.where(first, hi, lo)
    swap = pltpu.make_async_remote_copy(src_ref=psend, dst_ref=precv, send_sem=psend_sem, recv_sem=precv_sem,
                                        device_id={'cols': 1 - k}, device_id_type=MESH)
    swap.start()
    mine = jnp.where(first, lo, hi)
    for j in range(N_CHUNK):
        for i in range(3):
            message(j, i).wait_send()
    swap.wait()
    total = mine + precv[...]
    out_ref[0] = total[0:Q_BLK, 0:P_BLK].T
    out_ref[1] = total[0:Q_BLK, P_PAD:P_PAD + P_BLK].T


def solution(mesh):
    sample_spec = ('exam', 'rows', 'cols')
    vmem = pl.BlockSpec(memory_space=pltpu.VMEM)
    smem = pl.BlockSpec(memory_space=pltpu.SMEM)
    sds = jax.ShapeDtypeStruct

    def local_fn(kspace, wts_y, wts_x, idx_y, idx_x, coil_maps, deapod):
        n = kspace.shape[2]
        row_id = lax.axis_index('rows')
        col_id = lax.axis_index('cols')
        e1, e2 = dft_constants()
        y8, wy, wx, addr, roff = pl.pallas_call(
            exchange_kernel,
            out_shape=[sds((8, 2 * n), F32), sds((4, 2 * n), F32), sds((2, 4, n), F32), sds((32, 128), jnp.int32), sds((32, 128), jnp.int32)],
            in_specs=[vmem] * 5,
            out_specs=[vmem] * 5,
            scratch_shapes=[pltpu.VMEM((8, n), F32), pltpu.VMEM((16, 128), jnp.int32), pltpu.VMEM((16, 128), jnp.int32),
                            pltpu.SemaphoreType.DMA((5,)), pltpu.SemaphoreType.DMA((5,))],
            compiler_params=pltpu.CompilerParams(collective_id=0, has_side_effects=True),
            name='exchange',
        )(kspace, wts_y, wts_x, idx_y.reshape(16, 128), idx_x.reshape(16, 128))
        g, f0, f11, gp, gn = pl.pallas_call(
            spread_kernel,
            out_shape=[sds((KV, 1280), BF16), sds((KV, 128), F32), sds((KV, 128), F32), sds((96, 128), F32), sds((48, 128), F32)],
            in_specs=[smem] + [vmem] * 4,
            out_specs=[vmem] * 5,
            scratch_shapes=[pltpu.VMEM((N_SRC * VR, 128), F32)] * N_COPY + [pltpu.VMEM((2 * n, 128), F32), pltpu.VMEM((KV, 128), F32)],
            compiler_params=pltpu.CompilerParams(vmem_limit_bytes=50 * 2**20),
            name='spread',
        )(addr, y8, wy, wx, roff)
        part = pl.pallas_call(
            transform_kernel,
            out_shape=sds((2, P_BLK, Q_BLK), F32),
            in_specs=[vmem] * 8,
            out_specs=vmem,
            scratch_shapes=[
                pltpu.VMEM((KV, 256), BF16),
                pltpu.VMEM((N_CHUNK, 4, Q_PAD, 256), BF16),
                pltpu.VMEM((N_CHUNK, 4, Q_PAD, 256), BF16),
                pltpu.VMEM((96, 128), F32),
                pltpu.VMEM((48, 128), F32),
                pltpu.VMEM((N_CHUNK, 256, 768), BF16),
                pltpu.VMEM((2, 4, Q_PAD, 384), F32),
                pltpu.VMEM((4 * Q_PAD, 768), F32),
                pltpu.VMEM((Q_PAD, 384), F32),
                pltpu.VMEM((Q_PAD, 384), F32),
                pltpu.SemaphoreType.DMA((N_CHUNK, 3)),
                pltpu.SemaphoreType.DMA((N_CHUNK, 4)),
                pltpu.SemaphoreType.DMA((2,)),
                pltpu.SemaphoreType.DMA((2,)),
                pltpu.SemaphoreType.DMA,
                pltpu.SemaphoreType.DMA,
            ],
            compiler_params=pltpu.CompilerParams(collective_id=1, has_side_effects=True, vmem_limit_bytes=50 * 2**20),
            name='transform',
        )(g, f0, f11, gp, gn, e1, e2, coil_maps)
        d_rows = lax.dynamic_slice(deapod, (col_id * P_BLK,), (P_BLK,))
        d_cols = lax.dynamic_slice(deapod, (row_id * Q_BLK,), (Q_BLK,))
        return part * (d_rows[:, None] * d_cols[None, :])

    return jax.shard_map(
        local_fn,
        mesh=mesh,
        in_specs=(P(None, None, sample_spec), P(None, sample_spec), P(None, sample_spec), P(sample_spec), P(sample_spec), P(None, ('exam', 'cols'), None, 'rows'), P()),
        out_specs=P(None, ('exam', 'cols'), 'rows'),
        check_vma=False,
    )
```

time: 251 us -> 61.4 us (0.24)
  matrix products: 72.7 us -> 0 us
  waiting for transfers between devices: 60.8 us -> 0 us
  Pallas kernels: 0 us -> 52.1 us
  local copies, waits for them, and re-layouts: 56.3 us -> 8.1 us
  other arithmetic: 34.4 us -> 0.79 us
  between operations: 14.3 us -> 0.07 us
  starting transfers between devices: 10.7 us -> 0 us
    dot_general x10 -> x0, matrix products: 72.7 us -> none  [the longest x8 65.7 us: add_tile(): jnp.einsum('sclm,km->sclk', scaled, col_mat, precision=lax.Precision.HIGH...]
    pallas_call x0 -> x3, Pallas kernels: none -> 52.1 us  [the longest x1 25.3 us: local_fn(): pl.pallas_call(transform_kernel, out_shape=sds((2, P_BLK, Q_BLK), F32), i...]
    all_to_all x2 -> x0, waiting for transfers between devices: 36.6 us -> none  [the longest x1 18.9 us: local_fn(): lax.all_to_all(spread_buf.astype(jnp.bfloat16), 'cols', 1, 3, tiled=True)]
    unnamed x2 -> x0, waiting for transfers between devices: 17.4 us -> none
    reduce_sum x17 -> x0, other arithmetic: 12.5 us -> none  [the longest x16 12.3 us: tap_matrix(): jnp.sum(jnp.where(tap_off[None] == tap_ids, weights[..., None, :], 0.0),...]
    while x2 -> x0, local copies, waits for them, and re-layouts: 11.6 us -> none  [spread_block(): spread_buf, _ = lax.scan(add_tile, start_buf, tile_data)]
    all_to_all x4 -> x0, local copies, waits for them, and re-layouts: 11.1 us -> none  [the longest x2 8.59 us: local_fn(): lax.all_to_all(spread_buf.astype(jnp.bfloat16), 'cols', 1, 3, tiled=True)]
    split x4 -> x0, local copies, waits for them, and re-layouts: 10.7 us -> none  [fold_ghosts(): jnp.split(spread_buf, [half_w, 2 * half_w, core_len, core_len + half_w],...]
  transfers between devices with their start and end apart: 7 -> 0, of which waited for: 5 -> 0; matrix products, arithmetic and copies ran while one was open for 12% -> 0% of each run, Pallas kernels for 0% -> 0%
where the time goes in v1:
time: 61.4 us; the launch traced here: 61.1 us
  Pallas kernels  52.1 us (85%)
  local copies, waits for them, and re-layouts  8.1 us (13%)
  other arithmetic  0.79 us (1%)
    pallas_call x1, Pallas kernels, local_fn(): pl.pallas_call(transform_kernel, out_shape=sds((2, P_BLK, Q_BLK), F32), i...  25.3 us
    pallas_call x1, Pallas kernels, local_fn(): pl.pallas_call(spread_kernel, out_shape=[sds((KV, 1280), BF16), sds((KV,...  17.9 us
    pallas_call x1, Pallas kernels, local_fn(): pl.pallas_call(exchange_kernel, out_shape=[sds((8, 2 * n), F32), sds((4,...  9 us
    unnamed x19, local copies, waits for them, and re-layouts  7.95 us

profile of v1, /device:TPU:0, one launch (start us, length us, event | category | flops | bytes accessed | tf_op | source)
XLA Modules:
  0.0 61.1 jit_solution(2343967870643490172)
XLA Ops:
  0.0 9.0 %exchange.1 = (f32[8,4096]{1,0:T(8,128)}, f32[4,4096]{1,0:T(4,128)}, f32[2,4,2048]{2,1,0:T(4,128)}, s32[32,128]{1,0:T(8,128)}, s32[32,128]{1,0:T(8,128)}) custom-call(f32[2,8,2048]{2,1,0:T(8,128)} %y_ref.1, f32[4,2048]{1,0:T(4,128)} %wy_ref.1, f32[4,2048]{1,0:T(4,128)} %wx_ref.1, s32[16,128]{1,0:T(8,128)} %bitcast.2, s32[16,128]{1,0:T(8,128)} %bitcast.3), custom_call_target="tpu_custom_call" | custom-call | tf_op jit(solution)/shard_map/exchange/pallas_call | solution.py:358
  9.0 0.0 copy-start.3
  9.0 0.9 %copy-done.3 = f32[8,4096]{1,0:T(8,128)S(1)} copy-done((f32[8,4096]{1,0:T(8,128)S(1)}, f32[8,4096]{1,0:T(8,128)}, u32[]{:S(2)}) %copy-start.3) | copy-done | bytes 131096
  9.9 0.0 copy-start.4
  9.9 0.8 %copy-done.4 = f32[4,4096]{1,0:T(4,128)S(1)} copy-done((f32[4,4096]{1,0:T(4,128)S(1)}, f32[4,4096]{1,0:T(4,128)}, u32[]{:S(2)}) %copy-start.4) | copy-done | bytes 65560
  10.8 0.0 copy-start.5
  10.8 0.8 %copy-done.5 = f32[2,4,2048]{2,1,0:T(4,128)S(1)} copy-done((f32[2,4,2048]{2,1,0:T(4,128)S(1)}, f32[2,4,2048]{2,1,0:T(4,128)}, u32[]{:S(2)}) %copy-start.5) | copy-done | bytes 65560
  11.6 0.0 copy-start.6
  11.6 0.7 %copy-done.6 = s32[32,128]{1,0:T(8,128)S(1)} copy-done((s32[32,128]{1,0:T(8,128)S(1)}, s32[32,128]{1,0:T(8,128)}, u32[]{:S(2)}) %copy-start.6) | copy-done | bytes 16408
  12.3 0.0 copy-start.7
  12.3 0.7 %copy-done.7 = s32[32,128]{1,0:T(8,128)S(1)} copy-done((s32[32,128]{1,0:T(8,128)S(1)}, s32[32,128]{1,0:T(8,128)}, u32[]{:S(2)}) %copy-start.7) | copy-done | bytes 16408
  13.0 17.9 %spread.1 = (bf16[768,1280]{1,0:T(8,128)(2,1)S(1)}, f32[768,128]{1,0:T(8,128)S(1)}, f32[768,128]{1,0:T(8,128)S(1)}, f32[96,128]{1,0:T(8,128)S(1)}, f32[48,128]{1,0:T(8,128)S(1)}) custom-call(s32[32,128]{1,0:T(8,128)S(1)} %copy-done.6, f32[8,4096]{1,0:T(8,128)S(1)} %copy-done.3, f32[4,4096]{1,0:T(4,128)S(1)} %copy-done.4, f32[2,4,2048]{2,1,0:T(4,128)S(1)} %copy-done.5, ...), custom_call_target="tpu_custom_call" | custom-call | tf_op jit(solution)/shard_map/spread/pallas_call | solution.py:368
  30.9 0.0 copy-start
  30.9 1.3 %copy-done = bf16[768,1280]{1,0:T(8,128)(2,1)} copy-done((bf16[768,1280]{1,0:T(8,128)(2,1)}, bf16[768,1280]{1,0:T(8,128)(2,1)S(1)}, u32[]{:S(2)}) %copy-start) | copy-done | bytes 1966104
  32.2 0.0 copy-start.1
  32.2 0.0 copy-start.2
  32.2 2.6 %copy.10.s_ref = f32[2,4,368,92]{3,2,1,0:T(8,128)} copy(f32[2,4,368,92]{2,1,3,0:T(4,128)} %param.14) | data formatting | bytes 2166784 | tf_op args[5]
  34.8 0.0 copy-done.1
  34.8 0.0 copy-done.2
  34.8 0.0 copy-start.8
  34.9 25.3 %transform.1 = f32[2,184,92]{2,1,0:T(8,128)S(1)} custom-call(bf16[768,1280]{1,0:T(8,128)(2,1)} %copy-done, f32[768,128]{1,0:T(8,128)S(1)} %get-tuple-element.21.f0_ref, f32[768,128]{1,0:T(8,128)S(1)} %get-tuple-element.22.f11_ref, f32[96,128]{1,0:T(8,128)S(1)} %get-tuple-element.23.gp_ref, f32[48,128]{1,0:T(8,128)S(1)} %get-tuple-element.24.gn_ref, ...), custom_call_target="tpu_custom_call" | custom-call | tf_op jit(solution)/shard_map/transform/pallas_call | solution.py:377
  60.2 0.0 copy-done.8
  60.2 0.1 dynamic_slice.6
  60.2 0.1 dynamic_slice.7
  60.3 0.1 broadcast_multiply_fusion.1
  60.4 0.7 %broadcast_multiply_fusion = f32[2,184,92]{2,1,0:T(8,128)} fusion(f32[2,184,92]{2,1,0:T(8,128)S(1)} %transform.1, f32[184,92]{1,0:T(8,128)S(1)} %broadcast_multiply_fusion.1), kind=kLoop, calls=%fused_computation | loop fusion | flops 33856 | bytes 338560 | tf_op jit(solution)/shard_map/mul | solution.py:405
Async XLA Ops:
  9.0 0.9 %copy-start.3 = (f32[8,4096]{1,0:T(8,128)S(1)}, f32[8,4096]{1,0:T(8,128)}, u32[]{:S(2)}) copy-start(f32[8,4096]{1,0:T(8,128)} %get-tuple-element.16.y_ref) | copy-start | bytes 393220
  9.9 0.8 %copy-start.4 = (f32[4,4096]{1,0:T(4,128)S(1)}, f32[4,4096]{1,0:T(4,128)}, u32[]{:S(2)}) copy-start(f32[4,4096]{1,0:T(4,128)} %get-tuple-element.17.wy_ref) | copy-start | bytes 196612
  10.8 0.8 %copy-start.5 = (f32[2,4,2048]{2,1,0:T(4,128)S(1)}, f32[2,4,2048]{2,1,0:T(4,128)}, u32[]{:S(2)}) copy-start(f32[2,4,2048]{2,1,0:T(4,128)} %get-tuple-element.18.wx_ref) | copy-start | bytes 196612
  11.6 0.7 %copy-start.6 = (s32[32,128]{1,0:T(8,128)S(1)}, s32[32,128]{1,0:T(8,128)}, u32[]{:S(2)}) copy-start(s32[32,128]{1,0:T(8,128)} %get-tuple-element.15.addr_ref) | copy-start | bytes 49156
  12.3 0.7 %copy-start.7 = (s32[32,128]{1,0:T(8,128)S(1)}, s32[32,128]{1,0:T(8,128)}, u32[]{:S(2)}) copy-start(s32[32,128]{1,0:T(8,128)} %get-tuple-element.19.roff_ref) | copy-start | bytes 49156
  30.9 1.3 %copy-start = (bf16[768,1280]{1,0:T(8,128)(2,1)}, bf16[768,1280]{1,0:T(8,128)(2,1)S(1)}, u32[]{:S(2)}) copy-start(bf16[768,1280]{1,0:T(8,128)(2,1)S(1)} %get-tuple-element.20.g_ref) | copy-start | bytes 5898244
  32.2 2.6 %copy-start.1 = (bf16[768,768]{1,0:T(8,128)(2,1)S(1)}, bf16[768,768]{1,0:T(8,128)(2,1)}, u32[]{:S(2)}) copy-start(bf16[768,768]{1,0:T(8,128)(2,1)} %constant.23.e1_ref) | copy-start | bytes 3538948
  32.2 2.6 %copy-start.2 = (bf16[768,768]{1,0:T(8,128)(2,1)S(1)}, bf16[768,768]{1,0:T(8,128)(2,1)}, u32[]{:S(2)}) copy-start(bf16[768,768]{1,0:T(8,128)(2,1)} %constant.24.e2_ref) | copy-start | bytes 3538948
  34.8 25.3 %copy-start.8 = (f32[368]{0:T(512)S(1)}, f32[368]{0:T(512)}, u32[]{:S(2)}) copy-start(f32[368]{0:T(512)} %param.15) | copy-start | bytes 4420

commit v2 on v1

v2 whole, which is shorter than its diff:
```python
import functools
import functools
import math

import jax
import jax.numpy as jnp
import numpy as np
from jax import lax
from jax.experimental import pallas as pl
from jax.experimental.pallas import tpu as pltpu
from jax.sharding import PartitionSpec as P

F32, BF16 = jnp.float32, jnp.bfloat16
MESH = pl.DeviceIdType.MESH

N_IMG = 368
N_GRID = 736
ROW_BLK = 184
Q_BLK, Q_PAD = 92, 96
P_BLK, P_PAD, P_ALL = 184, 192, 384
N_CH = 8
TILE_U, STRIDE_U, N_SRC = 16, 13, 15
N_TGT = 12
COL_BLK = 368
VR = 384
KV = 2 * VR
LANES, ROWS = 128, 16
EDGE = 6
N_CHUNK = 6
N_COPY = 4
CHUNK_TILES = [(1 + 2 * j, 2 + 2 * j) for j in range(5)] + [(0, 11)]


def dft_constants():
    scale = 1.0 / math.sqrt(N_GRID)
    phase = ((np.arange(N_GRID)[:, None] - N_GRID // 2) * (np.arange(N_IMG)[None, :] - N_IMG // 2)) % N_GRID
    ang = phase.astype(np.float64) * (2.0 * math.pi / N_GRID)
    parts = (np.cos(ang) * scale, np.sin(ang) * scale)
    e1 = np.zeros((4, 2, Q_PAD, 2, VR))
    for dest in range(4):
        for cs in range(2):
            for half in range(2):
                    part = parts[cs][half * COL_BLK:(half + 1) * COL_BLK, dest * Q_BLK:(dest + 1) * Q_BLK]
                    e1[dest, cs, :Q_BLK, half, EDGE:EDGE + COL_BLK] = part.T
    e2 = np.zeros((N_CHUNK, 4, 2, TILE_U, 2, P_ALL))
    for j in range(N_CHUNK):
        for src in range(4):
            for tl in range(2):
                base = TILE_U * CHUNK_TILES[j][tl]
                rows = min(TILE_U, ROW_BLK - base)
                u0 = src * ROW_BLK + base
                for cs in range(2):
                    e2[j, src, tl, :rows, cs, :N_IMG] = parts[cs][u0:u0 + rows]
    return (jnp.asarray(e1.reshape(8 * Q_PAD, KV).astype(np.float32)).astype(BF16),
            jnp.asarray(e2.reshape(N_CHUNK * LANES, 2 * P_ALL).astype(np.float32)).astype(BF16))


def split3(x):
    hi = x.astype(BF16).astype(F32)
    rest = x - hi
    mid = rest.astype(BF16).astype(F32)
    return [hi, mid, rest - mid]


def spread_kernel(received, y_ref, wy_ref, wx_ref, iy_ref, ix_ref, *refs):
    accs = refs[:N_COPY]
    qa, qb, y_sel, roff, addr_v, addr, sem = refs[N_COPY:]
    k = lax.axis_index('cols')
    r = lax.axis_index('rows')
    half = 1 - k if received else k
    n = y_ref.shape[2]

    row = iy_ref[...] - r * ROW_BLK
    tile = jnp.zeros_like(row)
    for t in range(1, N_SRC):
        tile = tile + jnp.where(row >= STRIDE_U * t, 1, 0)
    addr_v[...] = tile * VR + (ix_ref[...] - half * COL_BLK)
    roff[...] = row - STRIDE_U * tile
    to_smem = pltpu.make_async_copy(addr_v, addr, sem)
    to_smem.start()
    y_re, y_im = y_ref[0], y_ref[1]
    low = jnp.concatenate([y_re[0:4], y_im[0:4]], axis=0)
    high = jnp.concatenate([y_re[4:8], y_im[4:8]], axis=0)
    y_sel[...] = jnp.where(k == 0, low, high)

    def zero(i, _):
        for a in accs:
            a[pl.ds(pl.multiple_of(i * VR, 8), VR), :] = jnp.zeros((VR, LANES), F32)
        return 0
    lax.fori_loop(0, N_SRC, zero, 0)

    r0 = lax.broadcasted_iota(jnp.int32, (80, 256), 0)
    l0 = lax.broadcasted_iota(jnp.int32, (80, 256), 1)
    ry = (r0 < 24) & (l0 < LANES) & ((r0 & 7) == (l0 >> 4))
    rw = (r0 >= 24) & (r0 < 72) & (l0 >= LANES) & (((r0 - 24) & 15) == (l0 & 15))
    expand = jnp.where(ry | rw, 1.0, 0.0).astype(BF16)
    rr = lax.broadcasted_iota(jnp.int32, (ROWS, 256), 0)
    n_blk = n // 256

    def prep(i, q_ref):
        ds = [pl.ds(pl.multiple_of((i + n_blk * h) * LANES, LANES), LANES) for h in range(2)]
        y = jnp.concatenate([y_sel[:, s] for s in ds], axis=1)
        wy = jnp.concatenate([wy_ref[:, s] for s in ds], axis=1)
        d = rr - jnp.concatenate([roff[pl.ds(i + n_blk * h, 1), :] for h in range(2)], axis=1)
        w16 = jnp.zeros((ROWS, 256), F32)
        for a in range(4):
            w16 = jnp.where(d == a, wy[a:a + 1], w16)
        lhs = jnp.concatenate(split3(y) + split3(w16) + [jnp.zeros((8, 256), F32)], axis=0).astype(BF16)
        o = lax.dot_general(lhs, expand, (((0,), (0,)), ((), ())), preferred_element_type=F32)
        q_ref[...] = o[:, :LANES] * o[:, LANES:]

    top = lax.broadcasted_iota(jnp.int32, (8, LANES), 0) < 4

    def scatter(i, q_ref):
        wx = jnp.concatenate([wx_ref[:, pl.ds(pl.multiple_of((i + n_blk * h) * LANES, LANES), LANES)] for h in range(2)], axis=0)
        for j in range(LANES):
            col = jnp.broadcast_to(wx[:, j:j + 1], (8, LANES))
            for h in range(2):
                acc = accs[(2 * j + h) % N_COPY]
                base = addr[i + n_blk * h, j] + (0 if h else 4)
                q = jnp.broadcast_to(q_ref[j + LANES * h:j + LANES * h + 1, :], (8, LANES))
                s = pl.ds(base, 8)
                c = jnp.where(top, 0.0, col) if h else jnp.where(top, col, 0.0)
                acc[s, :] = acc[s, :] + c * q

    prep(0, qa)
    to_smem.wait()

    def two_blocks(i, _):
        prep(2 * i + 1, qb)
        scatter(2 * i, qa)
        prep(lax.rem(2 * i + 2, n_blk), qa)
        scatter(2 * i + 1, qb)
        return 0
    lax.fori_loop(0, n_blk // 2, two_blocks, 0)


def transform_kernel(*refs):
    own, nbr = refs[:N_COPY], refs[N_COPY:2 * N_COPY]
    (e1_ref, e2_ref, s_ref, out_ref, gch, raw0, f0, f11, gps, gns, msg, recv, gpr, gnr, e2f, st, img, psend, precv,
     msend_sem, mrecv_sem, gsend_sem, grecv_sem, psend_sem, precv_sem) = refs[2 * N_COPY:]
    k = lax.axis_index('cols')
    r = lax.axis_index('rows')
    chip, core = r // 2, r % 2
    dests = [2 * (1 - chip) + core, 2 * (1 - chip) + (1 - core), 2 * chip + (1 - core)]
    nxt, prv = lax.rem(r + 1, 4), lax.rem(r + 3, 4)
    barrier = pltpu.get_barrier_semaphore()
    for d in dests:
        pl.semaphore_signal(barrier, inc=1, device_id={'rows': d}, device_id_type=MESH)
    pl.semaphore_signal(barrier, inc=1, device_id={'cols': 1 - k}, device_id_type=MESH)

    slots = ((own, k), (nbr, 1 - k))
    lane16 = lax.broadcasted_iota(jnp.int32, (ROWS, LANES), 1) & 15
    sub16 = lax.broadcasted_iota(jnp.int32, (ROWS, LANES), 0)

    def merged(accs, off, targets):
        wanted = {}
        for m in targets:
            deltas = {0: 0} if m is None else {t: STRIDE_U * t - TILE_U * m - 2 for t in range(N_SRC)}
            wanted[m] = {t: d for t, d in deltas.items() if abs(d) < ROWS}
        loaded = {}
        for t in sorted({t for w in wanted.values() for t in w}):
            s = pl.ds(t * VR + off, ROWS)
            v = accs[0][s, :]
            for acc in accs[1:]:
                v = v + acc[s, :]
            loaded[t] = v
        outs = []
        for m in targets:
            out = None
            for t, d in wanted[m].items():
                lo, hi = max(0, d), min(15, 15 + d)
                v = pltpu.roll(loaded[t], d % LANES, 1) if d else loaded[t]
                if lo > 0 or hi < 15:
                    v = jnp.where((lane16 >= lo) & (lane16 <= hi), v, 0.0)
                out = v if out is None else out + v
            outs.append(out)
        return outs

    def merge_all(targets, put):
        def rows(i, _):
            for accs, half in slots:
                off = pl.multiple_of(i * ROWS, ROWS)
                put(pl.multiple_of(half * VR + off, ROWS), merged(accs, off, targets))
            return 0
        lax.fori_loop(1, VR // ROWS - 1, rows, 0)
        last = VR - ROWS
        a = [merged(accs, 0, targets) for accs, _ in slots]
        b = [merged(accs, last, targets) for accs, _ in slots]
        for i, (_, half) in enumerate(slots):
            fix_a = [x + jnp.where(sub16 == 6, y, 0.0) for x, y in zip(a[i], b[1 - i])]
            fix_b = [y + jnp.where((sub16 == 4) | (sub16 == 5), x, 0.0) for x, y in zip(a[1 - i], b[i])]
            put(pl.multiple_of(half * VR, ROWS), fix_a)
            put(pl.multiple_of(half * VR + last, ROWS), fix_b)

    def put_chunk(off, vals):
        for i, v in enumerate(vals):
            gch[pl.ds(off, ROWS), LANES * i:LANES * (i + 1)] = v.astype(BF16)

    def put_edges(off, vals):
        for ref, v in zip((raw0, f0, f11), vals):
            ref[pl.ds(off, ROWS), :] = v

    lane = lax.broadcasted_iota(jnp.int32, (Q_PAD, 256), 1) & 127

    def first_dft(j, g):
        ab = jnp.dot(e1_ref[...], g, preferred_element_type=F32)
        for d in range(4):
            a = ab[192 * d:192 * d + 96]
            b = ab[192 * d + 96:192 * d + 192]
            b = jnp.concatenate([pltpu.roll(b[:, :128], 64, 1), pltpu.roll(b[:, 128:], 64, 1)], axis=1)
            msg[j, d] = jnp.where(lane < 64, a - b, a + b).astype(BF16)

    def message(j, i):
        d = dests[i]
        return pltpu.make_async_remote_copy(src_ref=msg.at[j, d], dst_ref=recv.at[j, r], send_sem=msend_sem.at[j, i],
                                            recv_sem=mrecv_sem.at[j, r], device_id={'rows': d}, device_id_type=MESH)

    def arrival(j, i):
        d = dests[i]
        return pltpu.make_async_remote_copy(src_ref=msg.at[j, d], dst_ref=recv.at[j, d], send_sem=msend_sem.at[j, i],
                                            recv_sem=mrecv_sem.at[j, d], device_id={'rows': d}, device_id_type=MESH)

    def post(j):
        for i in range(3):
            message(j, i).start()
        recv[j, r] = msg[j, r]

    merge_all(CHUNK_TILES[0], put_chunk)
    first_dft(0, gch[...])
    pl.semaphore_wait(barrier, 4)
    post(0)

    merge_all((None, 0, N_TGT - 1), put_edges)
    la = lax.broadcasted_iota(jnp.int32, (96, LANES), 1) & 15
    lb = lax.broadcasted_iota(jnp.int32, (48, LANES), 1) & 15

    def shifted(v, by):
        return pltpu.roll(v, by % LANES, 1) if by else v

    gp = jnp.zeros((96, LANES), F32)
    for c in range(8):
        gp = jnp.where((la >> 1) == c, shifted(raw0[96 * c:96 * c + 96, :], 2 * c), gp)
    gps[...] = gp
    gn = jnp.zeros((48, LANES), F32)
    for c in range(16):
        gn = jnp.where(lb == c, shifted(f11[48 * c:48 * c + 48, :], c - 8), gn)
    gns[...] = gn
    to_prv = pltpu.make_async_remote_copy(src_ref=gps, dst_ref=gpr, send_sem=gsend_sem.at[0], recv_sem=grecv_sem.at[0],
                                          device_id={'rows': prv}, device_id_type=MESH)
    to_nxt = pltpu.make_async_remote_copy(src_ref=gns, dst_ref=gnr, send_sem=gsend_sem.at[1], recv_sem=grecv_sem.at[1],
                                          device_id={'rows': nxt}, device_id_type=MESH)
    to_prv.start()
    to_nxt.start()

    for j in range(1, N_CHUNK - 1):
        merge_all(CHUNK_TILES[j], put_chunk)
        first_dft(j, gch[...])
        post(j)

    to_prv.wait()
    to_nxt.wait()
    gp, gn = gpr[...], gnr[...]
    for c in range(8):
        s = slice(96 * c, 96 * c + 96)
        gch[s, LANES:2 * LANES] = (f11[s, :] + jnp.where((la >> 1) == 3, shifted(gp, 6 - 2 * c), 0.0)).astype(BF16)
    for c in range(16):
        s = slice(48 * c, 48 * c + 48)
        gch[s, 0:LANES] = (f0[s, :] + jnp.where(lb == 0, shifted(gn, -c), 0.0)).astype(BF16)
    first_dft(N_CHUNK - 1, gch[...])
    post(N_CHUNK - 1)

    for j in range(N_CHUNK):
        v = e2_ref[128 * j:128 * j + 128, :]
        e2f[j, 0:128, :] = v
        e2f[j, 128:256, 0:P_ALL] = -v[:, P_ALL:2 * P_ALL]
        e2f[j, 128:256, P_ALL:2 * P_ALL] = v[:, 0:P_ALL]
    st[...] = jnp.zeros_like(st)
    for s in range(2):
        for c in range(4):
            st[s, c, 0:Q_BLK, 0:N_IMG] = s_ref[s, :, c, :]

    grp = lax.broadcasted_iota(jnp.int32, (Q_PAD, 128), 1) >> 4

    def regroup(j):
        v = [recv[j, s // 2, :, 128 * (s % 2):128 * (s % 2) + 128].astype(F32) for s in range(8)]
        for b in range(3):
            bit = 1 << b
            m = (grp & bit) == 0
            for s in range(8):
                if s & bit:
                    continue
                x, y = v[s], v[s | bit]
                v[s] = jnp.where(m, x, pltpu.roll(y, 16 * bit, 1))
                v[s | bit] = jnp.where(m, pltpu.roll(x, 128 - 16 * bit, 1), y)
        return [x.astype(BF16) for x in v]

    def second_dft(j):
        for i in range(3):
            arrival(j, i).wait_recv()
        v = regroup(j)
        lhs = jnp.concatenate([jnp.concatenate([v[c], v[4 + c]], axis=1) for c in range(4)], axis=0)
        return jnp.dot(lhs, e2f[j], preferred_element_type=F32)

    img[...] = second_dft(0)

    def accumulate(j, _):
        img[...] += second_dft(j)
        return 0
    lax.fori_loop(1, N_CHUNK, accumulate, 0)

    x_re = jnp.zeros((Q_PAD, P_ALL), F32)
    x_im = jnp.zeros((Q_PAD, P_ALL), F32)
    for c in range(4):
        i_re = img[96 * c:96 * c + 96, 0:P_ALL]
        i_im = img[96 * c:96 * c + 96, P_ALL:2 * P_ALL]
        x_re = x_re + st[0, c] * i_re + st[1, c] * i_im
        x_im = x_im + st[0, c] * i_im - st[1, c] * i_re
    lo = jnp.concatenate([x_re[:, 0:P_PAD], x_im[:, 0:P_PAD]], axis=1)
    hi = jnp.concatenate([x_re[:, P_BLK:P_BLK + P_PAD], x_im[:, P_BLK:P_BLK + P_PAD]], axis=1)
    first = k == 0
    psend[...] = jnp.where(first, hi, lo)
    swap = pltpu.make_async_remote_copy(src_ref=psend, dst_ref=precv, send_sem=psend_sem, recv_sem=precv_sem,
                                        device_id={'cols': 1 - k}, device_id_type=MESH)
    swap.start()
    mine = jnp.where(first, lo, hi)
    for j in range(N_CHUNK):
        for i in range(3):
            message(j, i).wait_send()
    swap.wait()
    total = mine + precv[...]
    out_ref[0] = total[0:Q_BLK, 0:P_BLK].T
    out_ref[1] = total[0:Q_BLK, P_PAD:P_PAD + P_BLK].T


def solution(mesh):
    sample_spec = ('exam', 'rows', 'cols')
    vmem = pl.BlockSpec(memory_space=pltpu.VMEM)
    sds = jax.ShapeDtypeStruct

    def local_fn(kspace, wts_y, wts_x, idx_y, idx_x, coil_maps, deapod):
        n = kspace.shape[2]
        row_id = lax.axis_index('rows')
        col_id = lax.axis_index('cols')
        e1, e2 = dft_constants()
        samples = (kspace, wts_y, wts_x, idx_y.reshape(16, LANES), idx_x.reshape(16, LANES))
        moved = [lax.ppermute(x, 'cols', [(0, 1), (1, 0)]) for x in samples]

        def spread(received, args):
            return pl.pallas_call(
                functools.partial(spread_kernel, received),
                out_shape=[sds((N_SRC * VR, LANES), F32)] * N_COPY,
                in_specs=[vmem] * 5,
                out_specs=[vmem] * N_COPY,
                scratch_shapes=[pltpu.VMEM((256, LANES), F32), pltpu.VMEM((256, LANES), F32), pltpu.VMEM((8, n), F32),
                                pltpu.VMEM((16, LANES), jnp.int32), pltpu.VMEM((16, LANES), jnp.int32),
                                pltpu.SMEM((16, LANES), jnp.int32), pltpu.SemaphoreType.DMA],
                compiler_params=pltpu.CompilerParams(vmem_limit_bytes=16 * 2**20),
                cost_estimate=pl.CostEstimate(flops=10**8, bytes_accessed=10**7, transcendentals=0),
                name='spread_received' if received else 'spread_own',
            )(*args)

        accs = spread(False, samples)
        accs += spread(True, moved)
        maps = jnp.transpose(coil_maps, (0, 3, 1, 2))
        part = pl.pallas_call(
            transform_kernel,
            out_shape=sds((2, P_BLK, Q_BLK), F32),
            in_specs=[vmem] * (2 * N_COPY + 3),
            out_specs=vmem,
            scratch_shapes=[pltpu.VMEM((KV, 256), BF16)] + [pltpu.VMEM((KV, LANES), F32)] * 3 + [
                pltpu.VMEM((96, LANES), F32),
                pltpu.VMEM((48, LANES), F32),
                pltpu.VMEM((N_CHUNK, 4, Q_PAD, 256), BF16),
                pltpu.VMEM((N_CHUNK, 4, Q_PAD, 256), BF16),
                pltpu.VMEM((96, LANES), F32),
                pltpu.VMEM((48, LANES), F32),
                pltpu.VMEM((N_CHUNK, 256, 2 * P_ALL), BF16),
                pltpu.VMEM((2, 4, Q_PAD, P_ALL), F32),
                pltpu.VMEM((4 * Q_PAD, 2 * P_ALL), F32),
                pltpu.VMEM((Q_PAD, P_ALL), F32),
                pltpu.VMEM((Q_PAD, P_ALL), F32),
                pltpu.SemaphoreType.DMA((N_CHUNK, 3)),
                pltpu.SemaphoreType.DMA((N_CHUNK, 4)),
                pltpu.SemaphoreType.DMA((2,)),
                pltpu.SemaphoreType.DMA((2,)),
                pltpu.SemaphoreType.DMA,
                pltpu.SemaphoreType.DMA,
            ],
            compiler_params=pltpu.CompilerParams(collective_id=1, has_side_effects=True, vmem_limit_bytes=24 * 2**20),
            name='transform',
        )(*accs, e1, e2, maps)
        d_rows = lax.dynamic_slice(deapod, (col_id * P_BLK,), (P_BLK,))
        d_cols = lax.dynamic_slice(deapod, (row_id * Q_BLK,), (Q_BLK,))
        return part * (d_rows[:, None] * d_cols[None, :])

    return jax.shard_map(
        local_fn,
        mesh=mesh,
        in_specs=(P(None, None, sample_spec), P(None, sample_spec), P(None, sample_spec), P(sample_spec), P(sample_spec), P(None, ('exam', 'cols'), None, 'rows'), P()),
        out_specs=P(None, ('exam', 'cols'), 'rows'),
        check_vma=False,
    )
```

time: 61.4 us -> 55.4 us (0.902)
  Pallas kernels: 52.1 us -> 37.5 us
  starting transfers between devices: 0 us -> 7.42 us
  local copies, waits for them, and re-layouts: 8.1 us -> 9.1 us
    pallas_call x2, Pallas kernels: 26.9 us -> 9.27 us  [spread(): pl.pallas_call(functools.partial(spread_kernel, received), out_shape=[sds...]
    ppermute x0 -> x5, starting transfers between devices: none -> 7.42 us  [local_fn(): moved = [lax.ppermute(x, 'cols', [(0, 1), (1, 0)]) for x in samples]]
    pallas_call x1, Pallas kernels: 25.3 us -> 28.2 us  [local_fn(): pl.pallas_call(transform_kernel, out_shape=sds((2, P_BLK, Q_BLK), F32), i...]
    dynamic_slice x1, local copies, waits for them, and re-layouts: 0.07 us -> 0.75 us  [local_fn(): d_cols = lax.dynamic_slice(deapod, (row_id * Q_BLK,), (Q_BLK,))]
    dynamic_slice x1, local copies, waits for them, and re-layouts: 0.08 us -> 0.75 us  [local_fn(): d_rows = lax.dynamic_slice(deapod, (col_id * P_BLK,), (P_BLK,))]
    unnamed x19 -> x16, local copies, waits for them, and re-layouts: 7.95 us -> 7.6 us
  transfers between devices with their start and end apart: 0 -> 5, of which waited for: 0 -> 0; matrix products, arithmetic and copies ran while one was open for 0% -> 3% of each run, Pallas kernels for 0% -> 8%
where the time goes in v2:
time: 55.4 us; the launch traced here: 54.9 us
  Pallas kernels  37.5 us (68%)
  local copies, waits for them, and re-layouts  9.1 us (16%)
  starting transfers between devices  7.42 us (13%)
  other arithmetic  0.79 us (1%)
    pallas_call x1, Pallas kernels, local_fn(): pl.pallas_call(transform_kernel, out_shape=sds((2, P_BLK, Q_BLK), F32), i...  28.2 us
    pallas_call x2, Pallas kernels, spread(): pl.pallas_call(functools.partial(spread_kernel, received), out_shape=[sds...  9.27 us
    unnamed x16, local copies, waits for them, and re-layouts  7.6 us
    ppermute x5, starting transfers between devices, local_fn(): moved = [lax.ppermute(x, 'cols', [(0, 1), (1, 0)]) for x in samples]  7.42 us
  transfers between devices with their start and end apart: 5, of which 0 were waited for; matrix products, arithmetic and copies ran while one was open for 3% of the time, Pallas kernels for 8%

profile of v2, /device:TPU:0, one launch (start us, length us, event | category | flops | bytes accessed | tf_op | source)
XLA Modules:
  0.0 54.9 jit_solution(14516676173290889845)
XLA Ops:
  0.0 3.4 %collective-permute-start.3 = (s32[16,128]{1,0:T(8,128)}, s32[16,128]{1,0:T(8,128)S(1)}, u32[]{:S(2)}, u32[]{:S(2)}) collective-permute-start(s32[16,128]{1,0:T(8,128)} %bitcast.4), channel_id=1, source_target_pairs={{0,4},{4,0},{1,5},{5,1},{2,6},{6,2},{3,7},{7,3}} | collective-permute-start | bytes 24584 | tf_op jit(solution)/shard_map/ppermute | solution.py:347
  3.4 0.0 collective-permute-start.4
  3.4 2.0 %collective-permute-start = (f32[2,8,2048]{2,1,0:T(8,128)}, f32[2,8,2048]{2,1,0:T(8,128)S(1)}, u32[]{:S(2)}, u32[]{:S(2)}) collective-permute-start(f32[2,8,2048]{2,1,0:T(8,128)} %y_ref.1), channel_id=1, source_target_pairs={{0,4},{4,0},{1,5},{5,1},{2,6},{6,2},{3,7},{7,3}} | collective-permute-start | bytes 393224 | tf_op jit(solution)/shard_map/ppermute | solution.py:347
  5.4 0.0 collective-permute-start.1
  5.4 2.0 %collective-permute-start.2 = (f32[4,2048]{1,0:T(4,128)}, f32[4,2048]{1,0:T(4,128)S(1)}, u32[]{:S(2)}, u32[]{:S(2)}) collective-permute-start(f32[4,2048]{1,0:T(4,128)} %wx_ref.1), channel_id=1, source_target_pairs={{0,4},{4,0},{1,5},{5,1},{2,6},{6,2},{3,7},{7,3}} | collective-permute-start | bytes 98312 | tf_op jit(solution)/shard_map/ppermute | solution.py:347
  7.4 0.8 %dynamic_slice.6 = f32[184]{0:T(256)S(1)} dynamic-slice(f32[368]{0:T(512)} %param.15, s32[]{:T(128)S(6)} %select_n.6), dynamic_slice_sizes={184} | dynamic-slice | bytes 1476 | tf_op jit(solution)/shard_map/dynamic_slice | solution.py:393
  8.2 0.8 %dynamic_slice.7 = f32[92]{0:T(128)S(1)} dynamic-slice(f32[368]{0:T(512)} %param.15, s32[]{:T(128)S(6)} %select_n.7), dynamic_slice_sizes={92} | dynamic-slice | bytes 740 | tf_op jit(solution)/shard_map/dynamic_slice | solution.py:394
  8.9 0.1 broadcast_multiply_fusion.1
  9.0 0.0 copy-start.3
  9.0 0.9 %copy-done.3 = f32[2,8,2048]{2,1,0:T(8,128)S(1)} copy-done((f32[2,8,2048]{2,1,0:T(8,128)S(1)}, f32[2,8,2048]{2,1,0:T(8,128)}, u32[]{:S(2)}) %copy-start.3) | copy-done | bytes 131096
  9.9 0.0 copy-start.4
  9.9 0.8 %copy-done.4 = f32[4,2048]{1,0:T(4,128)S(1)} copy-done((f32[4,2048]{1,0:T(4,128)S(1)}, f32[4,2048]{1,0:T(4,128)}, u32[]{:S(2)}) %copy-start.4) | copy-done | bytes 32792
  10.7 0.0 copy-start.5
  10.7 0.8 %copy-done.5 = f32[4,2048]{1,0:T(4,128)S(1)} copy-done((f32[4,2048]{1,0:T(4,128)S(1)}, f32[4,2048]{1,0:T(4,128)}, u32[]{:S(2)}) %copy-start.5) | copy-done | bytes 32792
  11.5 0.0 copy-start.6
  11.5 0.7 %copy-done.6 = s32[2048]{0:T(1024)S(1)} copy-done((s32[2048]{0:T(1024)S(1)}, s32[2048]{0:T(1024)}, u32[]{:S(2)}) %copy-start.6) | copy-done | bytes 8216
  12.2 0.0 copy-start.7
  12.2 0.7 %copy-done.7 = s32[2048]{0:T(1024)S(1)} copy-done((s32[2048]{0:T(1024)S(1)}, s32[2048]{0:T(1024)}, u32[]{:S(2)}) %copy-start.7) | copy-done | bytes 8216
  12.8 4.6 %spread_own.1 = (f32[5760,128]{1,0:T(8,128)S(1)}, f32[5760,128]{1,0:T(8,128)S(1)}, f32[5760,128]{1,0:T(8,128)S(1)}, f32[5760,128]{1,0:T(8,128)S(1)}) custom-call(f32[2,8,2048]{2,1,0:T(8,128)S(1)} %copy-done.3, f32[4,2048]{1,0:T(4,128)S(1)} %copy-done.4, f32[4,2048]{1,0:T(4,128)S(1)} %copy-done.5, s32[16,128]{1,0:T(8,128)S(1)} %bitcast.5, s32[16,128]{1,0:T(8,128)S(1)} %bitcast.7), custom_call_target="tpu_custom_call" | custom-call | flops 100000000 | bytes 10000000 | tf_op jit(solution)/shard_map/spread_own/pallas_call | solution.py:350
  17.5 0.0 collective-permute-done.3.iy_ref
  17.5 0.0 collective-permute-done.4.ix_ref
  17.5 0.0 collective-permute-done.1.wy_ref
  17.5 0.0 collective-permute-done.2.wx_ref
  17.5 0.0 collective-permute-done.y_ref
  17.5 4.6 %spread_received.1 = (f32[5760,128]{1,0:T(8,128)S(1)}, f32[5760,128]{1,0:T(8,128)S(1)}, f32[5760,128]{1,0:T(8,128)S(1)}, f32[5760,128]{1,0:T(8,128)S(1)}) custom-call(f32[2,8,2048]{2,1,0:T(8,128)S(1)} %collective-permute-done.y_ref, f32[4,2048]{1,0:T(4,128)S(1)} %collective-permute-done.1.wy_ref, f32[4,2048]{1,0:T(4,128)S(1)} %collective-permute-done.2.wx_ref, ...), custom_call_target="tpu_custom_call" | custom-call | flops 100000000 | bytes 10000000 | tf_op jit(solution)/shard_map/spread_received/pallas_call | solution.py:350
  22.2 0.0 copy-start
  22.2 1.3 %copy-done = bf16[768,768]{1,0:T(8,128)(2,1)S(1)} copy-done((bf16[768,768]{1,0:T(8,128)(2,1)S(1)}, bf16[768,768]{1,0:T(8,128)(2,1)}, u32[]{:S(2)}) %copy-start) | copy-done | bytes 1179672
  23.5 0.0 copy-start.1
  23.5 1.3 %copy-done.1 = bf16[768,768]{1,0:T(8,128)(2,1)S(1)} copy-done((bf16[768,768]{1,0:T(8,128)(2,1)S(1)}, bf16[768,768]{1,0:T(8,128)(2,1)}, u32[]{:S(2)}) %copy-start.1) | copy-done | bytes 1179672
  24.7 0.0 copy-start.2
  24.7 1.3 %copy-done.2 = f32[2,4,368,92]{2,1,3,0:T(4,128)S(1)} copy-done((f32[2,4,368,92]{2,1,3,0:T(4,128)S(1)}, f32[2,4,368,92]{2,1,3,0:T(4,128)}, u32[]{:S(2)}) %copy-start.2) | copy-done | bytes 1083416
  26.0 28.2 %transform.1 = f32[2,184,92]{2,1,0:T(8,128)S(1)} custom-call(f32[5760,128]{1,0:T(8,128)S(1)} %get-tuple-element.13.refs_0_, f32[5760,128]{1,0:T(8,128)S(1)} %get-tuple-element.14.refs_1_, f32[5760,128]{1,0:T(8,128)S(1)} %get-tuple-element.15.refs_2_, f32[5760,128]{1,0:T(8,128)S(1)} %get-tuple-element.16.refs_3_, f32[5760,128]{1,0:T(8,128)S(1)} %get-tuple-element.17.refs_4_, ...), custom_call_target="tpu_custom_call" | custom-call | tf_op jit(solution)/shard_map/transform/pallas_call | solution.py:366
  54.2 0.7 %broadcast_multiply_fusion = f32[2,184,92]{2,1,0:T(8,128)} fusion(f32[2,184,92]{2,1,0:T(8,128)S(1)} %transform.1, f32[184,92]{1,0:T(8,128)S(1)} %broadcast_multiply_fusion.1), kind=kLoop, calls=%fused_computation | loop fusion | flops 33856 | bytes 338560 | tf_op jit(solution)/shard_map/mul | solution.py:395
Async XLA Ops:
  0.0 17.5 %collective-permute-start.3 = (s32[16,128]{1,0:T(8,128)}, s32[16,128]{1,0:T(8,128)S(1)}, u32[]{:S(2)}, u32[]{:S(2)}) collective-permute-start(s32[16,128]{1,0:T(8,128)} %bitcast.4), channel_id=1, source_target_pairs={{0,4},{4,0},{1,5},{5,1},{2,6},{6,2},{3,7},{7,3}} | collective-permute-start | bytes 24584 | tf_op jit(solution)/shard_map/ppermute | solution.py:347
  3.4 14.1 %collective-permute-start.4 = (s32[16,128]{1,0:T(8,128)}, s32[16,128]{1,0:T(8,128)S(1)}, u32[]{:S(2)}, u32[]{:S(2)}) collective-permute-start(s32[16,128]{1,0:T(8,128)} %bitcast.6), channel_id=1, source_target_pairs={{0,4},{4,0},{1,5},{5,1},{2,6},{6,2},{3,7},{7,3}} | collective-permute-start | bytes 24584 | tf_op jit(solution)/shard_map/ppermute | solution.py:347
  3.4 14.1 %collective-permute-start = (f32[2,8,2048]{2,1,0:T(8,128)}, f32[2,8,2048]{2,1,0:T(8,128)S(1)}, u32[]{:S(2)}, u32[]{:S(2)}) collective-permute-start(f32[2,8,2048]{2,1,0:T(8,128)} %y_ref.1), channel_id=1, source_target_pairs={{0,4},{4,0},{1,5},{5,1},{2,6},{6,2},{3,7},{7,3}} | collective-permute-start | bytes 393224 | tf_op jit(solution)/shard_map/ppermute | solution.py:347
  5.4 12.1 %collective-permute-start.1 = (f32[4,2048]{1,0:T(4,128)}, f32[4,2048]{1,0:T(4,128)S(1)}, u32[]{:S(2)}, u32[]{:S(2)}) collective-permute-start(f32[4,2048]{1,0:T(4,128)} %wy_ref.1), channel_id=1, source_target_pairs={{0,4},{4,0},{1,5},{5,1},{2,6},{6,2},{3,7},{7,3}} | collective-permute-start | bytes 98312 | tf_op jit(solution)/shard_map/ppermute | solution.py:347
  5.4 12.1 %collective-permute-start.2 = (f32[4,2048]{1,0:T(4,128)}, f32[4,2048]{1,0:T(4,128)S(1)}, u32[]{:S(2)}, u32[]{:S(2)}) collective-permute-start(f32[4,2048]{1,0:T(4,128)} %wx_ref.1), channel_id=1, source_target_pairs={{0,4},{4,0},{1,5},{5,1},{2,6},{6,2},{3,7},{7,3}} | collective-permute-start | bytes 98312 | tf_op jit(solution)/shard_map/ppermute | solution.py:347
  9.0 0.9 %copy-start.3 = (f32[2,8,2048]{2,1,0:T(8,128)S(1)}, f32[2,8,2048]{2,1,0:T(8,128)}, u32[]{:S(2)}) copy-start(f32[2,8,2048]{2,1,0:T(8,128)} %y_ref.1) | copy-start | bytes 393220
  9.9 0.8 %copy-start.4 = (f32[4,2048]{1,0:T(4,128)S(1)}, f32[4,2048]{1,0:T(4,128)}, u32[]{:S(2)}) copy-start(f32[4,2048]{1,0:T(4,128)} %wy_ref.1) | copy-start | bytes 98308
  10.7 0.8 %copy-start.5 = (f32[4,2048]{1,0:T(4,128)S(1)}, f32[4,2048]{1,0:T(4,128)}, u32[]{:S(2)}) copy-start(f32[4,2048]{1,0:T(4,128)} %wx_ref.1) | copy-start | bytes 98308
  11.5 0.7 %copy-start.6 = (s32[2048]{0:T(1024)S(1)}, s32[2048]{0:T(1024)}, u32[]{:S(2)}) copy-start(s32[2048]{0:T(1024)} %param.12) | copy-start | bytes 24580
  12.2 0.7 %copy-start.7 = (s32[2048]{0:T(1024)S(1)}, s32[2048]{0:T(1024)}, u32[]{:S(2)}) copy-start(s32[2048]{0:T(1024)} %param.13) | copy-start | bytes 24580
  22.2 1.3 %copy-start = (bf16[768,768]{1,0:T(8,128)(2,1)S(1)}, bf16[768,768]{1,0:T(8,128)(2,1)}, u32[]{:S(2)}) copy-start(bf16[768,768]{1,0:T(8,128)(2,1)} %constant.23.refs_8_) | copy-start | bytes 3538948
  23.5 1.3 %copy-start.1 = (bf16[768,768]{1,0:T(8,128)(2,1)S(1)}, bf16[768,768]{1,0:T(8,128)(2,1)}, u32[]{:S(2)}) copy-start(bf16[768,768]{1,0:T(8,128)(2,1)} %constant.24.refs_9_) | copy-start | bytes 3538948
  24.7 1.3 %copy-start.2 = (f32[2,4,368,92]{2,1,3,0:T(4,128)S(1)}, f32[2,4,368,92]{2,1,3,0:T(4,128)}, u32[]{:S(2)}) copy-start(f32[2,4,368,92]{2,1,3,0:T(4,128)} %param.14) | copy-start | bytes 3250180

commit v3 on v2

--- a/solution.py
+++ b/solution.py
@@ -1,4 +1,3 @@
-import functools
 import functools
 import math
 
@@ -23,11 +22,12 @@
 N_TGT = 12
 COL_BLK = 368
 VR = 384
+VS = 392
 KV = 2 * VR
 LANES, ROWS = 128, 16
 EDGE = 6
 N_CHUNK = 6
-N_COPY = 4
+N_COPY = 3
 CHUNK_TILES = [(1 + 2 * j, 2 + 2 * j) for j in range(5)] + [(0, 11)]
 
 
@@ -55,6 +55,54 @@
             jnp.asarray(e2.reshape(N_CHUNK * LANES, 2 * P_ALL).astype(np.float32)).astype(BF16))
 
 
+def exchange_kernel(y_hbm, wy_hbm, wx_hbm, iy_hbm, ix_hbm, y_ref, wy_ref, wx_ref, addr_ref, roff_ref, *refs):
+    accs = refs[:2 * N_COPY]
+    y_in, iy, ix, y_send, in_sem, send_sem, recv_sem = refs[2 * N_COPY:]
+    k = lax.axis_index('cols')
+    r = lax.axis_index('rows')
+    other = {'cols': 1 - k}
+    barrier = pltpu.get_barrier_semaphore()
+    pl.semaphore_signal(barrier, inc=1, device_id=other, device_id_type=MESH)
+    loads = [(iy_hbm, iy), (ix_hbm, ix), (y_hbm, y_in), (wy_hbm, wy_ref.at[0]), (wx_hbm, wx_ref.at[0])]
+    loads = [pltpu.make_async_copy(a, b, in_sem.at[i]) for i, (a, b) in enumerate(loads)]
+    for c in loads:
+        c.start()
+
+    def send(i, src, dst):
+        c = pltpu.make_async_remote_copy(src_ref=src, dst_ref=dst, send_sem=send_sem.at[i], recv_sem=recv_sem.at[i],
+                                         device_id=other, device_id_type=MESH)
+        c.start()
+        return c
+
+    loads[0].wait()
+    loads[1].wait()
+    row = iy[...] - r * ROW_BLK
+    tile = jnp.zeros_like(row)
+    for t in range(1, N_SRC):
+        tile = tile + jnp.where(row >= STRIDE_U * t, 1, 0)
+    addr_ref[0] = tile * VS + (ix[...] - k * COL_BLK)
+    roff_ref[0] = row - STRIDE_U * tile
+    loads[2].wait()
+    y_re, y_im = y_in[0], y_in[1]
+    low = jnp.concatenate([y_re[0:4], y_im[0:4]], axis=0)
+    high = jnp.concatenate([y_re[4:8], y_im[4:8]], axis=0)
+    y_ref[0] = jnp.where(k == 0, low, high)
+    y_send[...] = jnp.where(k == 0, high, low)
+    loads[3].wait()
+    loads[4].wait()
+    pl.semaphore_wait(barrier, 1)
+    copies = [send(0, wy_ref.at[0], wy_ref.at[1]), send(1, wx_ref.at[0], wx_ref.at[1]), send(2, addr_ref.at[0], addr_ref.at[1]),
+              send(3, roff_ref.at[0], roff_ref.at[1]), send(4, y_send, y_ref.at[1])]
+
+    def zero(i, _):
+        for a in accs:
+            a[pl.ds(pl.multiple_of(i * VS, 8), VS), :] = jnp.zeros((VS, LANES), F32)
+        return 0
+    lax.fori_loop(0, N_SRC, zero, 0)
+    for c in copies:
+        c.wait()
+
+
 def split3(x):
     hi = x.astype(BF16).astype(F32)
     rest = x - hi
@@ -62,32 +110,13 @@
     return [hi, mid, rest - mid]
 
 
-def spread_kernel(received, y_ref, wy_ref, wx_ref, iy_ref, ix_ref, *refs):
-    accs = refs[:N_COPY]
-    qa, qb, y_sel, roff, addr_v, addr, sem = refs[N_COPY:]
-    k = lax.axis_index('cols')
-    r = lax.axis_index('rows')
-    half = 1 - k if received else k
+def spread_kernel(addr_ref, y_ref, wy_ref, wx_ref, roff_ref, *refs):
+    accs = refs[2 * N_COPY:4 * N_COPY]
+    addr, sem = refs[4 * N_COPY], refs[-1]
+    q_refs = refs[4 * N_COPY + 1:-1]
+    to_smem = pltpu.make_async_copy(addr_ref, addr, sem)
+    to_smem.start()
     n = y_ref.shape[2]
-
-    row = iy_ref[...] - r * ROW_BLK
-    tile = jnp.zeros_like(row)
-    for t in range(1, N_SRC):
-        tile = tile + jnp.where(row >= STRIDE_U * t, 1, 0)
-    addr_v[...] = tile * VR + (ix_ref[...] - half * COL_BLK)
-    roff[...] = row - STRIDE_U * tile
-    to_smem = pltpu.make_async_copy(addr_v, addr, sem)
-    to_smem.start()
-    y_re, y_im = y_ref[0], y_ref[1]
-    low = jnp.concatenate([y_re[0:4], y_im[0:4]], axis=0)
-    high = jnp.concatenate([y_re[4:8], y_im[4:8]], axis=0)
-    y_sel[...] = jnp.where(k == 0, low, high)
-
-    def zero(i, _):
-        for a in accs:
-            a[pl.ds(pl.multiple_of(i * VR, 8), VR), :] = jnp.zeros((VR, LANES), F32)
-        return 0
-    lax.fori_loop(0, N_SRC, zero, 0)
 
     r0 = lax.broadcasted_iota(jnp.int32, (80, 256), 0)
     l0 = lax.broadcasted_iota(jnp.int32, (80, 256), 1)
@@ -97,11 +126,11 @@
     rr = lax.broadcasted_iota(jnp.int32, (ROWS, 256), 0)
     n_blk = n // 256
 
-    def prep(i, q_ref):
+    def prep(i, slot, q_ref):
         ds = [pl.ds(pl.multiple_of((i + n_blk * h) * LANES, LANES), LANES) for h in range(2)]
-        y = jnp.concatenate([y_sel[:, s] for s in ds], axis=1)
-        wy = jnp.concatenate([wy_ref[:, s] for s in ds], axis=1)
-        d = rr - jnp.concatenate([roff[pl.ds(i + n_blk * h, 1), :] for h in range(2)], axis=1)
+        y = jnp.concatenate([y_ref[slot, :, s] for s in ds], axis=1)
+        wy = jnp.concatenate([wy_ref[slot, :, s] for s in ds], axis=1)
+        d = rr - jnp.concatenate([roff_ref[slot, pl.ds(i + n_blk * h, 1), :] for h in range(2)], axis=1)
         w16 = jnp.zeros((ROWS, 256), F32)
         for a in range(4):
             w16 = jnp.where(d == a, wy[a:a + 1], w16)
@@ -111,34 +140,38 @@
 
     top = lax.broadcasted_iota(jnp.int32, (8, LANES), 0) < 4
 
-    def scatter(i, q_ref):
-        wx = jnp.concatenate([wx_ref[:, pl.ds(pl.multiple_of((i + n_blk * h) * LANES, LANES), LANES)] for h in range(2)], axis=0)
+    def scatter(i, qs):
+        ds = [pl.ds(pl.multiple_of((i + n_blk * h) * LANES, LANES), LANES) for h in range(2)]
+        wx = [jnp.concatenate([wx_ref[slot, :, s] for s in ds], axis=0) for slot in range(2)]
         for j in range(LANES):
-            col = jnp.broadcast_to(wx[:, j:j + 1], (8, LANES))
+            cols = [jnp.broadcast_to(wx[slot][:, j:j + 1], (8, LANES)) for slot in range(2)]
             for h in range(2):
-                acc = accs[(2 * j + h) % N_COPY]
-                base = addr[i + n_blk * h, j] + (0 if h else 4)
-                q = jnp.broadcast_to(q_ref[j + LANES * h:j + LANES * h + 1, :], (8, LANES))
-                s = pl.ds(base, 8)
-                c = jnp.where(top, 0.0, col) if h else jnp.where(top, col, 0.0)
-                acc[s, :] = acc[s, :] + c * q
-
-    prep(0, qa)
+                for slot in range(2):
+                    acc = accs[slot * N_COPY + (2 * j + h) % N_COPY]
+                    base = addr[slot, i + n_blk * h, j] + (0 if h else 4)
+                    q = jnp.broadcast_to(qs[slot][j + LANES * h:j + LANES * h + 1, :], (8, LANES))
+                    s = pl.ds(base, 8)
+                    c = jnp.where(top, 0.0, cols[slot]) if h else jnp.where(top, cols[slot], 0.0)
+                    acc[s, :] = acc[s, :] + c * q
+
+    qa, qb = q_refs[:2], q_refs[2:]
+    for slot in range(2):
+        prep(0, slot, qa[slot])
     to_smem.wait()
 
     def two_blocks(i, _):
-        prep(2 * i + 1, qb)
-        scatter(2 * i, qa)
-        prep(lax.rem(2 * i + 2, n_blk), qa)
-        scatter(2 * i + 1, qb)
+        for step, now, then in ((0, qa, qb), (1, qb, qa)):
+            for slot in range(2):
+                prep(lax.rem(2 * i + step + 1, n_blk), slot, then[slot])
+            scatter(2 * i + step, now)
         return 0
     lax.fori_loop(0, n_blk // 2, two_blocks, 0)
 
 
 def transform_kernel(*refs):
     own, nbr = refs[:N_COPY], refs[N_COPY:2 * N_COPY]
-    (e1_ref, e2_ref, s_ref, out_ref, gch, raw0, f0, f11, gps, gns, msg, recv, gpr, gnr, e2f, st, img, psend, precv,
-     msend_sem, mrecv_sem, gsend_sem, grecv_sem, psend_sem, precv_sem) = refs[2 * N_COPY:]
+    (e1_hbm, e2_hbm, s_hbm, d_hbm, out_ref, e1_ref, e2_ref, s_ref, d_ref, dd, gch, raw0, f0, f11, gps, gns, msg, recv, gpr, gnr, e2f, st, img, psend, precv,
+     msend_sem, mrecv_sem, gsend_sem, grecv_sem, psend_sem, precv_sem, in_sem) = refs[2 * N_COPY:]
     k = lax.axis_index('cols')
     r = lax.axis_index('rows')
     chip, core = r // 2, r % 2
@@ -149,6 +182,10 @@
         pl.semaphore_signal(barrier, inc=1, device_id={'rows': d}, device_id_type=MESH)
     pl.semaphore_signal(barrier, inc=1, device_id={'cols': 1 - k}, device_id_type=MESH)
 
+    loads = [pltpu.make_async_copy(a, b, in_sem.at[i]) for i, (a, b) in
+             enumerate(((e1_hbm, e1_ref), (e2_hbm, e2_ref), (s_hbm, s_ref), (d_hbm, d_ref)))]
+    for c in loads:
+        c.start()
     slots = ((own, k), (nbr, 1 - k))
     lane16 = lax.broadcasted_iota(jnp.int32, (ROWS, LANES), 1) & 15
     sub16 = lax.broadcasted_iota(jnp.int32, (ROWS, LANES), 0)
@@ -160,7 +197,7 @@
             wanted[m] = {t: d for t, d in deltas.items() if abs(d) < ROWS}
         loaded = {}
         for t in sorted({t for w in wanted.values() for t in w}):
-            s = pl.ds(t * VR + off, ROWS)
+            s = pl.ds(t * VS + off, ROWS)
             v = accs[0][s, :]
             for acc in accs[1:]:
                 v = v + acc[s, :]
@@ -179,11 +216,12 @@
 
     def merge_all(targets, put):
         def rows(i, _):
-            for accs, half in slots:
-                off = pl.multiple_of(i * ROWS, ROWS)
-                put(pl.multiple_of(half * VR + off, ROWS), merged(accs, off, targets))
+            for step in range(2):
+                for accs, half in slots:
+                    off = pl.multiple_of((2 * i + 1 + step) * ROWS, ROWS)
+                    put(pl.multiple_of(half * VR + off, ROWS), merged(accs, off, targets))
             return 0
-        lax.fori_loop(1, VR // ROWS - 1, rows, 0)
+        lax.fori_loop(0, VR // (2 * ROWS) - 1, rows, 0)
         last = VR - ROWS
         a = [merged(accs, 0, targets) for accs, _ in slots]
         b = [merged(accs, last, targets) for accs, _ in slots]
@@ -227,6 +265,7 @@
         recv[j, r] = msg[j, r]
 
     merge_all(CHUNK_TILES[0], put_chunk)
+    loads[0].wait()
     first_dft(0, gch[...])
     pl.semaphore_wait(barrier, 4)
     post(0)
@@ -270,6 +309,8 @@
     first_dft(N_CHUNK - 1, gch[...])
     post(N_CHUNK - 1)
 
+    for c in loads[1:]:
+        c.wait()
     for j in range(N_CHUNK):
         v = e2_ref[128 * j:128 * j + 128, :]
         e2f[j, 0:128, :] = v
@@ -279,6 +320,13 @@
     for s in range(2):
         for c in range(4):
             st[s, c, 0:Q_BLK, 0:N_IMG] = s_ref[s, :, c, :]
+
+    half_p = jnp.where(k == 0, d_ref[:, 0:P_BLK], d_ref[:, P_BLK:2 * P_BLK])
+    part_q = d_ref[:, 0:Q_BLK]
+    for i in range(1, 4):
+        part_q = jnp.where(r == i, d_ref[:, Q_BLK * i:Q_BLK * (i + 1)], part_q)
+    part_q = jnp.concatenate([part_q, jnp.zeros((1, LANES - Q_BLK), F32)], axis=1)
+    dd[...] = jnp.broadcast_to(part_q, (8, LANES)).T[0:Q_BLK, 0:1] * half_p
 
     grp = lax.broadcasted_iota(jnp.int32, (Q_PAD, 128), 1) >> 4
 
@@ -329,46 +377,51 @@
             message(j, i).wait_send()
     swap.wait()
     total = mine + precv[...]
-    out_ref[0] = total[0:Q_BLK, 0:P_BLK].T
-    out_ref[1] = total[0:Q_BLK, P_PAD:P_PAD + P_BLK].T
+    out_ref[0] = (total[0:Q_BLK, 0:P_BLK] * dd[...]).T
+    out_ref[1] = (total[0:Q_BLK, P_PAD:P_PAD + P_BLK] * dd[...]).T
 
 
 def solution(mesh):
     sample_spec = ('exam', 'rows', 'cols')
     vmem = pl.BlockSpec(memory_space=pltpu.VMEM)
+    hbm = pl.BlockSpec(memory_space=pltpu.HBM)
     sds = jax.ShapeDtypeStruct
 
     def local_fn(kspace, wts_y, wts_x, idx_y, idx_x, coil_maps, deapod):
         n = kspace.shape[2]
-        row_id = lax.axis_index('rows')
-        col_id = lax.axis_index('cols')
         e1, e2 = dft_constants()
-        samples = (kspace, wts_y, wts_x, idx_y.reshape(16, LANES), idx_x.reshape(16, LANES))
-        moved = [lax.ppermute(x, 'cols', [(0, 1), (1, 0)]) for x in samples]
-
-        def spread(received, args):
-            return pl.pallas_call(
-                functools.partial(spread_kernel, received),
-                out_shape=[sds((N_SRC * VR, LANES), F32)] * N_COPY,
-                in_specs=[vmem] * 5,
-                out_specs=[vmem] * N_COPY,
-                scratch_shapes=[pltpu.VMEM((256, LANES), F32), pltpu.VMEM((256, LANES), F32), pltpu.VMEM((8, n), F32),
-                                pltpu.VMEM((16, LANES), jnp.int32), pltpu.VMEM((16, LANES), jnp.int32),
-                                pltpu.SMEM((16, LANES), jnp.int32), pltpu.SemaphoreType.DMA],
-                compiler_params=pltpu.CompilerParams(vmem_limit_bytes=16 * 2**20),
-                cost_estimate=pl.CostEstimate(flops=10**8, bytes_accessed=10**7, transcendentals=0),
-                name='spread_received' if received else 'spread_own',
-            )(*args)
-
-        accs = spread(False, samples)
-        accs += spread(True, moved)
+        acc_shape = [sds((N_SRC * VS, LANES), F32)] * (2 * N_COPY)
+        *samples, = pl.pallas_call(
+            exchange_kernel,
+            out_shape=[sds((2, 8, n), F32), sds((2, 4, n), F32), sds((2, 4, n), F32), sds((2, 16, LANES), jnp.int32),
+                       sds((2, 16, LANES), jnp.int32)] + acc_shape,
+            in_specs=[hbm] * 5,
+            out_specs=[vmem] * (5 + 2 * N_COPY),
+            scratch_shapes=[pltpu.VMEM((2, 8, n), F32), pltpu.VMEM((16, LANES), jnp.int32), pltpu.VMEM((16, LANES), jnp.int32),
+                            pltpu.VMEM((8, n), F32), pltpu.SemaphoreType.DMA((5,)), pltpu.SemaphoreType.DMA((5,)),
+                            pltpu.SemaphoreType.DMA((5,))],
+            compiler_params=pltpu.CompilerParams(collective_id=0, has_side_effects=True, vmem_limit_bytes=8 * 2**20),
+            name='exchange',
+        )(kspace, wts_y, wts_x, idx_y.reshape(16, LANES), idx_x.reshape(16, LANES))
+        y8, wy, wx, addr, roff = samples[:5]
+        accs = pl.pallas_call(
+            spread_kernel,
+            out_shape=acc_shape,
+            in_specs=[vmem] * (5 + 2 * N_COPY),
+            out_specs=[vmem] * (2 * N_COPY),
+            scratch_shapes=[pltpu.SMEM((2, 16, LANES), jnp.int32)] + [pltpu.VMEM((256, LANES), F32)] * 4 + [pltpu.SemaphoreType.DMA],
+            input_output_aliases={5 + i: i for i in range(2 * N_COPY)},
+            compiler_params=pltpu.CompilerParams(vmem_limit_bytes=8 * 2**20),
+            name='spread',
+        )(addr, y8, wy, wx, roff, *samples[5:])
         maps = jnp.transpose(coil_maps, (0, 3, 1, 2))
-        part = pl.pallas_call(
+        return pl.pallas_call(
             transform_kernel,
             out_shape=sds((2, P_BLK, Q_BLK), F32),
-            in_specs=[vmem] * (2 * N_COPY + 3),
+            in_specs=[vmem] * (2 * N_COPY) + [hbm] * 4,
             out_specs=vmem,
-            scratch_shapes=[pltpu.VMEM((KV, 256), BF16)] + [pltpu.VMEM((KV, LANES), F32)] * 3 + [
+            scratch_shapes=[pltpu.VMEM((KV, KV), BF16), pltpu.VMEM((KV, 2 * P_ALL), BF16), pltpu.VMEM((2, Q_BLK, 4, N_IMG), F32),
+                            pltpu.VMEM((1, N_IMG), F32), pltpu.VMEM((Q_BLK, P_BLK), F32), pltpu.VMEM((KV, 256), BF16)] + [pltpu.VMEM((KV, LANES), F32)] * 3 + [
                 pltpu.VMEM((96, LANES), F32),
                 pltpu.VMEM((48, LANES), F32),
                 pltpu.VMEM((N_CHUNK, 4, Q_PAD, 256), BF16),
@@ -386,13 +439,11 @@
                 pltpu.SemaphoreType.DMA((2,)),
                 pltpu.SemaphoreType.DMA,
                 pltpu.SemaphoreType.DMA,
+                pltpu.SemaphoreType.DMA((4,)),
             ],
             compiler_params=pltpu.CompilerParams(collective_id=1, has_side_effects=True, vmem_limit_bytes=24 * 2**20),
             name='transform',
-        )(*accs, e1, e2, maps)
-        d_rows = lax.dynamic_slice(deapod, (col_id * P_BLK,), (P_BLK,))
-        d_cols = lax.dynamic_slice(deapod, (row_id * Q_BLK,), (Q_BLK,))
-        return part * (d_rows[:, None] * d_cols[None, :])
+        )(*accs, e1, e2, maps, deapod.reshape(1, N_IMG))
 
     return jax.shard_map(
         local_fn,

time: 55.4 us -> 44.1 us (0.80)
  starting transfers between devices: 7.42 us -> 0 us
  local copies, waits for them, and re-layouts: 9.1 us -> 4.52 us
  Pallas kernels: 37.5 us -> 39.2 us
  other arithmetic: 0.79 us -> 0 us
    ppermute x5 -> x0, starting transfers between devices: 7.42 us -> none  [local_fn(): moved = [lax.ppermute(x, 'cols', [(0, 1), (1, 0)]) for x in samples]]
    pallas_call x2, Pallas kernels: 9.27 us -> 13.1 us  [the longest x1 7.64 us: local_fn(): pl.pallas_call(exchange_kernel, out_shape=[sds((2, 8, n), F32), sds((2, 4...]
    unnamed x16 -> x19, local copies, waits for them, and re-layouts: 7.6 us -> 4.51 us
    pallas_call x1, Pallas kernels: 28.2 us -> 26 us  [local_fn(): pl.pallas_call(transform_kernel, out_shape=sds((2, P_BLK, Q_BLK), F32), i...]
    dynamic_slice x2 -> x0, local copies, waits for them, and re-layouts: 1.51 us -> none  [the longest x1 0.75 us: local_fn(): d_cols = lax.dynamic_slice(deapod, (row_id * Q_BLK,), (Q_BLK,))]
    mul x2 -> x0, other arithmetic: 0.79 us -> none  [local_fn(): return part * (d_rows[:, None] * d_cols[None, :])]
  transfers between devices with their start and end apart: 5 -> 0, of which waited for: 0 -> 0; matrix products, arithmetic and copies ran while one was open for 3% -> 0% of each run, Pallas kernels for 8% -> 0%
where the time goes in v3:
time: 44.1 us; the launch traced here: 43.8 us
  Pallas kernels  39.2 us (89%)
  local copies, waits for them, and re-layouts  4.52 us (10%)
    pallas_call x1, Pallas kernels, local_fn(): pl.pallas_call(transform_kernel, out_shape=sds((2, P_BLK, Q_BLK), F32), i...  26 us
    pallas_call x1, Pallas kernels, local_fn(): pl.pallas_call(exchange_kernel, out_shape=[sds((2, 8, n), F32), sds((2, 4...  7.64 us
    pallas_call x1, Pallas kernels, local_fn(): pl.pallas_call(spread_kernel, out_shape=acc_shape, in_specs=[vmem] * (5 +...  5.48 us
    unnamed x19, local copies, waits for them, and re-layouts  4.51 us

profile of v3, /device:TPU:0, one launch (start us, length us, event | category | flops | bytes accessed | tf_op | source)
XLA Modules:
  0.0 43.8 jit_solution(3642691788846389473)
XLA Ops:
  0.0 0.0 copy-start.3
  0.0 0.9 %copy-done.3 = f32[2,8,2048]{2,1,0:T(8,128)S(1)} copy-done((f32[2,8,2048]{2,1,0:T(8,128)S(1)}, f32[2,8,2048]{2,1,0:T(8,128)}, u32[]{:S(2)}) %copy-start.3) | copy-done | bytes 131096
  0.9 0.0 copy-start.4
  0.9 0.8 %copy-done.4 = f32[4,2048]{1,0:T(4,128)S(1)} copy-done((f32[4,2048]{1,0:T(4,128)S(1)}, f32[4,2048]{1,0:T(4,128)}, u32[]{:S(2)}) %copy-start.4) | copy-done | bytes 32792
  1.7 0.0 copy-start.5
  1.7 0.8 %copy-done.5 = f32[4,2048]{1,0:T(4,128)S(1)} copy-done((f32[4,2048]{1,0:T(4,128)S(1)}, f32[4,2048]{1,0:T(4,128)}, u32[]{:S(2)}) %copy-start.5) | copy-done | bytes 32792
  2.4 0.0 copy-start.6
  2.4 0.7 %copy-done.6 = s32[2048]{0:T(1024)S(1)} copy-done((s32[2048]{0:T(1024)S(1)}, s32[2048]{0:T(1024)}, u32[]{:S(2)}) %copy-start.6) | copy-done | bytes 8216
  3.1 0.0 copy-start.7
  3.1 0.7 %copy-done.7 = s32[2048]{0:T(1024)S(1)} copy-done((s32[2048]{0:T(1024)S(1)}, s32[2048]{0:T(1024)}, u32[]{:S(2)}) %copy-start.7) | copy-done | bytes 8216
  3.8 7.6 %exchange.1 = (f32[2,8,2048]{2,1,0:T(8,128)S(1)}, f32[2,4,2048]{2,1,0:T(4,128)S(1)}, f32[2,4,2048]{2,1,0:T(4,128)S(1)}, s32[2,16,128]{2,1,0:T(8,128)S(1)}, s32[2...) custom-call(f32[2,8,2048]{2,1,0:T(8,128)S(1)} %copy-done.3, ...), custom_call_target="tpu_custom_call" | custom-call | tf_op jit(solution)/shard_map/exchange/pallas_call | solution.py:394
  11.5 0.0 copy-start.8
  11.5 0.0 copy-start
  11.5 0.0 copy-start.1
  11.5 0.0 copy-start.2
  11.5 5.5 %spread.1 = (f32[5880,128]{1,0:T(8,128)S(1)}, f32[5880,128]{1,0:T(8,128)S(1)}, f32[5880,128]{1,0:T(8,128)S(1)}, f32[5880,128]{1,0:T(8,128)S(1)}, f32[5880,128]{1,0:T(8,128)S(1)}, /*index=5*/f32[5880,128]{1,0:T(8,128)S(1)}) custom-call(s32[2,16,128]{2,1,0:T(8,128)S(1)} %get-tuple-element.22., ...), custom_call_target="tpu_custom_call", output_to_operand_aliasing={{0}: (5, {}), {1}: (6, {}), {2}: (7, {}), {3}: (8, {}), {4}... | custom-call | tf_op jit(solution)/shard_map/spread/pallas_call | solution.py:407
  17.0 0.0 copy-done.8
  17.0 0.0 copy-done
  17.0 0.0 copy-done.1
  17.0 0.0 copy-done.2
  17.1 26.0 %transform.1 = f32[2,184,92]{2,1,0:T(8,128)S(1)} custom-call(f32[5880,128]{1,0:T(8,128)S(1)} %get-tuple-element.33.refs_0_, f32[5880,128]{1,0:T(8,128)S(1)} %get-tuple-element.34.refs_1_, f32[5880,128]{1,0:T(8,128)S(1)} %get-tuple-element.35.refs_2_, f32[5880,128]{1,0:T(8,128)S(1)} %get-tuple-element.36.refs_3_, f32[5880,128]{1,0:T(8,128)S(1)} %get-tuple-element.37.refs_4_, ...), custom_call_target="tpu_custom_call" | custom-call | tf_op jit(solution)/shard_map/transform/pallas_call | solution.py:418
  43.1 0.7 %copy.23 = f32[2,184,92]{2,1,0:T(8,128)} copy(f32[2,184,92]{2,1,0:T(8,128)S(1)} %transform.1) | data formatting | bytes 270848
  (1 shorter events, 0.0 us)
Async XLA Ops:
  0.0 0.9 %copy-start.3 = (f32[2,8,2048]{2,1,0:T(8,128)S(1)}, f32[2,8,2048]{2,1,0:T(8,128)}, u32[]{:S(2)}) copy-start(f32[2,8,2048]{2,1,0:T(8,128)} %y_hbm.1) | copy-start | bytes 393220
  0.9 0.8 %copy-start.4 = (f32[4,2048]{1,0:T(4,128)S(1)}, f32[4,2048]{1,0:T(4,128)}, u32[]{:S(2)}) copy-start(f32[4,2048]{1,0:T(4,128)} %wy_hbm.1) | copy-start | bytes 98308
  1.7 0.8 %copy-start.5 = (f32[4,2048]{1,0:T(4,128)S(1)}, f32[4,2048]{1,0:T(4,128)}, u32[]{:S(2)}) copy-start(f32[4,2048]{1,0:T(4,128)} %wx_hbm.1) | copy-start | bytes 98308
  2.4 0.7 %copy-start.6 = (s32[2048]{0:T(1024)S(1)}, s32[2048]{0:T(1024)}, u32[]{:S(2)}) copy-start(s32[2048]{0:T(1024)} %param.12) | copy-start | bytes 24580
  3.1 0.7 %copy-start.7 = (s32[2048]{0:T(1024)S(1)}, s32[2048]{0:T(1024)}, u32[]{:S(2)}) copy-start(s32[2048]{0:T(1024)} %param.13) | copy-start | bytes 24580
  11.5 5.5 %copy-start.8 = (f32[368]{0:T(512)S(1)}, f32[368]{0:T(512)}, u32[]{:S(2)}) copy-start(f32[368]{0:T(512)} %param.15) | copy-start | bytes 4420
  11.5 5.6 %copy-start = (bf16[768,768]{1,0:T(8,128)(2,1)S(1)}, bf16[768,768]{1,0:T(8,128)(2,1)}, u32[]{:S(2)}) copy-start(bf16[768,768]{1,0:T(8,128)(2,1)} %constant.6.refs_6_) | copy-start | bytes 3538948
  11.5 5.5 %copy-start.1 = (bf16[768,768]{1,0:T(8,128)(2,1)S(1)}, bf16[768,768]{1,0:T(8,128)(2,1)}, u32[]{:S(2)}) copy-start(bf16[768,768]{1,0:T(8,128)(2,1)} %constant.7.refs_7_) | copy-start | bytes 3538948
  11.5 5.5 %copy-start.2 = (f32[2,4,368,92]{2,1,3,0:T(4,128)S(1)}, f32[2,4,368,92]{2,1,3,0:T(4,128)}, u32[]{:S(2)}) copy-start(f32[2,4,368,92]{2,1,3,0:T(4,128)} %param.14) | copy-start | bytes 3250180

commit v4 on v3

--- a/solution.py
+++ b/solution.py
@@ -81,7 +81,7 @@
     for t in range(1, N_SRC):
         tile = tile + jnp.where(row >= STRIDE_U * t, 1, 0)
     addr_ref[0] = tile * VS + (ix[...] - k * COL_BLK)
-    roff_ref[0] = row - STRIDE_U * tile
+    roff_ref[0] = (row + 14) & 15
     loads[2].wait()
     y_re, y_im = y_in[0], y_in[1]
     low = jnp.concatenate([y_re[0:4], y_im[0:4]], axis=0)
@@ -130,7 +130,7 @@
         ds = [pl.ds(pl.multiple_of((i + n_blk * h) * LANES, LANES), LANES) for h in range(2)]
         y = jnp.concatenate([y_ref[slot, :, s] for s in ds], axis=1)
         wy = jnp.concatenate([wy_ref[slot, :, s] for s in ds], axis=1)
-        d = rr - jnp.concatenate([roff_ref[slot, pl.ds(i + n_blk * h, 1), :] for h in range(2)], axis=1)
+        d = (rr - jnp.concatenate([roff_ref[slot, pl.ds(i + n_blk * h, 1), :] for h in range(2)], axis=1)) & 15
         w16 = jnp.zeros((ROWS, 256), F32)
         for a in range(4):
             w16 = jnp.where(d == a, wy[a:a + 1], w16)
@@ -207,7 +207,7 @@
             out = None
             for t, d in wanted[m].items():
                 lo, hi = max(0, d), min(15, 15 + d)
-                v = pltpu.roll(loaded[t], d % LANES, 1) if d else loaded[t]
+                v = loaded[t]
                 if lo > 0 or hi < 15:
                     v = jnp.where((lane16 >= lo) & (lane16 <= hi), v, 0.0)
                 out = v if out is None else out + v
@@ -279,7 +279,7 @@
 
     gp = jnp.zeros((96, LANES), F32)
     for c in range(8):
-        gp = jnp.where((la >> 1) == c, shifted(raw0[96 * c:96 * c + 96, :], 2 * c), gp)
+        gp = jnp.where((la >> 1) == c, shifted(raw0[96 * c:96 * c + 96, :], 2 * c - 14), gp)
     gps[...] = gp
     gn = jnp.zeros((48, LANES), F32)
     for c in range(16):
@@ -312,10 +312,11 @@
     for c in loads[1:]:
         c.wait()
     for j in range(N_CHUNK):
-        v = e2_ref[128 * j:128 * j + 128, :]
-        e2f[j, 0:128, :] = v
-        e2f[j, 128:256, 0:P_ALL] = -v[:, P_ALL:2 * P_ALL]
-        e2f[j, 128:256, P_ALL:2 * P_ALL] = v[:, 0:P_ALL]
+        for h in range(2):
+            v = e2_ref[LANES * j + 64 * h:LANES * j + 64 * h + 64, :]
+            e2f[j, LANES * h:LANES * h + 64, :] = v
+            e2f[j, LANES * h + 64:LANES * h + LANES, 0:P_ALL] = -v[:, P_ALL:2 * P_ALL]
+            e2f[j, LANES * h + 64:LANES * h + LANES, P_ALL:2 * P_ALL] = v[:, 0:P_ALL]
     st[...] = jnp.zeros_like(st)
     for s in range(2):
         for c in range(4):
@@ -328,26 +329,25 @@
     part_q = jnp.concatenate([part_q, jnp.zeros((1, LANES - Q_BLK), F32)], axis=1)
     dd[...] = jnp.broadcast_to(part_q, (8, LANES)).T[0:Q_BLK, 0:1] * half_p
 
-    grp = lax.broadcasted_iota(jnp.int32, (Q_PAD, 128), 1) >> 4
-
-    def regroup(j):
-        v = [recv[j, s // 2, :, 128 * (s % 2):128 * (s % 2) + 128].astype(F32) for s in range(8)]
-        for b in range(3):
-            bit = 1 << b
-            m = (grp & bit) == 0
-            for s in range(8):
+    coil = (lax.broadcasted_iota(jnp.int32, (Q_PAD, LANES), 1) >> 4) & 3
+
+    def regroup(j, pair):
+        v = [recv[j, 2 * pair + s // 2, :, LANES * (s % 2):LANES * (s % 2 + 1)] for s in range(4)]
+        for bit in (1, 2):
+            m = (coil & bit) == 0
+            for s in range(4):
                 if s & bit:
                     continue
                 x, y = v[s], v[s | bit]
-                v[s] = jnp.where(m, x, pltpu.roll(y, 16 * bit, 1))
-                v[s | bit] = jnp.where(m, pltpu.roll(x, 128 - 16 * bit, 1), y)
-        return [x.astype(BF16) for x in v]
+                v[s] = jnp.where(m, x, pltpu.roll(y, ROWS * bit, 1))
+                v[s | bit] = jnp.where(m, pltpu.roll(x, LANES - ROWS * bit, 1), y)
+        return v
 
     def second_dft(j):
         for i in range(3):
             arrival(j, i).wait_recv()
-        v = regroup(j)
-        lhs = jnp.concatenate([jnp.concatenate([v[c], v[4 + c]], axis=1) for c in range(4)], axis=0)
+        first, second = regroup(j, 0), regroup(j, 1)
+        lhs = jnp.concatenate([jnp.concatenate([first[c], second[c]], axis=1) for c in range(4)], axis=0)
         return jnp.dot(lhs, e2f[j], preferred_element_type=F32)
 
     img[...] = second_dft(0)

time: 44.1 us -> 41.7 us (0.946)
  Pallas kernels: 39.2 us -> 36.7 us
    pallas_call x1, Pallas kernels: 26 us -> 23.6 us  [local_fn(): pl.pallas_call(transform_kernel, out_shape=sds((2, P_BLK, Q_BLK), F32), i...]
where the time goes in v4:
time: 41.7 us; the launch traced here: 41.4 us
  Pallas kernels  36.7 us (88%)
  local copies, waits for them, and re-layouts  4.52 us (11%)
    pallas_call x1, Pallas kernels, local_fn(): pl.pallas_call(transform_kernel, out_shape=sds((2, P_BLK, Q_BLK), F32), i...  23.6 us
    pallas_call x1, Pallas kernels, local_fn(): pl.pallas_call(exchange_kernel, out_shape=[sds((2, 8, n), F32), sds((2, 4...  7.64 us
    pallas_call x1, Pallas kernels, local_fn(): pl.pallas_call(spread_kernel, out_shape=acc_shape, in_specs=[vmem] * (5 +...  5.49 us
    unnamed x19, local copies, waits for them, and re-layouts  4.51 us

profile of v4, /device:TPU:0, one launch (start us, length us, event | category | flops | bytes accessed | tf_op | source)
XLA Modules:
  0.0 41.4 jit_solution(8946239502162184941)
XLA Ops:
  0.0 0.0 copy-start.3
  0.0 0.9 %copy-done.3 = f32[2,8,2048]{2,1,0:T(8,128)S(1)} copy-done((f32[2,8,2048]{2,1,0:T(8,128)S(1)}, f32[2,8,2048]{2,1,0:T(8,128)}, u32[]{:S(2)}) %copy-start.3) | copy-done | bytes 131096
  0.9 0.0 copy-start.4
  0.9 0.8 %copy-done.4 = f32[4,2048]{1,0:T(4,128)S(1)} copy-done((f32[4,2048]{1,0:T(4,128)S(1)}, f32[4,2048]{1,0:T(4,128)}, u32[]{:S(2)}) %copy-start.4) | copy-done | bytes 32792
  1.7 0.0 copy-start.5
  1.7 0.8 %copy-done.5 = f32[4,2048]{1,0:T(4,128)S(1)} copy-done((f32[4,2048]{1,0:T(4,128)S(1)}, f32[4,2048]{1,0:T(4,128)}, u32[]{:S(2)}) %copy-start.5) | copy-done | bytes 32792
  2.4 0.0 copy-start.6
  2.4 0.7 %copy-done.6 = s32[2048]{0:T(1024)S(1)} copy-done((s32[2048]{0:T(1024)S(1)}, s32[2048]{0:T(1024)}, u32[]{:S(2)}) %copy-start.6) | copy-done | bytes 8216
  3.1 0.0 copy-start.7
  3.1 0.7 %copy-done.7 = s32[2048]{0:T(1024)S(1)} copy-done((s32[2048]{0:T(1024)S(1)}, s32[2048]{0:T(1024)}, u32[]{:S(2)}) %copy-start.7) | copy-done | bytes 8216
  3.8 7.6 %exchange.1 = (f32[2,8,2048]{2,1,0:T(8,128)S(1)}, f32[2,4,2048]{2,1,0:T(4,128)S(1)}, f32[2,4,2048]{2,1,0:T(4,128)S(1)}, s32[2,16,128]{2,1,0:T(8,128)S(1)}, s32[2...) custom-call(f32[2,8,2048]{2,1,0:T(8,128)S(1)} %copy-done.3, ...), custom_call_target="tpu_custom_call" | custom-call | tf_op jit(solution)/shard_map/exchange/pallas_call | solution.py:394
  11.5 0.0 copy-start.8
  11.5 0.0 copy-start
  11.5 0.0 copy-start.1
  11.5 0.0 copy-start.2
  11.5 5.5 %spread.1 = (f32[5880,128]{1,0:T(8,128)S(1)}, f32[5880,128]{1,0:T(8,128)S(1)}, f32[5880,128]{1,0:T(8,128)S(1)}, f32[5880,128]{1,0:T(8,128)S(1)}, f32[5880,128]{1,0:T(8,128)S(1)}, /*index=5*/f32[5880,128]{1,0:T(8,128)S(1)}) custom-call(s32[2,16,128]{2,1,0:T(8,128)S(1)} %get-tuple-element.22., ...), custom_call_target="tpu_custom_call", output_to_operand_aliasing={{0}: (5, {}), {1}: (6, {}), {2}: (7, {}), {3}: (8, {}), {4}... | custom-call | tf_op jit(solution)/shard_map/spread/pallas_call | solution.py:407
  17.0 0.0 copy-done.8
  17.0 0.0 copy-done
  17.0 0.0 copy-done.1
  17.1 0.0 copy-done.2
  17.1 23.6 %transform.1 = f32[2,184,92]{2,1,0:T(8,128)S(1)} custom-call(f32[5880,128]{1,0:T(8,128)S(1)} %get-tuple-element.33.refs_0_, f32[5880,128]{1,0:T(8,128)S(1)} %get-tuple-element.34.refs_1_, f32[5880,128]{1,0:T(8,128)S(1)} %get-tuple-element.35.refs_2_, f32[5880,128]{1,0:T(8,128)S(1)} %get-tuple-element.36.refs_3_, f32[5880,128]{1,0:T(8,128)S(1)} %get-tuple-element.37.refs_4_, ...), custom_call_target="tpu_custom_call" | custom-call | tf_op jit(solution)/shard_map/transform/pallas_call | solution.py:418
  40.7 0.7 %copy.23 = f32[2,184,92]{2,1,0:T(8,128)} copy(f32[2,184,92]{2,1,0:T(8,128)S(1)} %transform.1) | data formatting | bytes 270848
  (1 shorter events, 0.0 us)
Async XLA Ops:
  0.0 0.9 %copy-start.3 = (f32[2,8,2048]{2,1,0:T(8,128)S(1)}, f32[2,8,2048]{2,1,0:T(8,128)}, u32[]{:S(2)}) copy-start(f32[2,8,2048]{2,1,0:T(8,128)} %y_hbm.1) | copy-start | bytes 393220
  0.9 0.8 %copy-start.4 = (f32[4,2048]{1,0:T(4,128)S(1)}, f32[4,2048]{1,0:T(4,128)}, u32[]{:S(2)}) copy-start(f32[4,2048]{1,0:T(4,128)} %wy_hbm.1) | copy-start | bytes 98308
  1.7 0.8 %copy-start.5 = (f32[4,2048]{1,0:T(4,128)S(1)}, f32[4,2048]{1,0:T(4,128)}, u32[]{:S(2)}) copy-start(f32[4,2048]{1,0:T(4,128)} %wx_hbm.1) | copy-start | bytes 98308
  2.4 0.7 %copy-start.6 = (s32[2048]{0:T(1024)S(1)}, s32[2048]{0:T(1024)}, u32[]{:S(2)}) copy-start(s32[2048]{0:T(1024)} %param.12) | copy-start | bytes 24580
  3.1 0.7 %copy-start.7 = (s32[2048]{0:T(1024)S(1)}, s32[2048]{0:T(1024)}, u32[]{:S(2)}) copy-start(s32[2048]{0:T(1024)} %param.13) | copy-start | bytes 24580
  11.5 5.5 %copy-start.8 = (f32[368]{0:T(512)S(1)}, f32[368]{0:T(512)}, u32[]{:S(2)}) copy-start(f32[368]{0:T(512)} %param.15) | copy-start | bytes 4420
  11.5 5.6 %copy-start = (bf16[768,768]{1,0:T(8,128)(2,1)S(1)}, bf16[768,768]{1,0:T(8,128)(2,1)}, u32[]{:S(2)}) copy-start(bf16[768,768]{1,0:T(8,128)(2,1)} %constant.6.refs_6_) | copy-start | bytes 3538948
  11.5 5.6 %copy-start.1 = (bf16[768,768]{1,0:T(8,128)(2,1)S(1)}, bf16[768,768]{1,0:T(8,128)(2,1)}, u32[]{:S(2)}) copy-start(bf16[768,768]{1,0:T(8,128)(2,1)} %constant.7.refs_7_) | copy-start | bytes 3538948
  11.5 5.5 %copy-start.2 = (f32[2,4,368,92]{2,1,3,0:T(4,128)S(1)}, f32[2,4,368,92]{2,1,3,0:T(4,128)}, u32[]{:S(2)}) copy-start(f32[2,4,368,92]{2,1,3,0:T(4,128)} %param.14) | copy-start | bytes 3250180

commit v5 on v4

--- a/solution.py
+++ b/solution.py
@@ -1,4 +1,3 @@
-import functools
 import math
 
 import jax
@@ -26,8 +25,13 @@
 KV = 2 * VR
 LANES, ROWS = 128, 16
 EDGE = 6
+WIDE, P_TWO, GN_ROWS, MIB = 2 * LANES, 2 * P_ALL, 48, 2**20
 N_CHUNK = 6
 N_COPY = 3
+N_ACC = 2 * N_COPY
+SUBS = [(0, 48), (48, 32), (80, 16)]
+POSTS = [[(j, s) for s in range(3)] for j in range(2)] + [[(j, 0)] for j in range(2, N_CHUNK)]
+POSTS[-1] += [(j, s) for s in (1, 2) for j in range(2, N_CHUNK)]
 CHUNK_TILES = [(1 + 2 * j, 2 + 2 * j) for j in range(5)] + [(0, 11)]
 
 
@@ -40,8 +44,8 @@
     for dest in range(4):
         for cs in range(2):
             for half in range(2):
-                    part = parts[cs][half * COL_BLK:(half + 1) * COL_BLK, dest * Q_BLK:(dest + 1) * Q_BLK]
-                    e1[dest, cs, :Q_BLK, half, EDGE:EDGE + COL_BLK] = part.T
+                part = parts[cs][half * COL_BLK:(half + 1) * COL_BLK, dest * Q_BLK:(dest + 1) * Q_BLK]
+                e1[dest, cs, :Q_BLK, half, EDGE:EDGE + COL_BLK] = part.T
     e2 = np.zeros((N_CHUNK, 4, 2, TILE_U, 2, P_ALL))
     for j in range(N_CHUNK):
         for src in range(4):
@@ -52,12 +56,22 @@
                 for cs in range(2):
                     e2[j, src, tl, :rows, cs, :N_IMG] = parts[cs][u0:u0 + rows]
     return (jnp.asarray(e1.reshape(8 * Q_PAD, KV).astype(np.float32)).astype(BF16),
-            jnp.asarray(e2.reshape(N_CHUNK * LANES, 2 * P_ALL).astype(np.float32)).astype(BF16))
-
-
-def exchange_kernel(y_hbm, wy_hbm, wx_hbm, iy_hbm, ix_hbm, y_ref, wy_ref, wx_ref, addr_ref, roff_ref, *refs):
-    accs = refs[:2 * N_COPY]
-    y_in, iy, ix, y_send, in_sem, send_sem, recv_sem = refs[2 * N_COPY:]
+            jnp.asarray(e2.reshape(N_CHUNK * LANES, P_TWO).astype(np.float32)).astype(BF16))
+
+
+def zero_kernel(*refs):
+    *accs, token = refs
+
+    def zero(i, _):
+        for a in accs:
+            a[pl.ds(pl.multiple_of(i * VS, 8), VS), :] = jnp.zeros((VS, LANES), F32)
+        return 0
+    lax.fori_loop(0, N_SRC, zero, 0)
+    token[...] = jnp.zeros_like(token)
+
+
+def exchange_kernel(_, y_hbm, wy_hbm, wx_hbm, iy_hbm, ix_hbm, y_ref, wy_ref, wx_ref, addr_ref, roff_ref, *refs):
+    y_in, iy, ix, y_send, in_sem, send_sem, recv_sem = refs
     k = lax.axis_index('cols')
     r = lax.axis_index('rows')
     other = {'cols': 1 - k}
@@ -94,11 +108,6 @@
     copies = [send(0, wy_ref.at[0], wy_ref.at[1]), send(1, wx_ref.at[0], wx_ref.at[1]), send(2, addr_ref.at[0], addr_ref.at[1]),
               send(3, roff_ref.at[0], roff_ref.at[1]), send(4, y_send, y_ref.at[1])]
 
-    def zero(i, _):
-        for a in accs:
-            a[pl.ds(pl.multiple_of(i * VS, 8), VS), :] = jnp.zeros((VS, LANES), F32)
-        return 0
-    lax.fori_loop(0, N_SRC, zero, 0)
     for c in copies:
         c.wait()
 
@@ -111,30 +120,30 @@
 
 
 def spread_kernel(addr_ref, y_ref, wy_ref, wx_ref, roff_ref, *refs):
-    accs = refs[2 * N_COPY:4 * N_COPY]
+    accs = refs[N_ACC:4 * N_COPY]
     addr, sem = refs[4 * N_COPY], refs[-1]
     q_refs = refs[4 * N_COPY + 1:-1]
     to_smem = pltpu.make_async_copy(addr_ref, addr, sem)
     to_smem.start()
     n = y_ref.shape[2]
 
-    r0 = lax.broadcasted_iota(jnp.int32, (80, 256), 0)
-    l0 = lax.broadcasted_iota(jnp.int32, (80, 256), 1)
+    r0 = lax.broadcasted_iota(jnp.int32, (80, WIDE), 0)
+    l0 = lax.broadcasted_iota(jnp.int32, (80, WIDE), 1)
     ry = (r0 < 24) & (l0 < LANES) & ((r0 & 7) == (l0 >> 4))
     rw = (r0 >= 24) & (r0 < 72) & (l0 >= LANES) & (((r0 - 24) & 15) == (l0 & 15))
     expand = jnp.where(ry | rw, 1.0, 0.0).astype(BF16)
-    rr = lax.broadcasted_iota(jnp.int32, (ROWS, 256), 0)
-    n_blk = n // 256
+    rr = lax.broadcasted_iota(jnp.int32, (ROWS, WIDE), 0)
+    n_blk = n // WIDE
 
     def prep(i, slot, q_ref):
         ds = [pl.ds(pl.multiple_of((i + n_blk * h) * LANES, LANES), LANES) for h in range(2)]
         y = jnp.concatenate([y_ref[slot, :, s] for s in ds], axis=1)
         wy = jnp.concatenate([wy_ref[slot, :, s] for s in ds], axis=1)
         d = (rr - jnp.concatenate([roff_ref[slot, pl.ds(i + n_blk * h, 1), :] for h in range(2)], axis=1)) & 15
-        w16 = jnp.zeros((ROWS, 256), F32)
+        w16 = jnp.zeros((ROWS, WIDE), F32)
         for a in range(4):
             w16 = jnp.where(d == a, wy[a:a + 1], w16)
-        lhs = jnp.concatenate(split3(y) + split3(w16) + [jnp.zeros((8, 256), F32)], axis=0).astype(BF16)
+        lhs = jnp.concatenate(split3(y) + split3(w16) + [jnp.zeros((8, WIDE), F32)], axis=0).astype(BF16)
         o = lax.dot_general(lhs, expand, (((0,), (0,)), ((), ())), preferred_element_type=F32)
         q_ref[...] = o[:, :LANES] * o[:, LANES:]
 
@@ -169,9 +178,9 @@
 
 
 def transform_kernel(*refs):
-    own, nbr = refs[:N_COPY], refs[N_COPY:2 * N_COPY]
-    (e1_hbm, e2_hbm, s_hbm, d_hbm, out_ref, e1_ref, e2_ref, s_ref, d_ref, dd, gch, raw0, f0, f11, gps, gns, msg, recv, gpr, gnr, e2f, st, img, psend, precv,
-     msend_sem, mrecv_sem, gsend_sem, grecv_sem, psend_sem, precv_sem, in_sem) = refs[2 * N_COPY:]
+    own, nbr = refs[:N_COPY], refs[N_COPY:N_ACC]
+    (e1_hbm, e2_hbm, s_hbm, d_hbm, out_ref, e1_ref, e2_ref, s_ref, d_ref, dd, gch, raw0, f0, f11, gps, gns, msg, recv, gpr, gnr, e2f, st, img, mine, psend, precv,
+     msend_sem, mrecv_sem, gsend_sem, grecv_sem, psend_sem, precv_sem, in_sem) = refs[N_ACC:]
     k = lax.axis_index('cols')
     r = lax.axis_index('rows')
     chip, core = r // 2, r % 2
@@ -239,30 +248,32 @@
         for ref, v in zip((raw0, f0, f11), vals):
             ref[pl.ds(off, ROWS), :] = v
 
-    lane = lax.broadcasted_iota(jnp.int32, (Q_PAD, 256), 1) & 127
+    lane = lax.broadcasted_iota(jnp.int32, (Q_PAD, WIDE), 1) & 127
+
+    def swap(sub):
+        rows = pl.ds(*SUBS[sub])
+        return pltpu.make_async_remote_copy(src_ref=psend.at[rows], dst_ref=precv.at[rows], send_sem=psend_sem.at[sub],
+                                            recv_sem=precv_sem.at[sub], device_id={'cols': 1 - k}, device_id_type=MESH)
 
     def first_dft(j, g):
         ab = jnp.dot(e1_ref[...], g, preferred_element_type=F32)
         for d in range(4):
-            a = ab[192 * d:192 * d + 96]
-            b = ab[192 * d + 96:192 * d + 192]
+            a = ab[192 * d:192 * d + Q_PAD]
+            b = ab[192 * d + Q_PAD:192 * d + 192]
             b = jnp.concatenate([pltpu.roll(b[:, :128], 64, 1), pltpu.roll(b[:, 128:], 64, 1)], axis=1)
             msg[j, d] = jnp.where(lane < 64, a - b, a + b).astype(BF16)
 
-    def message(j, i):
+    def copy_of(j, sub, i, slot):
         d = dests[i]
-        return pltpu.make_async_remote_copy(src_ref=msg.at[j, d], dst_ref=recv.at[j, r], send_sem=msend_sem.at[j, i],
-                                            recv_sem=mrecv_sem.at[j, r], device_id={'rows': d}, device_id_type=MESH)
-
-    def arrival(j, i):
-        d = dests[i]
-        return pltpu.make_async_remote_copy(src_ref=msg.at[j, d], dst_ref=recv.at[j, d], send_sem=msend_sem.at[j, i],
-                                            recv_sem=mrecv_sem.at[j, d], device_id={'rows': d}, device_id_type=MESH)
-
-    def post(j):
-        for i in range(3):
-            message(j, i).start()
-        recv[j, r] = msg[j, r]
+        rows = pl.ds(*SUBS[sub])
+        return pltpu.make_async_remote_copy(src_ref=msg.at[j, d, rows], dst_ref=recv.at[j, slot, rows], send_sem=msend_sem.at[j, sub, i],
+                                            recv_sem=mrecv_sem.at[j, sub, slot], device_id={'rows': d}, device_id_type=MESH)
+
+    def post(chunk):
+        for j, sub in POSTS[chunk]:
+            for i in range(3):
+                copy_of(j, sub, i, r).start()
+        recv[chunk, r] = msg[chunk, r]
 
     merge_all(CHUNK_TILES[0], put_chunk)
     loads[0].wait()
@@ -271,19 +282,19 @@
     post(0)
 
     merge_all((None, 0, N_TGT - 1), put_edges)
-    la = lax.broadcasted_iota(jnp.int32, (96, LANES), 1) & 15
-    lb = lax.broadcasted_iota(jnp.int32, (48, LANES), 1) & 15
+    la = lax.broadcasted_iota(jnp.int32, (Q_PAD, LANES), 1) & 15
+    lb = lax.broadcasted_iota(jnp.int32, (GN_ROWS, LANES), 1) & 15
 
     def shifted(v, by):
         return pltpu.roll(v, by % LANES, 1) if by else v
 
-    gp = jnp.zeros((96, LANES), F32)
+    gp = jnp.zeros((Q_PAD, LANES), F32)
     for c in range(8):
-        gp = jnp.where((la >> 1) == c, shifted(raw0[96 * c:96 * c + 96, :], 2 * c - 14), gp)
+        gp = jnp.where((la >> 1) == c, shifted(raw0[Q_PAD * c:Q_PAD * c + Q_PAD, :], 2 * c - 14), gp)
     gps[...] = gp
-    gn = jnp.zeros((48, LANES), F32)
+    gn = jnp.zeros((GN_ROWS, LANES), F32)
     for c in range(16):
-        gn = jnp.where(lb == c, shifted(f11[48 * c:48 * c + 48, :], c - 8), gn)
+        gn = jnp.where(lb == c, shifted(f11[GN_ROWS * c:GN_ROWS * c + GN_ROWS, :], c - 8), gn)
     gns[...] = gn
     to_prv = pltpu.make_async_remote_copy(src_ref=gps, dst_ref=gpr, send_sem=gsend_sem.at[0], recv_sem=grecv_sem.at[0],
                                           device_id={'rows': prv}, device_id_type=MESH)
@@ -301,10 +312,10 @@
     to_nxt.wait()
     gp, gn = gpr[...], gnr[...]
     for c in range(8):
-        s = slice(96 * c, 96 * c + 96)
-        gch[s, LANES:2 * LANES] = (f11[s, :] + jnp.where((la >> 1) == 3, shifted(gp, 6 - 2 * c), 0.0)).astype(BF16)
+        s = slice(Q_PAD * c, Q_PAD * c + Q_PAD)
+        gch[s, LANES:WIDE] = (f11[s, :] + jnp.where((la >> 1) == 3, shifted(gp, 6 - 2 * c), 0.0)).astype(BF16)
     for c in range(16):
-        s = slice(48 * c, 48 * c + 48)
+        s = slice(GN_ROWS * c, GN_ROWS * c + GN_ROWS)
         gch[s, 0:LANES] = (f0[s, :] + jnp.where(lb == 0, shifted(gn, -c), 0.0)).astype(BF16)
     first_dft(N_CHUNK - 1, gch[...])
     post(N_CHUNK - 1)
@@ -315,8 +326,8 @@
         for h in range(2):
             v = e2_ref[LANES * j + 64 * h:LANES * j + 64 * h + 64, :]
             e2f[j, LANES * h:LANES * h + 64, :] = v
-            e2f[j, LANES * h + 64:LANES * h + LANES, 0:P_ALL] = -v[:, P_ALL:2 * P_ALL]
-            e2f[j, LANES * h + 64:LANES * h + LANES, P_ALL:2 * P_ALL] = v[:, 0:P_ALL]
+            e2f[j, LANES * h + 64:LANES * h + LANES, 0:P_ALL] = -v[:, P_ALL:P_TWO]
+            e2f[j, LANES * h + 64:LANES * h + LANES, P_ALL:P_TWO] = v[:, 0:P_ALL]
     st[...] = jnp.zeros_like(st)
     for s in range(2):
         for c in range(4):
@@ -329,54 +340,58 @@
     part_q = jnp.concatenate([part_q, jnp.zeros((1, LANES - Q_BLK), F32)], axis=1)
     dd[...] = jnp.broadcast_to(part_q, (8, LANES)).T[0:Q_BLK, 0:1] * half_p
 
-    coil = (lax.broadcasted_iota(jnp.int32, (Q_PAD, LANES), 1) >> 4) & 3
-
-    def regroup(j, pair):
-        v = [recv[j, 2 * pair + s // 2, :, LANES * (s % 2):LANES * (s % 2 + 1)] for s in range(4)]
-        for bit in (1, 2):
-            m = (coil & bit) == 0
-            for s in range(4):
-                if s & bit:
-                    continue
-                x, y = v[s], v[s | bit]
-                v[s] = jnp.where(m, x, pltpu.roll(y, ROWS * bit, 1))
-                v[s | bit] = jnp.where(m, pltpu.roll(x, LANES - ROWS * bit, 1), y)
-        return v
-
-    def second_dft(j):
-        for i in range(3):
-            arrival(j, i).wait_recv()
-        first, second = regroup(j, 0), regroup(j, 1)
-        lhs = jnp.concatenate([jnp.concatenate([first[c], second[c]], axis=1) for c in range(4)], axis=0)
-        return jnp.dot(lhs, e2f[j], preferred_element_type=F32)
-
-    img[...] = second_dft(0)
-
-    def accumulate(j, _):
-        img[...] += second_dft(j)
-        return 0
-    lax.fori_loop(1, N_CHUNK, accumulate, 0)
-
-    x_re = jnp.zeros((Q_PAD, P_ALL), F32)
-    x_im = jnp.zeros((Q_PAD, P_ALL), F32)
-    for c in range(4):
-        i_re = img[96 * c:96 * c + 96, 0:P_ALL]
-        i_im = img[96 * c:96 * c + 96, P_ALL:2 * P_ALL]
-        x_re = x_re + st[0, c] * i_re + st[1, c] * i_im
-        x_im = x_im + st[0, c] * i_im - st[1, c] * i_re
-    lo = jnp.concatenate([x_re[:, 0:P_PAD], x_im[:, 0:P_PAD]], axis=1)
-    hi = jnp.concatenate([x_re[:, P_BLK:P_BLK + P_PAD], x_im[:, P_BLK:P_BLK + P_PAD]], axis=1)
-    first = k == 0
-    psend[...] = jnp.where(first, hi, lo)
-    swap = pltpu.make_async_remote_copy(src_ref=psend, dst_ref=precv, send_sem=psend_sem, recv_sem=precv_sem,
-                                        device_id={'cols': 1 - k}, device_id_type=MESH)
-    swap.start()
-    mine = jnp.where(first, lo, hi)
+    first_col = k == 0
+    for sub, (row0, rows) in enumerate(SUBS):
+        coil = (lax.broadcasted_iota(jnp.int32, (rows, LANES), 1) >> 4) & 3
+
+        def regroup(j, pair):
+            v = [recv[j, 2 * pair + t // 2, pl.ds(row0, rows), LANES * (t % 2):LANES * (t % 2 + 1)] for t in range(4)]
+            for bit in (1, 2):
+                m = (coil & bit) == 0
+                for t in range(4):
+                    if t & bit:
+                        continue
+                    x, y = v[t], v[t | bit]
+                    v[t] = jnp.where(m, x, pltpu.roll(y, ROWS * bit, 1))
+                    v[t | bit] = jnp.where(m, pltpu.roll(x, LANES - ROWS * bit, 1), y)
+            return v
+
+        def second_dft(j):
+            for i in range(3):
+                copy_of(j, sub, i, dests[i]).wait_recv()
+            both = regroup(j, 0), regroup(j, 1)
+            lhs = jnp.concatenate([jnp.concatenate([both[0][c], both[1][c]], axis=1) for c in range(4)], axis=0)
+            return jnp.dot(lhs, e2f[j], preferred_element_type=F32)
+
+        acc = img.at[pl.ds(4 * row0, 4 * rows)]
+        acc[...] = second_dft(0)
+
+        def accumulate(j, _):
+            acc[...] += second_dft(j)
+            return 0
+        lax.fori_loop(1, N_CHUNK, accumulate, 0)
+
+        x_re = jnp.zeros((rows, P_ALL), F32)
+        x_im = jnp.zeros((rows, P_ALL), F32)
+        for c in range(4):
+            i_re = acc[rows * c:rows * (c + 1), 0:P_ALL]
+            i_im = acc[rows * c:rows * (c + 1), P_ALL:P_TWO]
+            s_re, s_im = st[0, c, row0:row0 + rows], st[1, c, row0:row0 + rows]
+            x_re = x_re + s_re * i_re + s_im * i_im
+            x_im = x_im + s_re * i_im - s_im * i_re
+        lo = jnp.concatenate([x_re[:, 0:P_PAD], x_im[:, 0:P_PAD]], axis=1)
+        hi = jnp.concatenate([x_re[:, P_BLK:P_BLK + P_PAD], x_im[:, P_BLK:P_BLK + P_PAD]], axis=1)
+        psend[row0:row0 + rows] = jnp.where(first_col, hi, lo)
+        swap(sub).start()
+        mine[row0:row0 + rows] = jnp.where(first_col, lo, hi)
+
     for j in range(N_CHUNK):
-        for i in range(3):
-            message(j, i).wait_send()
-    swap.wait()
-    total = mine + precv[...]
+        for sub in range(len(SUBS)):
+            for i in range(3):
+                copy_of(j, sub, i, r).wait_send()
+    for sub in range(len(SUBS)):
+        swap(sub).wait()
+    total = mine[...] + precv[...]
     out_ref[0] = (total[0:Q_BLK, 0:P_BLK] * dd[...]).T
     out_ref[1] = (total[0:Q_BLK, P_PAD:P_PAD + P_BLK] * dd[...]).T
 
@@ -390,58 +405,67 @@
     def local_fn(kspace, wts_y, wts_x, idx_y, idx_x, coil_maps, deapod):
         n = kspace.shape[2]
         e1, e2 = dft_constants()
-        acc_shape = [sds((N_SRC * VS, LANES), F32)] * (2 * N_COPY)
-        *samples, = pl.pallas_call(
+        acc_shape = [sds((N_SRC * VS, LANES), F32)] * (N_ACC)
+        *accs, token = pl.pallas_call(
+            zero_kernel,
+            out_shape=acc_shape + [sds((8, LANES), F32)],
+            out_specs=[vmem] * (N_ACC + 1),
+            compiler_params=pltpu.CompilerParams(vmem_limit_bytes=MIB),
+            cost_estimate=pl.CostEstimate(flops=2 * 10**9, bytes_accessed=2 * 10**7, transcendentals=0),
+            name='zero',
+        )()
+        samples = pl.pallas_call(
             exchange_kernel,
             out_shape=[sds((2, 8, n), F32), sds((2, 4, n), F32), sds((2, 4, n), F32), sds((2, 16, LANES), jnp.int32),
-                       sds((2, 16, LANES), jnp.int32)] + acc_shape,
-            in_specs=[hbm] * 5,
-            out_specs=[vmem] * (5 + 2 * N_COPY),
+                       sds((2, 16, LANES), jnp.int32)],
+            in_specs=[vmem] + [hbm] * 5,
+            out_specs=[vmem] * 5,
             scratch_shapes=[pltpu.VMEM((2, 8, n), F32), pltpu.VMEM((16, LANES), jnp.int32), pltpu.VMEM((16, LANES), jnp.int32),
                             pltpu.VMEM((8, n), F32), pltpu.SemaphoreType.DMA((5,)), pltpu.SemaphoreType.DMA((5,)),
                             pltpu.SemaphoreType.DMA((5,))],
-            compiler_params=pltpu.CompilerParams(collective_id=0, has_side_effects=True, vmem_limit_bytes=8 * 2**20),
+            compiler_params=pltpu.CompilerParams(collective_id=0, has_side_effects=True, vmem_limit_bytes=8 * MIB),
             name='exchange',
-        )(kspace, wts_y, wts_x, idx_y.reshape(16, LANES), idx_x.reshape(16, LANES))
-        y8, wy, wx, addr, roff = samples[:5]
+        )(token, kspace, wts_y, wts_x, idx_y.reshape(16, LANES), idx_x.reshape(16, LANES))
+        y8, wy, wx, addr, roff = samples
         accs = pl.pallas_call(
             spread_kernel,
             out_shape=acc_shape,
-            in_specs=[vmem] * (5 + 2 * N_COPY),
-            out_specs=[vmem] * (2 * N_COPY),
-            scratch_shapes=[pltpu.SMEM((2, 16, LANES), jnp.int32)] + [pltpu.VMEM((256, LANES), F32)] * 4 + [pltpu.SemaphoreType.DMA],
-            input_output_aliases={5 + i: i for i in range(2 * N_COPY)},
-            compiler_params=pltpu.CompilerParams(vmem_limit_bytes=8 * 2**20),
+            in_specs=[vmem] * (5 + N_ACC),
+            out_specs=[vmem] * (N_ACC),
+            scratch_shapes=[pltpu.SMEM((2, 16, LANES), jnp.int32)] + [pltpu.VMEM((WIDE, LANES), F32)] * 4 + [pltpu.SemaphoreType.DMA],
+            input_output_aliases={5 + i: i for i in range(N_ACC)},
+            compiler_params=pltpu.CompilerParams(vmem_limit_bytes=8 * MIB),
             name='spread',
-        )(addr, y8, wy, wx, roff, *samples[5:])
+        )(addr, y8, wy, wx, roff, *accs)
         maps = jnp.transpose(coil_maps, (0, 3, 1, 2))
         return pl.pallas_call(
             transform_kernel,
             out_shape=sds((2, P_BLK, Q_BLK), F32),
-            in_specs=[vmem] * (2 * N_COPY) + [hbm] * 4,
+            in_specs=[vmem] * (N_ACC) + [hbm] * 4,
             out_specs=vmem,
-            scratch_shapes=[pltpu.VMEM((KV, KV), BF16), pltpu.VMEM((KV, 2 * P_ALL), BF16), pltpu.VMEM((2, Q_BLK, 4, N_IMG), F32),
-                            pltpu.VMEM((1, N_IMG), F32), pltpu.VMEM((Q_BLK, P_BLK), F32), pltpu.VMEM((KV, 256), BF16)] + [pltpu.VMEM((KV, LANES), F32)] * 3 + [
-                pltpu.VMEM((96, LANES), F32),
-                pltpu.VMEM((48, LANES), F32),
-                pltpu.VMEM((N_CHUNK, 4, Q_PAD, 256), BF16),
-                pltpu.VMEM((N_CHUNK, 4, Q_PAD, 256), BF16),
-                pltpu.VMEM((96, LANES), F32),
-                pltpu.VMEM((48, LANES), F32),
-                pltpu.VMEM((N_CHUNK, 256, 2 * P_ALL), BF16),
+            scratch_shapes=[pltpu.VMEM((KV, KV), BF16), pltpu.VMEM((KV, P_TWO), BF16), pltpu.VMEM((2, Q_BLK, 4, N_IMG), F32),
+                            pltpu.VMEM((1, N_IMG), F32), pltpu.VMEM((Q_BLK, P_BLK), F32), pltpu.VMEM((KV, WIDE), BF16)] + [pltpu.VMEM((KV, LANES), F32)] * 3 + [
+                pltpu.VMEM((Q_PAD, LANES), F32),
+                pltpu.VMEM((GN_ROWS, LANES), F32),
+                pltpu.VMEM((N_CHUNK, 4, Q_PAD, WIDE), BF16),
+                pltpu.VMEM((N_CHUNK, 4, Q_PAD, WIDE), BF16),
+                pltpu.VMEM((Q_PAD, LANES), F32),
+                pltpu.VMEM((GN_ROWS, LANES), F32),
+                pltpu.VMEM((N_CHUNK, WIDE, P_TWO), BF16),
                 pltpu.VMEM((2, 4, Q_PAD, P_ALL), F32),
-                pltpu.VMEM((4 * Q_PAD, 2 * P_ALL), F32),
+                pltpu.VMEM((4 * Q_PAD, P_TWO), F32),
                 pltpu.VMEM((Q_PAD, P_ALL), F32),
                 pltpu.VMEM((Q_PAD, P_ALL), F32),
-                pltpu.SemaphoreType.DMA((N_CHUNK, 3)),
-                pltpu.SemaphoreType.DMA((N_CHUNK, 4)),
+                pltpu.VMEM((Q_PAD, P_ALL), F32),
+                pltpu.SemaphoreType.DMA((N_CHUNK, len(SUBS), 3)),
+                pltpu.SemaphoreType.DMA((N_CHUNK, len(SUBS), 4)),
                 pltpu.SemaphoreType.DMA((2,)),
                 pltpu.SemaphoreType.DMA((2,)),
-                pltpu.SemaphoreType.DMA,
-                pltpu.SemaphoreType.DMA,
+                pltpu.SemaphoreType.DMA((len(SUBS),)),
+                pltpu.SemaphoreType.DMA((len(SUBS),)),
                 pltpu.SemaphoreType.DMA((4,)),
             ],
-            compiler_params=pltpu.CompilerParams(collective_id=1, has_side_effects=True, vmem_limit_bytes=24 * 2**20),
+            compiler_params=pltpu.CompilerParams(collective_id=1, has_side_effects=True, vmem_limit_bytes=24 * MIB),
             name='transform',
         )(*accs, e1, e2, maps, deapod.reshape(1, N_IMG))
 

time: 41.7 us -> 38.7 us (0.928)
  local copies, waits for them, and re-layouts: 4.52 us -> 0.72 us
  Pallas kernels: 36.7 us -> 37.7 us
    unnamed x19, local copies, waits for them, and re-layouts: 4.51 us -> 0.72 us
    pallas_call x0 -> x1, Pallas kernels: none -> 1.19 us  [local_fn(): pl.pallas_call(zero_kernel, out_shape=acc_shape + [sds((8, LANES), F32)],...]
where the time goes in v5:
time: 38.7 us; the launch traced here: 38.6 us
  Pallas kernels  37.7 us (97%)
  local copies, waits for them, and re-layouts  0.72 us (2%)
    pallas_call x1, Pallas kernels, local_fn(): pl.pallas_call(transform_kernel, out_shape=sds((2, P_BLK, Q_BLK), F32), i...  23.3 us
    pallas_call x1, Pallas kernels, local_fn(): pl.pallas_call(exchange_kernel, out_shape=[sds((2, 8, n), F32), sds((2, 4...  7.7 us
    pallas_call x1, Pallas kernels, local_fn(): pl.pallas_call(spread_kernel, out_shape=acc_shape, in_specs=[vmem] * (5 +...  5.5 us
    pallas_call x1, Pallas kernels, local_fn(): pl.pallas_call(zero_kernel, out_shape=acc_shape + [sds((8, LANES), F32)],...  1.19 us

profile of v5, /device:TPU:0, one launch (start us, length us, event | category | flops | bytes accessed | tf_op | source)
XLA Modules:
  0.0 38.6 jit_solution(1006662078396848050)
XLA Ops:
  0.0 0.0 copy-start.6
  0.0 0.0 copy-start.7
  0.0 0.0 copy-start.4
  0.0 0.0 copy-start.5
  0.0 0.0 copy-start.3
  0.0 1.2 %zero.1 = (f32[5880,128]{1,0:T(8,128)S(1)}, f32[5880,128]{1,0:T(8,128)S(1)}, f32[5880,128]{1,0:T(8,128)S(1)}, f32[5880,128]{1,0:T(8,128)S(1)}, f32[5880,128]{1,0...) custom-call(), custom_call_target="tpu_custom_call" | custom-call | flops 2000000000 | bytes 20000000 | tf_op jit(solution)/shard_map/zero/pallas_call | solution.py:409
  1.2 0.0 copy-done.6
  1.2 0.0 copy-done.7
  1.2 0.0 copy-done.4
  1.2 0.0 copy-done.5
  1.2 0.0 copy-done.3
  1.3 7.7 %exchange.1 = (f32[2,8,2048]{2,1,0:T(8,128)S(1)}, f32[2,4,2048]{2,1,0:T(4,128)S(1)}, f32[2,4,2048]{2,1,0:T(4,128)S(1)}, s32[2,16,128]{2,1,0:T(8,128)S(1)}, s32[2,16,128]{2,1,0:T(8,128)S(1)}) custom-call(f32[8,128]{1,0:T(8,128)S(1)} %get-tuple-element.23._, f32[2,8,2048]{2,1,0:T(8,128)S(1)} %copy-done.3, f32[4,2048]{1,0:T(4,128)S(1)} %copy-done.4, ...), custom_call_target="tpu_custom_call" | custom-call | tf_op jit(solution)/shard_map/exchange/pallas_call | solution.py:417
  9.0 0.0 copy-start.8
  9.0 0.0 copy-start
  9.0 0.0 copy-start.1
  9.0 0.0 copy-start.2
  9.0 5.5 %spread.1 = (f32[5880,128]{1,0:T(8,128)S(1)}, f32[5880,128]{1,0:T(8,128)S(1)}, f32[5880,128]{1,0:T(8,128)S(1)}, f32[5880,128]{1,0:T(8,128)S(1)}, f32[5880,128]{1,0:T(8,128)S(1)}, /*index=5*/f32[5880,128]{1,0:T(8,128)S(1)}) custom-call(s32[2,16,128]{2,1,0:T(8,128)S(1)} %get-tuple-element.24., ...), custom_call_target="tpu_custom_call", output_to_operand_aliasing={{0}: (5, {}), {1}: (6, {}), {2}: (7, {}), {3}: (8, {}), {4}... | custom-call | tf_op jit(solution)/shard_map/spread/pallas_call | solution.py:430
  14.5 0.0 copy-done.8
  14.5 0.0 copy-done
  14.6 0.0 copy-done.1
  14.6 0.0 copy-done.2
  14.6 23.3 %transform.1 = f32[2,184,92]{2,1,0:T(8,128)S(1)} custom-call(f32[5880,128]{1,0:T(8,128)S(1)} %get-tuple-element.35.refs_0_, f32[5880,128]{1,0:T(8,128)S(1)} %get-tuple-element.36.refs_1_, f32[5880,128]{1,0:T(8,128)S(1)} %get-tuple-element.37.refs_2_, f32[5880,128]{1,0:T(8,128)S(1)} %get-tuple-element.38.refs_3_, f32[5880,128]{1,0:T(8,128)S(1)} %get-tuple-element.39.refs_4_, ...), custom_call_target="tpu_custom_call" | custom-call | tf_op jit(solution)/shard_map/transform/pallas_call | solution.py:441
  37.9 0.7 %copy.23 = f32[2,184,92]{2,1,0:T(8,128)} copy(f32[2,184,92]{2,1,0:T(8,128)S(1)} %transform.1) | data formatting | bytes 270848
  (1 shorter events, 0.0 us)
Async XLA Ops:
  0.0 1.2 %copy-start.6 = (s32[2048]{0:T(1024)S(1)}, s32[2048]{0:T(1024)}, u32[]{:S(2)}) copy-start(s32[2048]{0:T(1024)} %param.12) | copy-start | bytes 24580
  0.0 1.2 %copy-start.7 = (s32[2048]{0:T(1024)S(1)}, s32[2048]{0:T(1024)}, u32[]{:S(2)}) copy-start(s32[2048]{0:T(1024)} %param.13) | copy-start | bytes 24580
  0.0 1.2 %copy-start.4 = (f32[4,2048]{1,0:T(4,128)S(1)}, f32[4,2048]{1,0:T(4,128)}, u32[]{:S(2)}) copy-start(f32[4,2048]{1,0:T(4,128)} %wy_hbm.1) | copy-start | bytes 98308
  0.0 1.2 %copy-start.5 = (f32[4,2048]{1,0:T(4,128)S(1)}, f32[4,2048]{1,0:T(4,128)}, u32[]{:S(2)}) copy-start(f32[4,2048]{1,0:T(4,128)} %wx_hbm.1) | copy-start | bytes 98308
  0.0 1.2 %copy-start.3 = (f32[2,8,2048]{2,1,0:T(8,128)S(1)}, f32[2,8,2048]{2,1,0:T(8,128)}, u32[]{:S(2)}) copy-start(f32[2,8,2048]{2,1,0:T(8,128)} %y_hbm.1) | copy-start | bytes 393220
  9.0 5.6 %copy-start.8 = (f32[368]{0:T(512)S(1)}, f32[368]{0:T(512)}, u32[]{:S(2)}) copy-start(f32[368]{0:T(512)} %param.15) | copy-start | bytes 4420
  9.0 5.6 %copy-start = (bf16[768,768]{1,0:T(8,128)(2,1)S(1)}, bf16[768,768]{1,0:T(8,128)(2,1)}, u32[]{:S(2)}) copy-start(bf16[768,768]{1,0:T(8,128)(2,1)} %constant.6.refs_6_) | copy-start | bytes 3538948
  9.0 5.6 %copy-start.1 = (bf16[768,768]{1,0:T(8,128)(2,1)S(1)}, bf16[768,768]{1,0:T(8,128)(2,1)}, u32[]{:S(2)}) copy-start(bf16[768,768]{1,0:T(8,128)(2,1)} %constant.7.refs_7_) | copy-start | bytes 3538948
  9.0 5.6 %copy-start.2 = (f32[2,4,368,92]{2,1,3,0:T(4,128)S(1)}, f32[2,4,368,92]{2,1,3,0:T(4,128)}, u32[]{:S(2)}) copy-start(f32[2,4,368,92]{2,1,3,0:T(4,128)} %param.14) | copy-start | bytes 3250180

commit v6 on v5

--- a/solution.py
+++ b/solution.py
@@ -29,9 +29,12 @@
 N_CHUNK = 6
 N_COPY = 3
 N_ACC = 2 * N_COPY
-SUBS = [(0, 48), (48, 32), (80, 16)]
-POSTS = [[(j, s) for s in range(3)] for j in range(2)] + [[(j, 0)] for j in range(2, N_CHUNK)]
-POSTS[-1] += [(j, s) for s in (1, 2) for j in range(2, N_CHUNK)]
+SUBS = [(0, 64), (64, 32), (0, Q_PAD)]
+FULL, N_WHOLE = 2, 2
+WHOLE, SPLIT = range(N_WHOLE), range(N_WHOLE, N_CHUNK)
+POSTS = [[(j, FULL)] for j in WHOLE] + [[(j, 0)] for j in SPLIT]
+POSTS[-1] += [(j, 1) for j in SPLIT]
+SENT = [(j, FULL) for j in WHOLE] + [(j, sub) for j in SPLIT for sub in range(2)]
 CHUNK_TILES = [(1 + 2 * j, 2 + 2 * j) for j in range(5)] + [(0, 11)]
 
 
@@ -70,7 +73,8 @@
     token[...] = jnp.zeros_like(token)
 
 
-def exchange_kernel(_, y_hbm, wy_hbm, wx_hbm, iy_hbm, ix_hbm, y_ref, wy_ref, wx_ref, addr_ref, roff_ref, *refs):
+def exchange_kernel(_, y_hbm, wy_hbm, wx_hbm, iy_hbm, ix_hbm, e2_ref, s_ref, d_ref,
+                    y_ref, wy_ref, wx_ref, addr_ref, roff_ref, e2f, st, dd, *refs):
     y_in, iy, ix, y_send, in_sem, send_sem, recv_sem = refs
     k = lax.axis_index('cols')
     r = lax.axis_index('rows')
@@ -108,6 +112,24 @@
     copies = [send(0, wy_ref.at[0], wy_ref.at[1]), send(1, wx_ref.at[0], wx_ref.at[1]), send(2, addr_ref.at[0], addr_ref.at[1]),
               send(3, roff_ref.at[0], roff_ref.at[1]), send(4, y_send, y_ref.at[1])]
 
+    for j in range(N_CHUNK):
+        for h in range(2):
+            v = e2_ref[LANES * j + 64 * h:LANES * j + 64 * h + 64, :]
+            e2f[j, LANES * h:LANES * h + 64, :] = v
+            e2f[j, LANES * h + 64:LANES * h + LANES, 0:P_ALL] = -v[:, P_ALL:P_TWO]
+            e2f[j, LANES * h + 64:LANES * h + LANES, P_ALL:P_TWO] = v[:, 0:P_ALL]
+    st[...] = jnp.zeros_like(st)
+    for s in range(2):
+        for c in range(4):
+            st[s, c, 0:Q_BLK, 0:N_IMG] = s_ref[s, :, c, :]
+
+    half_p = jnp.where(k == 0, d_ref[:, 0:P_BLK], d_ref[:, P_BLK:2 * P_BLK])
+    part_q = d_ref[:, 0:Q_BLK]
+    for i in range(1, 4):
+        part_q = jnp.where(r == i, d_ref[:, Q_BLK * i:Q_BLK * (i + 1)], part_q)
+    part_q = jnp.concatenate([part_q, jnp.zeros((1, LANES - Q_BLK), F32)], axis=1)
+    dd[...] = jnp.broadcast_to(part_q, (8, LANES)).T[0:Q_BLK, 0:1] * half_p
+
     for c in copies:
         c.wait()
 
@@ -179,8 +201,8 @@
 
 def transform_kernel(*refs):
     own, nbr = refs[:N_COPY], refs[N_COPY:N_ACC]
-    (e1_hbm, e2_hbm, s_hbm, d_hbm, out_ref, e1_ref, e2_ref, s_ref, d_ref, dd, gch, raw0, f0, f11, gps, gns, msg, recv, gpr, gnr, e2f, st, img, mine, psend, precv,
-     msend_sem, mrecv_sem, gsend_sem, grecv_sem, psend_sem, precv_sem, in_sem) = refs[N_ACC:]
+    (e1_ref, e2f, st, dd, out_ref, gch, raw0, f0, f11, gps, gns, msg, recv, gpr, gnr, img, mine, psend, precv,
+     msend_sem, mrecv_sem, gsend_sem, grecv_sem, psend_sem, precv_sem) = refs[N_ACC:]
     k = lax.axis_index('cols')
     r = lax.axis_index('rows')
     chip, core = r // 2, r % 2
@@ -191,10 +213,6 @@
         pl.semaphore_signal(barrier, inc=1, device_id={'rows': d}, device_id_type=MESH)
     pl.semaphore_signal(barrier, inc=1, device_id={'cols': 1 - k}, device_id_type=MESH)
 
-    loads = [pltpu.make_async_copy(a, b, in_sem.at[i]) for i, (a, b) in
-             enumerate(((e1_hbm, e1_ref), (e2_hbm, e2_ref), (s_hbm, s_ref), (d_hbm, d_ref)))]
-    for c in loads:
-        c.start()
     slots = ((own, k), (nbr, 1 - k))
     lane16 = lax.broadcasted_iota(jnp.int32, (ROWS, LANES), 1) & 15
     sub16 = lax.broadcasted_iota(jnp.int32, (ROWS, LANES), 0)
@@ -276,7 +294,6 @@
         recv[chunk, r] = msg[chunk, r]
 
     merge_all(CHUNK_TILES[0], put_chunk)
-    loads[0].wait()
     first_dft(0, gch[...])
     pl.semaphore_wait(barrier, 4)
     post(0)
@@ -320,31 +337,15 @@
     first_dft(N_CHUNK - 1, gch[...])
     post(N_CHUNK - 1)
 
-    for c in loads[1:]:
-        c.wait()
-    for j in range(N_CHUNK):
-        for h in range(2):
-            v = e2_ref[LANES * j + 64 * h:LANES * j + 64 * h + 64, :]
-            e2f[j, LANES * h:LANES * h + 64, :] = v
-            e2f[j, LANES * h + 64:LANES * h + LANES, 0:P_ALL] = -v[:, P_ALL:P_TWO]
-            e2f[j, LANES * h + 64:LANES * h + LANES, P_ALL:P_TWO] = v[:, 0:P_ALL]
-    st[...] = jnp.zeros_like(st)
-    for s in range(2):
-        for c in range(4):
-            st[s, c, 0:Q_BLK, 0:N_IMG] = s_ref[s, :, c, :]
-
-    half_p = jnp.where(k == 0, d_ref[:, 0:P_BLK], d_ref[:, P_BLK:2 * P_BLK])
-    part_q = d_ref[:, 0:Q_BLK]
-    for i in range(1, 4):
-        part_q = jnp.where(r == i, d_ref[:, Q_BLK * i:Q_BLK * (i + 1)], part_q)
-    part_q = jnp.concatenate([part_q, jnp.zeros((1, LANES - Q_BLK), F32)], axis=1)
-    dd[...] = jnp.broadcast_to(part_q, (8, LANES)).T[0:Q_BLK, 0:1] * half_p
-
     first_col = k == 0
-    for sub, (row0, rows) in enumerate(SUBS):
+
+    def second_dft(j, sub):
+        row0, rows = SUBS[sub]
+        for i in range(3):
+            copy_of(j, sub, i, dests[i]).wait_recv()
         coil = (lax.broadcasted_iota(jnp.int32, (rows, LANES), 1) >> 4) & 3
-
-        def regroup(j, pair):
+        halves = []
+        for pair in range(2):
             v = [recv[j, 2 * pair + t // 2, pl.ds(row0, rows), LANES * (t % 2):LANES * (t % 2 + 1)] for t in range(4)]
             for bit in (1, 2):
                 m = (coil & bit) == 0
@@ -354,28 +355,28 @@
                     x, y = v[t], v[t | bit]
                     v[t] = jnp.where(m, x, pltpu.roll(y, ROWS * bit, 1))
                     v[t | bit] = jnp.where(m, pltpu.roll(x, LANES - ROWS * bit, 1), y)
-            return v
-
-        def second_dft(j):
-            for i in range(3):
-                copy_of(j, sub, i, dests[i]).wait_recv()
-            both = regroup(j, 0), regroup(j, 1)
-            lhs = jnp.concatenate([jnp.concatenate([both[0][c], both[1][c]], axis=1) for c in range(4)], axis=0)
-            return jnp.dot(lhs, e2f[j], preferred_element_type=F32)
-
-        acc = img.at[pl.ds(4 * row0, 4 * rows)]
-        acc[...] = second_dft(0)
+            halves.append(v)
+        lhs = jnp.concatenate([jnp.concatenate([halves[0][c], halves[1][c]], axis=1) for c in range(4)], axis=0)
+        return jnp.dot(lhs, e2f[j], preferred_element_type=F32)
+
+    img[...] = second_dft(0, FULL)
+    for j in WHOLE[1:]:
+        img[...] += second_dft(j, FULL)
+    for sub in range(2):
+        row0, rows = SUBS[sub]
 
         def accumulate(j, _):
-            acc[...] += second_dft(j)
+            part = second_dft(j, sub)
+            for c in range(4):
+                img[Q_PAD * c + row0:Q_PAD * c + row0 + rows] += part[rows * c:rows * (c + 1)]
             return 0
-        lax.fori_loop(1, N_CHUNK, accumulate, 0)
+        lax.fori_loop(N_WHOLE, N_CHUNK, accumulate, 0)
 
         x_re = jnp.zeros((rows, P_ALL), F32)
         x_im = jnp.zeros((rows, P_ALL), F32)
         for c in range(4):
-            i_re = acc[rows * c:rows * (c + 1), 0:P_ALL]
-            i_im = acc[rows * c:rows * (c + 1), P_ALL:P_TWO]
+            i_re = img[Q_PAD * c + row0:Q_PAD * c + row0 + rows, 0:P_ALL]
+            i_im = img[Q_PAD * c + row0:Q_PAD * c + row0 + rows, P_ALL:P_TWO]
             s_re, s_im = st[0, c, row0:row0 + rows], st[1, c, row0:row0 + rows]
             x_re = x_re + s_re * i_re + s_im * i_im
             x_im = x_im + s_re * i_im - s_im * i_re
@@ -385,11 +386,10 @@
         swap(sub).start()
         mine[row0:row0 + rows] = jnp.where(first_col, lo, hi)
 
-    for j in range(N_CHUNK):
-        for sub in range(len(SUBS)):
-            for i in range(3):
-                copy_of(j, sub, i, r).wait_send()
-    for sub in range(len(SUBS)):
+    for j, sub in SENT:
+        for i in range(3):
+            copy_of(j, sub, i, r).wait_send()
+    for sub in range(2):
         swap(sub).wait()
     total = mine[...] + precv[...]
     out_ref[0] = (total[0:Q_BLK, 0:P_BLK] * dd[...]).T
@@ -405,6 +405,7 @@
     def local_fn(kspace, wts_y, wts_x, idx_y, idx_x, coil_maps, deapod):
         n = kspace.shape[2]
         e1, e2 = dft_constants()
+        maps = jnp.transpose(coil_maps, (0, 3, 1, 2))
         acc_shape = [sds((N_SRC * VS, LANES), F32)] * (N_ACC)
         *accs, token = pl.pallas_call(
             zero_kernel,
@@ -417,16 +418,16 @@
         samples = pl.pallas_call(
             exchange_kernel,
             out_shape=[sds((2, 8, n), F32), sds((2, 4, n), F32), sds((2, 4, n), F32), sds((2, 16, LANES), jnp.int32),
-                       sds((2, 16, LANES), jnp.int32)],
-            in_specs=[vmem] + [hbm] * 5,
-            out_specs=[vmem] * 5,
+                       sds((2, 16, LANES), jnp.int32), sds((N_CHUNK, WIDE, P_TWO), BF16), sds((2, 4, Q_PAD, P_ALL), F32), sds((Q_BLK, P_BLK), F32)],
+            in_specs=[vmem] + [hbm] * 5 + [vmem] * 3,
+            out_specs=[vmem] * 8,
             scratch_shapes=[pltpu.VMEM((2, 8, n), F32), pltpu.VMEM((16, LANES), jnp.int32), pltpu.VMEM((16, LANES), jnp.int32),
                             pltpu.VMEM((8, n), F32), pltpu.SemaphoreType.DMA((5,)), pltpu.SemaphoreType.DMA((5,)),
                             pltpu.SemaphoreType.DMA((5,))],
             compiler_params=pltpu.CompilerParams(collective_id=0, has_side_effects=True, vmem_limit_bytes=8 * MIB),
             name='exchange',
-        )(token, kspace, wts_y, wts_x, idx_y.reshape(16, LANES), idx_x.reshape(16, LANES))
-        y8, wy, wx, addr, roff = samples
+        )(token, kspace, wts_y, wts_x, idx_y.reshape(16, LANES), idx_x.reshape(16, LANES), e2, maps, deapod.reshape(1, N_IMG))
+        y8, wy, wx, addr, roff, e2f, st, dd = samples
         accs = pl.pallas_call(
             spread_kernel,
             out_shape=acc_shape,
@@ -435,24 +436,21 @@
             scratch_shapes=[pltpu.SMEM((2, 16, LANES), jnp.int32)] + [pltpu.VMEM((WIDE, LANES), F32)] * 4 + [pltpu.SemaphoreType.DMA],
             input_output_aliases={5 + i: i for i in range(N_ACC)},
             compiler_params=pltpu.CompilerParams(vmem_limit_bytes=8 * MIB),
+            cost_estimate=pl.CostEstimate(flops=2 * 10**9, bytes_accessed=2 * 10**7, transcendentals=0),
             name='spread',
         )(addr, y8, wy, wx, roff, *accs)
-        maps = jnp.transpose(coil_maps, (0, 3, 1, 2))
         return pl.pallas_call(
             transform_kernel,
             out_shape=sds((2, P_BLK, Q_BLK), F32),
-            in_specs=[vmem] * (N_ACC) + [hbm] * 4,
+            in_specs=[vmem] * (N_ACC + 4),
             out_specs=vmem,
-            scratch_shapes=[pltpu.VMEM((KV, KV), BF16), pltpu.VMEM((KV, P_TWO), BF16), pltpu.VMEM((2, Q_BLK, 4, N_IMG), F32),
-                            pltpu.VMEM((1, N_IMG), F32), pltpu.VMEM((Q_BLK, P_BLK), F32), pltpu.VMEM((KV, WIDE), BF16)] + [pltpu.VMEM((KV, LANES), F32)] * 3 + [
+            scratch_shapes=[pltpu.VMEM((KV, WIDE), BF16)] + [pltpu.VMEM((KV, LANES), F32)] * 3 + [
                 pltpu.VMEM((Q_PAD, LANES), F32),
                 pltpu.VMEM((GN_ROWS, LANES), F32),
                 pltpu.VMEM((N_CHUNK, 4, Q_PAD, WIDE), BF16),
                 pltpu.VMEM((N_CHUNK, 4, Q_PAD, WIDE), BF16),
                 pltpu.VMEM((Q_PAD, LANES), F32),
                 pltpu.VMEM((GN_ROWS, LANES), F32),
-                pltpu.VMEM((N_CHUNK, WIDE, P_TWO), BF16),
-                pltpu.VMEM((2, 4, Q_PAD, P_ALL), F32),
                 pltpu.VMEM((4 * Q_PAD, P_TWO), F32),
                 pltpu.VMEM((Q_PAD, P_ALL), F32),
                 pltpu.VMEM((Q_PAD, P_ALL), F32),
@@ -463,11 +461,10 @@
                 pltpu.SemaphoreType.DMA((2,)),
                 pltpu.SemaphoreType.DMA((len(SUBS),)),
                 pltpu.SemaphoreType.DMA((len(SUBS),)),
-                pltpu.SemaphoreType.DMA((4,)),
             ],
             compiler_params=pltpu.CompilerParams(collective_id=1, has_side_effects=True, vmem_limit_bytes=24 * MIB),
             name='transform',
-        )(*accs, e1, e2, maps, deapod.reshape(1, N_IMG))
+        )(*accs, e1, e2f, st, dd)
 
     return jax.shard_map(
         local_fn,

time: 38.7 us -> 38.5 us (level)
  Pallas kernels: 37.7 us -> 36.5 us
  local copies, waits for them, and re-layouts: 0.72 us -> 1.76 us
    pallas_call x1, Pallas kernels: 23.3 us -> 22.1 us  [local_fn(): pl.pallas_call(transform_kernel, out_shape=sds((2, P_BLK, Q_BLK), F32), i...]
    reshape x1, local copies, waits for them, and re-layouts: 0.01 us -> 0.68 us  [local_fn(): deapod.reshape(1, N_IMG)]
    unnamed x19 -> x17, local copies, waits for them, and re-layouts: 0.72 us -> 1.07 us
where the time goes in v6:
time: 38.5 us; the launch traced here: 38.4 us
  Pallas kernels  36.5 us (95%)
  local copies, waits for them, and re-layouts  1.76 us (5%)
    pallas_call x1, Pallas kernels, local_fn(): pl.pallas_call(transform_kernel, out_shape=sds((2, P_BLK, Q_BLK), F32), i...  22.1 us
    pallas_call x1, Pallas kernels, local_fn(): pl.pallas_call(exchange_kernel, out_shape=[sds((2, 8, n), F32), sds((2, 4...  7.69 us
    pallas_call x1, Pallas kernels, local_fn(): pl.pallas_call(spread_kernel, out_shape=acc_shape, in_specs=[vmem] * (5 +...  5.49 us
    pallas_call x1, Pallas kernels, local_fn(): pl.pallas_call(zero_kernel, out_shape=acc_shape + [sds((8, LANES), F32)],...  1.19 us
    unnamed x17, local copies, waits for them, and re-layouts  1.07 us

profile of v6, /device:TPU:0, one launch (start us, length us, event | category | flops | bytes accessed | tf_op | source)
XLA Modules:
  0.0 38.4 jit_solution(3252041572583741517)
XLA Ops:
  0.0 0.7 %reshape.11.d_ref = f32[1,368]{1,0:T(1,128)S(1)} reshape(f32[368]{0:T(512)} %param.15) | data formatting | bytes 2944 | tf_op jit(solution)/shard_map/reshape | solution.py:429
  0.7 0.0 copy-start.1
  0.7 0.0 copy-start.2
  0.7 0.0 copy-start.3
  0.7 0.0 copy-start.4
  0.7 0.0 copy-start.5
  0.7 0.0 copy-start.6
  0.7 0.0 copy-start.7
  0.7 1.2 %zero.1 = (f32[5880,128]{1,0:T(8,128)S(1)}, f32[5880,128]{1,0:T(8,128)S(1)}, f32[5880,128]{1,0:T(8,128)S(1)}, f32[5880,128]{1,0:T(8,128)S(1)}, f32[5880,128]{1,0...) custom-call(), custom_call_target="tpu_custom_call" | custom-call | flops 2000000000 | bytes 20000000 | tf_op jit(solution)/shard_map/zero/pallas_call | solution.py:410
  1.9 0.0 copy-done.1
  2.0 0.3 copy-done.2
  2.3 0.0 copy-done.3
  2.3 0.0 copy-done.4
  2.3 0.0 copy-done.5
  2.3 0.0 copy-done.6
  2.3 0.0 copy-done.7
  2.3 7.7 %exchange.1 = (f32[2,8,2048]{2,1,0:T(8,128)S(1)}, f32[2,4,2048]{2,1,0:T(4,128)S(1)}, f32[2,4,2048]{2,1,0:T(4,128)S(1)}, s32[2,16,128]{2,1,0:T(8,128)S(1)}, s32[2...) custom-call(f32[8,128]{1,0:T(8,128)S(1)} %get-tuple-element.26._, ...), custom_call_target="tpu_custom_call" | custom-call | tf_op jit(solution)/shard_map/exchange/pallas_call | solution.py:418
  10.0 0.0 copy-start
  10.0 5.5 %spread.1 = (f32[5880,128]{1,0:T(8,128)S(1)}, f32[5880,128]{1,0:T(8,128)S(1)}, f32[5880,128]{1,0:T(8,128)S(1)}, f32[5880,128]{1,0:T(8,128)S(1)}, f32[5880,128]{1,0:T(8,128)S(1)}, /*index=5*/f32[5880,128]{1,0:T(8,128)S(1)}) custom-call(s32[2,16,128]{2,1,0:T(8,128)S(1)} %get-tuple-element.27., ...), custom_call_target="tpu_custom_call", output_to_operand_aliasing={{0}: (5, {}), {1}: (6, {}), {2}: (7, {}), {3}: (8, {}), {4}... | custom-call | flops 2000000000 | bytes 20000000 | tf_op jit(solution)/shard_map/spread/pallas_call | solution.py:431
  15.5 0.0 copy-done
  15.5 22.1 %transform.1 = f32[2,184,92]{2,1,0:T(8,128)S(1)} custom-call(f32[5880,128]{1,0:T(8,128)S(1)} %get-tuple-element.38.refs_0_, f32[5880,128]{1,0:T(8,128)S(1)} %get-tuple-element.39.refs_1_, f32[5880,128]{1,0:T(8,128)S(1)} %get-tuple-element.40.refs_2_, f32[5880,128]{1,0:T(8,128)S(1)} %get-tuple-element.41.refs_3_, f32[5880,128]{1,0:T(8,128)S(1)} %get-tuple-element.42.refs_4_, ...), custom_call_target="tpu_custom_call" | custom-call | tf_op jit(solution)/shard_map/transform/pallas_call | solution.py:442
  37.7 0.7 %copy.23 = f32[2,184,92]{2,1,0:T(8,128)} copy(f32[2,184,92]{2,1,0:T(8,128)S(1)} %transform.1) | data formatting | bytes 270848
Async XLA Ops:
  0.7 1.3 %copy-start.1 = (bf16[768,768]{1,0:T(8,128)(2,1)S(1)}, bf16[768,768]{1,0:T(8,128)(2,1)}, u32[]{:S(2)}) copy-start(bf16[768,768]{1,0:T(8,128)(2,1)} %constant.6.e2_ref) | copy-start | bytes 3538948
  0.7 1.6 %copy-start.2 = (f32[2,4,368,92]{2,1,3,0:T(4,128)S(1)}, f32[2,4,368,92]{2,1,3,0:T(4,128)}, u32[]{:S(2)}) copy-start(f32[2,4,368,92]{2,1,3,0:T(4,128)} %param.14) | copy-start | bytes 3250180
  0.7 1.6 %copy-start.3 = (f32[2,8,2048]{2,1,0:T(8,128)S(1)}, f32[2,8,2048]{2,1,0:T(8,128)}, u32[]{:S(2)}) copy-start(f32[2,8,2048]{2,1,0:T(8,128)} %y_hbm.1) | copy-start | bytes 393220
  0.7 1.6 %copy-start.4 = (f32[4,2048]{1,0:T(4,128)S(1)}, f32[4,2048]{1,0:T(4,128)}, u32[]{:S(2)}) copy-start(f32[4,2048]{1,0:T(4,128)} %wy_hbm.1) | copy-start | bytes 98308
  0.7 1.6 %copy-start.5 = (f32[4,2048]{1,0:T(4,128)S(1)}, f32[4,2048]{1,0:T(4,128)}, u32[]{:S(2)}) copy-start(f32[4,2048]{1,0:T(4,128)} %wx_hbm.1) | copy-start | bytes 98308
  0.7 1.6 %copy-start.6 = (s32[2048]{0:T(1024)S(1)}, s32[2048]{0:T(1024)}, u32[]{:S(2)}) copy-start(s32[2048]{0:T(1024)} %param.12) | copy-start | bytes 24580
  0.7 1.6 %copy-start.7 = (s32[2048]{0:T(1024)S(1)}, s32[2048]{0:T(1024)}, u32[]{:S(2)}) copy-start(s32[2048]{0:T(1024)} %param.13) | copy-start | bytes 24580
  10.0 5.5 %copy-start = (bf16[768,768]{1,0:T(8,128)(2,1)S(1)}, bf16[768,768]{1,0:T(8,128)(2,1)}, u32[]{:S(2)}) copy-start(bf16[768,768]{1,0:T(8,128)(2,1)} %constant.7.refs_6_) | copy-start | bytes 3538948

commit v7 on v6

--- a/solution.py
+++ b/solution.py
@@ -33,7 +33,7 @@
 FULL, N_WHOLE = 2, 2
 WHOLE, SPLIT = range(N_WHOLE), range(N_WHOLE, N_CHUNK)
 POSTS = [[(j, FULL)] for j in WHOLE] + [[(j, 0)] for j in SPLIT]
-POSTS[-1] += [(j, 1) for j in SPLIT]
+POSTS += [[(j, 1) for j in SPLIT]]
 SENT = [(j, FULL) for j in WHOLE] + [(j, sub) for j in SPLIT for sub in range(2)]
 CHUNK_TILES = [(1 + 2 * j, 2 + 2 * j) for j in range(5)] + [(0, 11)]
 
@@ -73,8 +73,8 @@
     token[...] = jnp.zeros_like(token)
 
 
-def exchange_kernel(_, y_hbm, wy_hbm, wx_hbm, iy_hbm, ix_hbm, e2_ref, s_ref, d_ref,
-                    y_ref, wy_ref, wx_ref, addr_ref, roff_ref, e2f, st, dd, *refs):
+def exchange_kernel(_, y_hbm, wy_hbm, wx_hbm, iy_hbm, ix_hbm, e2_ref,
+                    y_ref, wy_ref, wx_ref, addr_ref, roff_ref, e2f, *refs):
     y_in, iy, ix, y_send, in_sem, send_sem, recv_sem = refs
     k = lax.axis_index('cols')
     r = lax.axis_index('rows')
@@ -118,18 +118,6 @@
             e2f[j, LANES * h:LANES * h + 64, :] = v
             e2f[j, LANES * h + 64:LANES * h + LANES, 0:P_ALL] = -v[:, P_ALL:P_TWO]
             e2f[j, LANES * h + 64:LANES * h + LANES, P_ALL:P_TWO] = v[:, 0:P_ALL]
-    st[...] = jnp.zeros_like(st)
-    for s in range(2):
-        for c in range(4):
-            st[s, c, 0:Q_BLK, 0:N_IMG] = s_ref[s, :, c, :]
-
-    half_p = jnp.where(k == 0, d_ref[:, 0:P_BLK], d_ref[:, P_BLK:2 * P_BLK])
-    part_q = d_ref[:, 0:Q_BLK]
-    for i in range(1, 4):
-        part_q = jnp.where(r == i, d_ref[:, Q_BLK * i:Q_BLK * (i + 1)], part_q)
-    part_q = jnp.concatenate([part_q, jnp.zeros((1, LANES - Q_BLK), F32)], axis=1)
-    dd[...] = jnp.broadcast_to(part_q, (8, LANES)).T[0:Q_BLK, 0:1] * half_p
-
     for c in copies:
         c.wait()
 
@@ -201,7 +189,7 @@
 
 def transform_kernel(*refs):
     own, nbr = refs[:N_COPY], refs[N_COPY:N_ACC]
-    (e1_ref, e2f, st, dd, out_ref, gch, raw0, f0, f11, gps, gns, msg, recv, gpr, gnr, img, mine, psend, precv,
+    (e1_ref, e2f, s_ref, d_ref, out_ref, st, dd, gch, raw0, f0, f11, gps, gns, msg, recv, gpr, gnr, img, mine, psend, precv,
      msend_sem, mrecv_sem, gsend_sem, grecv_sem, psend_sem, precv_sem) = refs[N_ACC:]
     k = lax.axis_index('cols')
     r = lax.axis_index('rows')
@@ -291,7 +279,8 @@
         for j, sub in POSTS[chunk]:
             for i in range(3):
                 copy_of(j, sub, i, r).start()
-        recv[chunk, r] = msg[chunk, r]
+        if chunk < N_CHUNK:
+            recv[chunk, r] = msg[chunk, r]
 
     merge_all(CHUNK_TILES[0], put_chunk)
     first_dft(0, gch[...])
@@ -336,6 +325,19 @@
         gch[s, 0:LANES] = (f0[s, :] + jnp.where(lb == 0, shifted(gn, -c), 0.0)).astype(BF16)
     first_dft(N_CHUNK - 1, gch[...])
     post(N_CHUNK - 1)
+
+    d_all = d_ref[...].reshape(1, N_IMG)
+    st[...] = jnp.zeros_like(st)
+    for s in range(2):
+        for c in range(4):
+            st[s, c, 0:Q_BLK, 0:N_IMG] = s_ref[s, :, c, :]
+
+    half_p = jnp.where(k == 0, d_all[:, 0:P_BLK], d_all[:, P_BLK:2 * P_BLK])
+    part_q = d_all[:, 0:Q_BLK]
+    for i in range(1, 4):
+        part_q = jnp.where(r == i, d_all[:, Q_BLK * i:Q_BLK * (i + 1)], part_q)
+    part_q = jnp.concatenate([part_q, jnp.zeros((1, LANES - Q_BLK), F32)], axis=1)
+    dd[...] = jnp.broadcast_to(part_q, (8, LANES)).T[0:Q_BLK, 0:1] * half_p
 
     first_col = k == 0
 
@@ -370,7 +372,10 @@
             for c in range(4):
                 img[Q_PAD * c + row0:Q_PAD * c + row0 + rows] += part[rows * c:rows * (c + 1)]
             return 0
-        lax.fori_loop(N_WHOLE, N_CHUNK, accumulate, 0)
+        lax.fori_loop(N_WHOLE, N_CHUNK - 1, accumulate, 0)
+        if sub == 0:
+            post(N_CHUNK)
+        accumulate(N_CHUNK - 1, 0)
 
         x_re = jnp.zeros((rows, P_ALL), F32)
         x_im = jnp.zeros((rows, P_ALL), F32)
@@ -418,16 +423,16 @@
         samples = pl.pallas_call(
             exchange_kernel,
             out_shape=[sds((2, 8, n), F32), sds((2, 4, n), F32), sds((2, 4, n), F32), sds((2, 16, LANES), jnp.int32),
-                       sds((2, 16, LANES), jnp.int32), sds((N_CHUNK, WIDE, P_TWO), BF16), sds((2, 4, Q_PAD, P_ALL), F32), sds((Q_BLK, P_BLK), F32)],
-            in_specs=[vmem] + [hbm] * 5 + [vmem] * 3,
-            out_specs=[vmem] * 8,
+                       sds((2, 16, LANES), jnp.int32), sds((N_CHUNK, WIDE, P_TWO), BF16)],
+            in_specs=[vmem] + [hbm] * 5 + [vmem],
+            out_specs=[vmem] * 6,
             scratch_shapes=[pltpu.VMEM((2, 8, n), F32), pltpu.VMEM((16, LANES), jnp.int32), pltpu.VMEM((16, LANES), jnp.int32),
                             pltpu.VMEM((8, n), F32), pltpu.SemaphoreType.DMA((5,)), pltpu.SemaphoreType.DMA((5,)),
                             pltpu.SemaphoreType.DMA((5,))],
             compiler_params=pltpu.CompilerParams(collective_id=0, has_side_effects=True, vmem_limit_bytes=8 * MIB),
             name='exchange',
-        )(token, kspace, wts_y, wts_x, idx_y.reshape(16, LANES), idx_x.reshape(16, LANES), e2, maps, deapod.reshape(1, N_IMG))
-        y8, wy, wx, addr, roff, e2f, st, dd = samples
+        )(token, kspace, wts_y, wts_x, idx_y.reshape(16, LANES), idx_x.reshape(16, LANES), e2)
+        y8, wy, wx, addr, roff, e2f = samples
         accs = pl.pallas_call(
             spread_kernel,
             out_shape=acc_shape,
@@ -444,7 +449,7 @@
             out_shape=sds((2, P_BLK, Q_BLK), F32),
             in_specs=[vmem] * (N_ACC + 4),
             out_specs=vmem,
-            scratch_shapes=[pltpu.VMEM((KV, WIDE), BF16)] + [pltpu.VMEM((KV, LANES), F32)] * 3 + [
+            scratch_shapes=[pltpu.VMEM((2, 4, Q_PAD, P_ALL), F32), pltpu.VMEM((Q_BLK, P_BLK), F32), pltpu.VMEM((KV, WIDE), BF16)] + [pltpu.VMEM((KV, LANES), F32)] * 3 + [
                 pltpu.VMEM((Q_PAD, LANES), F32),
                 pltpu.VMEM((GN_ROWS, LANES), F32),
                 pltpu.VMEM((N_CHUNK, 4, Q_PAD, WIDE), BF16),
@@ -464,7 +469,7 @@
             ],
             compiler_params=pltpu.CompilerParams(collective_id=1, has_side_effects=True, vmem_limit_bytes=24 * MIB),
             name='transform',
-        )(*accs, e1, e2f, st, dd)
+        )(*accs, e1, e2f, maps, deapod)
 
     return jax.shard_map(
         local_fn,

time: 38.5 us -> 39.1 us (1.016)
  Pallas kernels: 36.5 us -> 38.1 us
  local copies, waits for them, and re-layouts: 1.76 us -> 0.77 us
    pallas_call x1, Pallas kernels: 22.1 us -> 23.7 us  [local_fn(): pl.pallas_call(transform_kernel, out_shape=sds((2, P_BLK, Q_BLK), F32), i...]
    reshape x1 -> x0, local copies, waits for them, and re-layouts: 0.68 us -> none  [local_fn(): deapod.reshape(1, N_IMG)]
    unnamed x17 -> x19, local copies, waits for them, and re-layouts: 1.07 us -> 0.77 us
where the time goes in v7:
time: 39.1 us; the launch traced here: 38.9 us
  Pallas kernels  38.1 us (97%)
  local copies, waits for them, and re-layouts  0.77 us (2%)
    pallas_call x1, Pallas kernels, local_fn(): pl.pallas_call(transform_kernel, out_shape=sds((2, P_BLK, Q_BLK), F32), i...  23.7 us
    pallas_call x1, Pallas kernels, local_fn(): pl.pallas_call(exchange_kernel, out_shape=[sds((2, 8, n), F32), sds((2, 4...  7.68 us
    pallas_call x1, Pallas kernels, local_fn(): pl.pallas_call(spread_kernel, out_shape=acc_shape, in_specs=[vmem] * (5 +...  5.47 us
    pallas_call x1, Pallas kernels, local_fn(): pl.pallas_call(zero_kernel, out_shape=acc_shape + [sds((8, LANES), F32)],...  1.19 us

profile of v7, /device:TPU:0, one launch (start us, length us, event | category | flops | bytes accessed | tf_op | source)
XLA Modules:
  0.0 38.9 jit_solution(7900512681583542327)
XLA Ops:
  0.0 0.0 copy-start.1
  0.0 0.0 copy-start.3
  0.0 0.0 copy-start.4
  0.0 0.0 copy-start.5
  0.0 0.0 copy-start.6
  0.0 0.0 copy-start.7
  0.0 1.2 %zero.1 = (f32[5880,128]{1,0:T(8,128)S(1)}, f32[5880,128]{1,0:T(8,128)S(1)}, f32[5880,128]{1,0:T(8,128)S(1)}, f32[5880,128]{1,0:T(8,128)S(1)}, f32[5880,128]{1,0...) custom-call(), custom_call_target="tpu_custom_call" | custom-call | flops 2000000000 | bytes 20000000 | tf_op jit(solution)/shard_map/zero/pallas_call | solution.py:415
  1.2 0.1 copy-done.1
  1.3 0.0 copy-done.3
  1.3 0.0 copy-done.4
  1.3 0.0 copy-done.5
  1.3 0.0 copy-done.6
  1.3 0.0 copy-done.7
  1.3 7.7 %exchange.1 = (f32[2,8,2048]{2,1,0:T(8,128)S(1)}, f32[2,4,2048]{2,1,0:T(4,128)S(1)}, f32[2,4,2048]{2,1,0:T(4,128)S(1)}, s32[2,16,128]{2,1,0:T(8,128)S(1)}, s32[2...) custom-call(f32[8,128]{1,0:T(8,128)S(1)} %get-tuple-element.24._, f32[2,8,2048]{2,1,0:T(8,128)S(1)} %copy-done.3, ...), custom_call_target="tpu_custom_call" | custom-call | tf_op jit(solution)/shard_map/exchange/pallas_call | solution.py:423
  9.0 0.0 copy-start
  9.0 0.0 copy-start.2
  9.0 0.0 copy-start.8
  9.0 5.5 %spread.1 = (f32[5880,128]{1,0:T(8,128)S(1)}, f32[5880,128]{1,0:T(8,128)S(1)}, f32[5880,128]{1,0:T(8,128)S(1)}, f32[5880,128]{1,0:T(8,128)S(1)}, f32[5880,128]{1,0:T(8,128)S(1)}, /*index=5*/f32[5880,128]{1,0:T(8,128)S(1)}) custom-call(s32[2,16,128]{2,1,0:T(8,128)S(1)} %get-tuple-element.25., ...), custom_call_target="tpu_custom_call", output_to_operand_aliasing={{0}: (5, {}), {1}: (6, {}), {2}: (7, {}), {3}: (8, {}), {4}... | custom-call | flops 2000000000 | bytes 20000000 | tf_op jit(solution)/shard_map/spread/pallas_call | solution.py:436
  14.5 0.0 copy-done
  14.5 0.0 copy-done.2
  14.5 0.0 copy-done.8
  14.5 23.7 %transform.1 = f32[2,184,92]{2,1,0:T(8,128)S(1)} custom-call(f32[5880,128]{1,0:T(8,128)S(1)} %get-tuple-element.36.refs_0_, f32[5880,128]{1,0:T(8,128)S(1)} %get-tuple-element.37.refs_1_, f32[5880,128]{1,0:T(8,128)S(1)} %get-tuple-element.38.refs_2_, f32[5880,128]{1,0:T(8,128)S(1)} %get-tuple-element.39.refs_3_, f32[5880,128]{1,0:T(8,128)S(1)} %get-tuple-element.40.refs_4_, ...), custom_call_target="tpu_custom_call" | custom-call | tf_op jit(solution)/shard_map/transform/pallas_call | solution.py:447
  38.3 0.7 %copy.23 = f32[2,184,92]{2,1,0:T(8,128)} copy(f32[2,184,92]{2,1,0:T(8,128)S(1)} %transform.1) | data formatting | bytes 270848
Async XLA Ops:
  0.0 1.3 %copy-start.1 = (bf16[768,768]{1,0:T(8,128)(2,1)S(1)}, bf16[768,768]{1,0:T(8,128)(2,1)}, u32[]{:S(2)}) copy-start(bf16[768,768]{1,0:T(8,128)(2,1)} %constant.6.e2_ref) | copy-start | bytes 3538948
  0.0 1.3 %copy-start.3 = (f32[2,8,2048]{2,1,0:T(8,128)S(1)}, f32[2,8,2048]{2,1,0:T(8,128)}, u32[]{:S(2)}) copy-start(f32[2,8,2048]{2,1,0:T(8,128)} %y_hbm.1) | copy-start | bytes 393220
  0.0 1.3 %copy-start.4 = (f32[4,2048]{1,0:T(4,128)S(1)}, f32[4,2048]{1,0:T(4,128)}, u32[]{:S(2)}) copy-start(f32[4,2048]{1,0:T(4,128)} %wy_hbm.1) | copy-start | bytes 98308
  0.0 1.3 %copy-start.5 = (f32[4,2048]{1,0:T(4,128)S(1)}, f32[4,2048]{1,0:T(4,128)}, u32[]{:S(2)}) copy-start(f32[4,2048]{1,0:T(4,128)} %wx_hbm.1) | copy-start | bytes 98308
  0.0 1.3 %copy-start.6 = (s32[2048]{0:T(1024)S(1)}, s32[2048]{0:T(1024)}, u32[]{:S(2)}) copy-start(s32[2048]{0:T(1024)} %param.12) | copy-start | bytes 24580
  0.0 1.3 %copy-start.7 = (s32[2048]{0:T(1024)S(1)}, s32[2048]{0:T(1024)}, u32[]{:S(2)}) copy-start(s32[2048]{0:T(1024)} %param.13) | copy-start | bytes 24580
  9.0 5.5 %copy-start = (bf16[768,768]{1,0:T(8,128)(2,1)S(1)}, bf16[768,768]{1,0:T(8,128)(2,1)}, u32[]{:S(2)}) copy-start(bf16[768,768]{1,0:T(8,128)(2,1)} %constant.7.refs_6_) | copy-start | bytes 3538948
  9.0 5.5 %copy-start.2 = (f32[2,4,368,92]{2,1,3,0:T(4,128)S(1)}, f32[2,4,368,92]{2,1,3,0:T(4,128)}, u32[]{:S(2)}) copy-start(f32[2,4,368,92]{2,1,3,0:T(4,128)} %param.14) | copy-start | bytes 3250180
  9.0 5.5 %copy-start.8 = (f32[368]{0:T(512)S(1)}, f32[368]{0:T(512)}, u32[]{:S(2)}) copy-start(f32[368]{0:T(512)} %refs_9_.1) | copy-start | bytes 4420

commit v8 on v7

--- a/solution.py
+++ b/solution.py
@@ -34,6 +34,8 @@
 WHOLE, SPLIT = range(N_WHOLE), range(N_WHOLE, N_CHUNK)
 POSTS = [[(j, FULL)] for j in WHOLE] + [[(j, 0)] for j in SPLIT]
 POSTS += [[(j, 1) for j in SPLIT]]
+LAST = N_CHUNK - 1
+SUBS_LAST = [(0, 96), (96, 48)]
 SENT = [(j, FULL) for j in WHOLE] + [(j, sub) for j in SPLIT for sub in range(2)]
 CHUNK_TILES = [(1 + 2 * j, 2 + 2 * j) for j in range(5)] + [(0, 11)]
 
@@ -62,6 +64,10 @@
             jnp.asarray(e2.reshape(N_CHUNK * LANES, P_TWO).astype(np.float32)).astype(BF16))
 
 
+def j_is_last(j):
+    return isinstance(j, int) and j == LAST
+
+
 def zero_kernel(*refs):
     *accs, token = refs
 
@@ -189,7 +195,7 @@
 
 def transform_kernel(*refs):
     own, nbr = refs[:N_COPY], refs[N_COPY:N_ACC]
-    (e1_ref, e2f, s_ref, d_ref, out_ref, st, dd, gch, raw0, f0, f11, gps, gns, msg, recv, gpr, gnr, img, mine, psend, precv,
+    (e1_ref, e2f, s_ref, d_ref, out_ref, st, dd, gch, raw0, f0, f11, gps, gns, msg, recv, msg_last, recv_last, gpr, gnr, img, mine, psend, precv,
      msend_sem, mrecv_sem, gsend_sem, grecv_sem, psend_sem, precv_sem) = refs[N_ACC:]
     k = lax.axis_index('cols')
     r = lax.axis_index('rows')
@@ -267,20 +273,37 @@
             a = ab[192 * d:192 * d + Q_PAD]
             b = ab[192 * d + Q_PAD:192 * d + 192]
             b = jnp.concatenate([pltpu.roll(b[:, :128], 64, 1), pltpu.roll(b[:, 128:], 64, 1)], axis=1)
-            msg[j, d] = jnp.where(lane < 64, a - b, a + b).astype(BF16)
+            h = jnp.where(lane < 64, a - b, a + b).astype(BF16)
+            if not j_is_last(j):
+                msg[j, d] = h
+                continue
+            for sub, (at, _) in enumerate(SUBS_LAST):
+                row0, rows = SUBS[sub]
+                half = rows // 2
+                upper = h[row0:row0 + half, LANES:WIDE]
+                lower = pltpu.roll(h[row0 + half:row0 + rows, LANES:WIDE], 8, 1)
+                msg_last[d, at:at + rows] = h[row0:row0 + rows, 0:LANES]
+                msg_last[d, at + rows:at + rows + half] = jnp.where((lane[0:half, 0:LANES] & 8) == 0, upper, lower)
 
     def copy_of(j, sub, i, slot):
         d = dests[i]
-        rows = pl.ds(*SUBS[sub])
-        return pltpu.make_async_remote_copy(src_ref=msg.at[j, d, rows], dst_ref=recv.at[j, slot, rows], send_sem=msend_sem.at[j, sub, i],
+        if j_is_last(j):
+            rows = pl.ds(*SUBS_LAST[sub])
+            src, dst = msg_last.at[d, rows], recv_last.at[slot, rows]
+        else:
+            rows = pl.ds(*SUBS[sub])
+            src, dst = msg.at[j, d, rows], recv.at[j, slot, rows]
+        return pltpu.make_async_remote_copy(src_ref=src, dst_ref=dst, send_sem=msend_sem.at[j, sub, i],
                                             recv_sem=mrecv_sem.at[j, sub, slot], device_id={'rows': d}, device_id_type=MESH)
 
     def post(chunk):
         for j, sub in POSTS[chunk]:
             for i in range(3):
                 copy_of(j, sub, i, r).start()
-        if chunk < N_CHUNK:
+        if chunk < LAST:
             recv[chunk, r] = msg[chunk, r]
+        elif chunk == LAST:
+            recv_last[r] = msg_last[r]
 
     merge_all(CHUNK_TILES[0], put_chunk)
     first_dft(0, gch[...])
@@ -323,8 +346,8 @@
     for c in range(16):
         s = slice(GN_ROWS * c, GN_ROWS * c + GN_ROWS)
         gch[s, 0:LANES] = (f0[s, :] + jnp.where(lb == 0, shifted(gn, -c), 0.0)).astype(BF16)
-    first_dft(N_CHUNK - 1, gch[...])
-    post(N_CHUNK - 1)
+    first_dft(LAST, gch[...])
+    post(LAST)
 
     d_all = d_ref[...].reshape(1, N_IMG)
     st[...] = jnp.zeros_like(st)
@@ -348,7 +371,14 @@
         coil = (lax.broadcasted_iota(jnp.int32, (rows, LANES), 1) >> 4) & 3
         halves = []
         for pair in range(2):
-            v = [recv[j, 2 * pair + t // 2, pl.ds(row0, rows), LANES * (t % 2):LANES * (t % 2 + 1)] for t in range(4)]
+            v = []
+            for src in (2 * pair, 2 * pair + 1):
+                if j_is_last(j):
+                    at = SUBS_LAST[sub][0]
+                    folded = recv_last[src, at + rows:at + rows + rows // 2]
+                    v += [recv_last[src, at:at + rows], jnp.concatenate([folded, pltpu.roll(folded, LANES - 8, 1)], axis=0)]
+                else:
+                    v += [recv[j, src, pl.ds(row0, rows), LANES * t:LANES * (t + 1)] for t in range(2)]
             for bit in (1, 2):
                 m = (coil & bit) == 0
                 for t in range(4):
@@ -372,10 +402,11 @@
             for c in range(4):
                 img[Q_PAD * c + row0:Q_PAD * c + row0 + rows] += part[rows * c:rows * (c + 1)]
             return 0
-        lax.fori_loop(N_WHOLE, N_CHUNK - 1, accumulate, 0)
+        lax.fori_loop(N_WHOLE, N_WHOLE + 1, accumulate, 0)
         if sub == 0:
             post(N_CHUNK)
-        accumulate(N_CHUNK - 1, 0)
+        lax.fori_loop(N_WHOLE + 1, LAST, accumulate, 0)
+        accumulate(LAST, 0)
 
         x_re = jnp.zeros((rows, P_ALL), F32)
         x_im = jnp.zeros((rows, P_ALL), F32)
@@ -452,8 +483,10 @@
             scratch_shapes=[pltpu.VMEM((2, 4, Q_PAD, P_ALL), F32), pltpu.VMEM((Q_BLK, P_BLK), F32), pltpu.VMEM((KV, WIDE), BF16)] + [pltpu.VMEM((KV, LANES), F32)] * 3 + [
                 pltpu.VMEM((Q_PAD, LANES), F32),
                 pltpu.VMEM((GN_ROWS, LANES), F32),
-                pltpu.VMEM((N_CHUNK, 4, Q_PAD, WIDE), BF16),
-                pltpu.VMEM((N_CHUNK, 4, Q_PAD, WIDE), BF16),
+                pltpu.VMEM((LAST, 4, Q_PAD, WIDE), BF16),
+                pltpu.VMEM((LAST, 4, Q_PAD, WIDE), BF16),
+                pltpu.VMEM((4, 144, LANES), BF16),
+                pltpu.VMEM((4, 144, LANES), BF16),
                 pltpu.VMEM((Q_PAD, LANES), F32),
                 pltpu.VMEM((GN_ROWS, LANES), F32),
                 pltpu.VMEM((4 * Q_PAD, P_TWO), F32),

time: 39.1 us -> 36.6 us (0.936)
  Pallas kernels: 38.1 us -> 35.6 us
    pallas_call x1, Pallas kernels: 23.7 us -> 21.3 us  [local_fn(): pl.pallas_call(transform_kernel, out_shape=sds((2, P_BLK, Q_BLK), F32), i...]
where the time goes in v8:
time: 36.6 us; the launch traced here: 36.5 us
  Pallas kernels  35.6 us (97%)
  local copies, waits for them, and re-layouts  0.77 us (2%)
    pallas_call x1, Pallas kernels, local_fn(): pl.pallas_call(transform_kernel, out_shape=sds((2, P_BLK, Q_BLK), F32), i...  21.3 us
    pallas_call x1, Pallas kernels, local_fn(): pl.pallas_call(exchange_kernel, out_shape=[sds((2, 8, n), F32), sds((2, 4...  7.68 us
    pallas_call x1, Pallas kernels, local_fn(): pl.pallas_call(spread_kernel, out_shape=acc_shape, in_specs=[vmem] * (5 +...  5.49 us
    pallas_call x1, Pallas kernels, local_fn(): pl.pallas_call(zero_kernel, out_shape=acc_shape + [sds((8, LANES), F32)],...  1.19 us
    unnamed x19, local copies, waits for them, and re-layouts  0.77 us

profile of v8, /device:TPU:0, one launch (start us, length us, event | category | flops | bytes accessed | tf_op | source)
XLA Modules:
  0.0 36.5 jit_solution(14301470126229430997)
XLA Ops:
  0.0 0.0 copy-start.1
  0.0 0.0 copy-start.3
  0.0 0.0 copy-start.4
  0.0 0.0 copy-start.5
  0.0 0.0 copy-start.6
  0.0 0.0 copy-start.7
  0.0 1.2 %zero.1 = (f32[5880,128]{1,0:T(8,128)S(1)}, f32[5880,128]{1,0:T(8,128)S(1)}, f32[5880,128]{1,0:T(8,128)S(1)}, f32[5880,128]{1,0:T(8,128)S(1)}, f32[5880,128]{1,0...) custom-call(), custom_call_target="tpu_custom_call" | custom-call | flops 2000000000 | bytes 20000000 | tf_op jit(solution)/shard_map/zero/pallas_call | solution.py:446
  1.2 0.1 copy-done.1
  1.3 0.0 copy-done.3
  1.3 0.0 copy-done.4
  1.3 0.0 copy-done.5
  1.3 0.0 copy-done.6
  1.3 0.0 copy-done.7
  1.3 7.7 %exchange.1 = (f32[2,8,2048]{2,1,0:T(8,128)S(1)}, f32[2,4,2048]{2,1,0:T(4,128)S(1)}, f32[2,4,2048]{2,1,0:T(4,128)S(1)}, s32[2,16,128]{2,1,0:T(8,128)S(1)}, s32[2...) custom-call(f32[8,128]{1,0:T(8,128)S(1)} %get-tuple-element.24._, f32[2,8,2048]{2,1,0:T(8,128)S(1)} %copy-done.3, ...), custom_call_target="tpu_custom_call" | custom-call | tf_op jit(solution)/shard_map/exchange/pallas_call | solution.py:454
  9.0 0.0 copy-start
  9.0 0.0 copy-start.2
  9.0 0.0 copy-start.8
  9.0 5.5 %spread.1 = (f32[5880,128]{1,0:T(8,128)S(1)}, f32[5880,128]{1,0:T(8,128)S(1)}, f32[5880,128]{1,0:T(8,128)S(1)}, f32[5880,128]{1,0:T(8,128)S(1)}, f32[5880,128]{1,0:T(8,128)S(1)}, /*index=5*/f32[5880,128]{1,0:T(8,128)S(1)}) custom-call(s32[2,16,128]{2,1,0:T(8,128)S(1)} %get-tuple-element.25., ...), custom_call_target="tpu_custom_call", output_to_operand_aliasing={{0}: (5, {}), {1}: (6, {}), {2}: (7, {}), {3}: (8, {}), {4}... | custom-call | flops 2000000000 | bytes 20000000 | tf_op jit(solution)/shard_map/spread/pallas_call | solution.py:467
  14.5 0.0 copy-done
  14.5 0.0 copy-done.2
  14.5 0.0 copy-done.8
  14.6 21.3 %transform.1 = f32[2,184,92]{2,1,0:T(8,128)S(1)} custom-call(f32[5880,128]{1,0:T(8,128)S(1)} %get-tuple-element.36.refs_0_, f32[5880,128]{1,0:T(8,128)S(1)} %get-tuple-element.37.refs_1_, f32[5880,128]{1,0:T(8,128)S(1)} %get-tuple-element.38.refs_2_, f32[5880,128]{1,0:T(8,128)S(1)} %get-tuple-element.39.refs_3_, f32[5880,128]{1,0:T(8,128)S(1)} %get-tuple-element.40.refs_4_, ...), custom_call_target="tpu_custom_call" | custom-call | tf_op jit(solution)/shard_map/transform/pallas_call | solution.py:478
  35.8 0.7 %copy.23 = f32[2,184,92]{2,1,0:T(8,128)} copy(f32[2,184,92]{2,1,0:T(8,128)S(1)} %transform.1) | data formatting | bytes 270848
Async XLA Ops:
  0.0 1.3 %copy-start.1 = (bf16[768,768]{1,0:T(8,128)(2,1)S(1)}, bf16[768,768]{1,0:T(8,128)(2,1)}, u32[]{:S(2)}) copy-start(bf16[768,768]{1,0:T(8,128)(2,1)} %constant.6.e2_ref) | copy-start | bytes 3538948
  0.0 1.3 %copy-start.3 = (f32[2,8,2048]{2,1,0:T(8,128)S(1)}, f32[2,8,2048]{2,1,0:T(8,128)}, u32[]{:S(2)}) copy-start(f32[2,8,2048]{2,1,0:T(8,128)} %y_hbm.1) | copy-start | bytes 393220
  0.0 1.3 %copy-start.4 = (f32[4,2048]{1,0:T(4,128)S(1)}, f32[4,2048]{1,0:T(4,128)}, u32[]{:S(2)}) copy-start(f32[4,2048]{1,0:T(4,128)} %wy_hbm.1) | copy-start | bytes 98308
  0.0 1.3 %copy-start.5 = (f32[4,2048]{1,0:T(4,128)S(1)}, f32[4,2048]{1,0:T(4,128)}, u32[]{:S(2)}) copy-start(f32[4,2048]{1,0:T(4,128)} %wx_hbm.1) | copy-start | bytes 98308
  0.0 1.3 %copy-start.6 = (s32[2048]{0:T(1024)S(1)}, s32[2048]{0:T(1024)}, u32[]{:S(2)}) copy-start(s32[2048]{0:T(1024)} %param.12) | copy-start | bytes 24580
  0.0 1.3 %copy-start.7 = (s32[2048]{0:T(1024)S(1)}, s32[2048]{0:T(1024)}, u32[]{:S(2)}) copy-start(s32[2048]{0:T(1024)} %param.13) | copy-start | bytes 24580
  9.0 5.5 %copy-start = (bf16[768,768]{1,0:T(8,128)(2,1)S(1)}, bf16[768,768]{1,0:T(8,128)(2,1)}, u32[]{:S(2)}) copy-start(bf16[768,768]{1,0:T(8,128)(2,1)} %constant.7.refs_6_) | copy-start | bytes 3538948
  9.0 5.5 %copy-start.2 = (f32[2,4,368,92]{2,1,3,0:T(4,128)S(1)}, f32[2,4,368,92]{2,1,3,0:T(4,128)}, u32[]{:S(2)}) copy-start(f32[2,4,368,92]{2,1,3,0:T(4,128)} %param.14) | copy-start | bytes 3250180
  9.0 5.5 %copy-start.8 = (f32[368]{0:T(512)S(1)}, f32[368]{0:T(512)}, u32[]{:S(2)}) copy-start(f32[368]{0:T(512)} %refs_9_.1) | copy-start | bytes 4420

commit v9 on v8

--- a/solution.py
+++ b/solution.py
@@ -68,26 +68,15 @@
     return isinstance(j, int) and j == LAST
 
 
-def zero_kernel(*refs):
-    *accs, token = refs
-
-    def zero(i, _):
-        for a in accs:
-            a[pl.ds(pl.multiple_of(i * VS, 8), VS), :] = jnp.zeros((VS, LANES), F32)
-        return 0
-    lax.fori_loop(0, N_SRC, zero, 0)
-    token[...] = jnp.zeros_like(token)
-
-
-def exchange_kernel(_, y_hbm, wy_hbm, wx_hbm, iy_hbm, ix_hbm, e2_ref,
-                    y_ref, wy_ref, wx_ref, addr_ref, roff_ref, e2f, *refs):
-    y_in, iy, ix, y_send, in_sem, send_sem, recv_sem = refs
+def exchange_kernel(y_hbm, wy_hbm, wx_hbm, iy_hbm, ix_hbm, e2_hbm, y_ref, wy_ref, wx_ref, addr_ref, roff_ref, e2f, *refs):
+    accs = refs[:N_ACC]
+    e2_ref, y_in, iy, ix, y_send, in_sem, send_sem, recv_sem = refs[N_ACC:]
     k = lax.axis_index('cols')
     r = lax.axis_index('rows')
     other = {'cols': 1 - k}
     barrier = pltpu.get_barrier_semaphore()
     pl.semaphore_signal(barrier, inc=1, device_id=other, device_id_type=MESH)
-    loads = [(iy_hbm, iy), (ix_hbm, ix), (y_hbm, y_in), (wy_hbm, wy_ref.at[0]), (wx_hbm, wx_ref.at[0])]
+    loads = [(iy_hbm, iy), (ix_hbm, ix), (y_hbm, y_in), (wy_hbm, wy_ref.at[0]), (wx_hbm, wx_ref.at[0]), (e2_hbm, e2_ref)]
     loads = [pltpu.make_async_copy(a, b, in_sem.at[i]) for i, (a, b) in enumerate(loads)]
     for c in loads:
         c.start()
@@ -98,6 +87,10 @@
         c.start()
         return c
 
+    loads[3].wait()
+    loads[4].wait()
+    pl.semaphore_wait(barrier, 1)
+    copies = [send(0, wy_ref.at[0], wy_ref.at[1]), send(1, wx_ref.at[0], wx_ref.at[1])]
     loads[0].wait()
     loads[1].wait()
     row = iy[...] - r * ROW_BLK
@@ -112,12 +105,14 @@
     high = jnp.concatenate([y_re[4:8], y_im[4:8]], axis=0)
     y_ref[0] = jnp.where(k == 0, low, high)
     y_send[...] = jnp.where(k == 0, high, low)
-    loads[3].wait()
-    loads[4].wait()
-    pl.semaphore_wait(barrier, 1)
-    copies = [send(0, wy_ref.at[0], wy_ref.at[1]), send(1, wx_ref.at[0], wx_ref.at[1]), send(2, addr_ref.at[0], addr_ref.at[1]),
-              send(3, roff_ref.at[0], roff_ref.at[1]), send(4, y_send, y_ref.at[1])]
-
+    copies += [send(2, addr_ref.at[0], addr_ref.at[1]), send(3, roff_ref.at[0], roff_ref.at[1]), send(4, y_send, y_ref.at[1])]
+
+    def zero(i, _):
+        for a in accs:
+            a[pl.ds(pl.multiple_of(i * VS, 8), VS), :] = jnp.zeros((VS, LANES), F32)
+        return 0
+    lax.fori_loop(0, N_SRC, zero, 0)
+    loads[-1].wait()
     for j in range(N_CHUNK):
         for h in range(2):
             v = e2_ref[LANES * j + 64 * h:LANES * j + 64 * h + 64, :]
@@ -443,27 +438,20 @@
         e1, e2 = dft_constants()
         maps = jnp.transpose(coil_maps, (0, 3, 1, 2))
         acc_shape = [sds((N_SRC * VS, LANES), F32)] * (N_ACC)
-        *accs, token = pl.pallas_call(
-            zero_kernel,
-            out_shape=acc_shape + [sds((8, LANES), F32)],
-            out_specs=[vmem] * (N_ACC + 1),
-            compiler_params=pltpu.CompilerParams(vmem_limit_bytes=MIB),
-            cost_estimate=pl.CostEstimate(flops=2 * 10**9, bytes_accessed=2 * 10**7, transcendentals=0),
-            name='zero',
-        )()
-        samples = pl.pallas_call(
+        inputs = (kspace, wts_y, wts_x, idx_y.reshape(16, LANES), idx_x.reshape(16, LANES), e2)
+        *samples, = pl.pallas_call(
             exchange_kernel,
             out_shape=[sds((2, 8, n), F32), sds((2, 4, n), F32), sds((2, 4, n), F32), sds((2, 16, LANES), jnp.int32),
-                       sds((2, 16, LANES), jnp.int32), sds((N_CHUNK, WIDE, P_TWO), BF16)],
-            in_specs=[vmem] + [hbm] * 5 + [vmem],
-            out_specs=[vmem] * 6,
-            scratch_shapes=[pltpu.VMEM((2, 8, n), F32), pltpu.VMEM((16, LANES), jnp.int32), pltpu.VMEM((16, LANES), jnp.int32),
-                            pltpu.VMEM((8, n), F32), pltpu.SemaphoreType.DMA((5,)), pltpu.SemaphoreType.DMA((5,)),
+                       sds((2, 16, LANES), jnp.int32), sds((N_CHUNK, WIDE, P_TWO), BF16)] + acc_shape,
+            in_specs=[hbm] * 6,
+            out_specs=[vmem] * (6 + N_ACC),
+            scratch_shapes=[pltpu.VMEM((KV, P_TWO), BF16), pltpu.VMEM((2, 8, n), F32), pltpu.VMEM((16, LANES), jnp.int32), pltpu.VMEM((16, LANES), jnp.int32),
+                            pltpu.VMEM((8, n), F32), pltpu.SemaphoreType.DMA((6,)), pltpu.SemaphoreType.DMA((5,)),
                             pltpu.SemaphoreType.DMA((5,))],
             compiler_params=pltpu.CompilerParams(collective_id=0, has_side_effects=True, vmem_limit_bytes=8 * MIB),
             name='exchange',
-        )(token, kspace, wts_y, wts_x, idx_y.reshape(16, LANES), idx_x.reshape(16, LANES), e2)
-        y8, wy, wx, addr, roff, e2f = samples
+        )(*[pltpu.with_memory_space_constraint(x, pltpu.HBM) for x in inputs])
+        y8, wy, wx, addr, roff, e2f = samples[:6]
         accs = pl.pallas_call(
             spread_kernel,
             out_shape=acc_shape,
@@ -474,7 +462,7 @@
             compiler_params=pltpu.CompilerParams(vmem_limit_bytes=8 * MIB),
             cost_estimate=pl.CostEstimate(flops=2 * 10**9, bytes_accessed=2 * 10**7, transcendentals=0),
             name='spread',
-        )(addr, y8, wy, wx, roff, *accs)
+        )(addr, y8, wy, wx, roff, *samples[6:])
         return pl.pallas_call(
             transform_kernel,
             out_shape=sds((2, P_BLK, Q_BLK), F32),

time: 36.6 us -> 35.3 us (0.964)
  Pallas kernels: 35.6 us -> 34.4 us
    pallas_call x1 -> x0, Pallas kernels: 1.19 us -> none  [local_fn(): pl.pallas_call(zero_kernel, out_shape=acc_shape + [sds((8, LANES), F32)],...]
    pallas_call x1, Pallas kernels: 21.3 us -> 20.7 us  [local_fn(): pl.pallas_call(transform_kernel, out_shape=sds((2, P_BLK, Q_BLK), F32), i...]
    pallas_call x1, Pallas kernels: 7.68 us -> 8.22 us  [local_fn(): pl.pallas_call(exchange_kernel, out_shape=[sds((2, 8, n), F32), sds((2, 4...]
    unnamed x19 -> x7, local copies, waits for them, and re-layouts: 0.77 us -> 0.7 us
where the time goes in v9:
time: 35.3 us; the launch traced here: 35.2 us
  Pallas kernels  34.4 us (97%)
  local copies, waits for them, and re-layouts  0.7 us (2%)
    pallas_call x1, Pallas kernels, local_fn(): pl.pallas_call(transform_kernel, out_shape=sds((2, P_BLK, Q_BLK), F32), i...  20.7 us
    pallas_call x1, Pallas kernels, local_fn(): pl.pallas_call(exchange_kernel, out_shape=[sds((2, 8, n), F32), sds((2, 4...  8.22 us
    pallas_call x1, Pallas kernels, local_fn(): pl.pallas_call(spread_kernel, out_shape=acc_shape, in_specs=[vmem] * (5 +...  5.51 us

profile of v9, /device:TPU:0, one launch (start us, length us, event | category | flops | bytes accessed | tf_op | source)
XLA Modules:
  0.0 35.2 jit_solution(15219296921372748961)
XLA Ops:
  0.0 8.2 %exchange.1 = (f32[2,8,2048]{2,1,0:T(8,128)S(1)}, f32[2,4,2048]{2,1,0:T(4,128)S(1)}, f32[2,4,2048]{2,1,0:T(4,128)S(1)}, s32[2,16,128]{2,1,0:T(8,128)S(1)}, s32[2...) custom-call(f32[2,8,2048]{2,1,0:T(8,128)} %y_hbm.1, ...), custom_call_target="tpu_custom_call" | custom-call | tf_op jit(solution)/shard_map/exchange/pallas_call | solution.py:442
  8.2 0.0 copy-start
  8.2 0.0 copy-start.1
  8.3 0.0 copy-start.2
  8.3 5.5 %spread.1 = (f32[5880,128]{1,0:T(8,128)S(1)}, f32[5880,128]{1,0:T(8,128)S(1)}, f32[5880,128]{1,0:T(8,128)S(1)}, f32[5880,128]{1,0:T(8,128)S(1)}, f32[5880,128]{1,0:T(8,128)S(1)}, /*index=5*/f32[5880,128]{1,0:T(8,128)S(1)}) custom-call(s32[2,16,128]{2,1,0:T(8,128)S(1)} %get-tuple-element.23., ...), custom_call_target="tpu_custom_call", output_to_operand_aliasing={{0}: (5, {}), {1}: (6, {}), {2}: (7, {}), {3}: (8, {}), {4}... | custom-call | flops 2000000000 | bytes 20000000 | tf_op jit(solution)/shard_map/spread/pallas_call | solution.py:455
  13.8 0.0 copy-done
  13.8 0.0 copy-done.1
  13.8 0.0 copy-done.2
  13.8 20.7 %transform.1 = f32[2,184,92]{2,1,0:T(8,128)S(1)} custom-call(f32[5880,128]{1,0:T(8,128)S(1)} %get-tuple-element.34.refs_0_, f32[5880,128]{1,0:T(8,128)S(1)} %get-tuple-element.35.refs_1_, f32[5880,128]{1,0:T(8,128)S(1)} %get-tuple-element.36.refs_2_, f32[5880,128]{1,0:T(8,128)S(1)} %get-tuple-element.37.refs_3_, f32[5880,128]{1,0:T(8,128)S(1)} %get-tuple-element.38.refs_4_, ...), custom_call_target="tpu_custom_call" | custom-call | tf_op jit(solution)/shard_map/transform/pallas_call | solution.py:466
  34.5 0.7 %copy.23 = f32[2,184,92]{2,1,0:T(8,128)} copy(f32[2,184,92]{2,1,0:T(8,128)S(1)} %transform.1) | data formatting | bytes 270848
Async XLA Ops:
  8.2 5.6 %copy-start = (bf16[768,768]{1,0:T(8,128)(2,1)S(1)}, bf16[768,768]{1,0:T(8,128)(2,1)}, u32[]{:S(2)}) copy-start(bf16[768,768]{1,0:T(8,128)(2,1)} %constant.7.refs_6_) | copy-start | bytes 3538948
  8.2 5.6 %copy-start.1 = (f32[2,4,368,92]{2,1,3,0:T(4,128)S(1)}, f32[2,4,368,92]{2,1,3,0:T(4,128)}, u32[]{:S(2)}) copy-start(f32[2,4,368,92]{2,1,3,0:T(4,128)} %param.14) | copy-start | bytes 3250180
  8.3 5.6 %copy-start.2 = (f32[368]{0:T(512)S(1)}, f32[368]{0:T(512)}, u32[]{:S(2)}) copy-start(f32[368]{0:T(512)} %refs_9_.1) | copy-start | bytes 4420

commit v10 on v9

--- a/solution.py
+++ b/solution.py
@@ -68,7 +68,7 @@
     return isinstance(j, int) and j == LAST
 
 
-def exchange_kernel(y_hbm, wy_hbm, wx_hbm, iy_hbm, ix_hbm, e2_hbm, y_ref, wy_ref, wx_ref, addr_ref, roff_ref, e2f, *refs):
+def exchange_kernel(y_hbm, wy_hbm, wx_hbm, iy_hbm, ix_hbm, e2_hbm, y_ref, wy_ref, wx_ref, place_ref, e2f, *refs):
     accs = refs[:N_ACC]
     e2_ref, y_in, iy, ix, y_send, in_sem, send_sem, recv_sem = refs[N_ACC:]
     k = lax.axis_index('cols')
@@ -97,15 +97,14 @@
     tile = jnp.zeros_like(row)
     for t in range(1, N_SRC):
         tile = tile + jnp.where(row >= STRIDE_U * t, 1, 0)
-    addr_ref[0] = tile * VS + (ix[...] - k * COL_BLK)
-    roff_ref[0] = (row + 14) & 15
+    place_ref[0] = (tile * VS + (ix[...] - k * COL_BLK)) * ROWS + ((row + 14) & 15)
     loads[2].wait()
     y_re, y_im = y_in[0], y_in[1]
     low = jnp.concatenate([y_re[0:4], y_im[0:4]], axis=0)
     high = jnp.concatenate([y_re[4:8], y_im[4:8]], axis=0)
     y_ref[0] = jnp.where(k == 0, low, high)
     y_send[...] = jnp.where(k == 0, high, low)
-    copies += [send(2, addr_ref.at[0], addr_ref.at[1]), send(3, roff_ref.at[0], roff_ref.at[1]), send(4, y_send, y_ref.at[1])]
+    copies += [send(2, place_ref.at[0], place_ref.at[1]), send(3, y_send, y_ref.at[1])]
 
     def zero(i, _):
         for a in accs:
@@ -130,11 +129,13 @@
     return [hi, mid, rest - mid]
 
 
-def spread_kernel(addr_ref, y_ref, wy_ref, wx_ref, roff_ref, *refs):
+def spread_kernel(place_ref, y_ref, wy_ref, wx_ref, *refs):
     accs = refs[N_ACC:4 * N_COPY]
-    addr, sem = refs[4 * N_COPY], refs[-1]
-    q_refs = refs[4 * N_COPY + 1:-1]
-    to_smem = pltpu.make_async_copy(addr_ref, addr, sem)
+    addr, addr_v, roff, sem, *q_refs = refs[4 * N_COPY:]
+    place = place_ref[...]
+    addr_v[...] = place >> 4
+    roff[...] = place & 15
+    to_smem = pltpu.make_async_copy(addr_v, addr, sem)
     to_smem.start()
     n = y_ref.shape[2]
 
@@ -150,7 +151,7 @@
         ds = [pl.ds(pl.multiple_of((i + n_blk * h) * LANES, LANES), LANES) for h in range(2)]
         y = jnp.concatenate([y_ref[slot, :, s] for s in ds], axis=1)
         wy = jnp.concatenate([wy_ref[slot, :, s] for s in ds], axis=1)
-        d = (rr - jnp.concatenate([roff_ref[slot, pl.ds(i + n_blk * h, 1), :] for h in range(2)], axis=1)) & 15
+        d = (rr - jnp.concatenate([roff[slot, pl.ds(i + n_blk * h, 1), :] for h in range(2)], axis=1)) & 15
         w16 = jnp.zeros((ROWS, WIDE), F32)
         for a in range(4):
             w16 = jnp.where(d == a, wy[a:a + 1], w16)
@@ -170,9 +171,12 @@
                     acc = accs[slot * N_COPY + (2 * j + h) % N_COPY]
                     base = addr[slot, i + n_blk * h, j] + (0 if h else 4)
                     q = jnp.broadcast_to(qs[slot][j + LANES * h:j + LANES * h + 1, :], (8, LANES))
-                    s = pl.ds(base, 8)
-                    c = jnp.where(top, 0.0, cols[slot]) if h else jnp.where(top, cols[slot], 0.0)
-                    acc[s, :] = acc[s, :] + c * q
+                    if h:
+                        s = pl.ds(base, 8)
+                        acc[s, :] = acc[s, :] + jnp.where(top, 0.0, cols[slot]) * q
+                    else:
+                        s = pl.ds(base, 4)
+                        acc[s, :] = acc[s, :] + cols[slot][0:4] * q[0:4]
 
     qa, qb = q_refs[:2], q_refs[2:]
     for slot in range(2):
@@ -422,9 +426,12 @@
             copy_of(j, sub, i, r).wait_send()
     for sub in range(2):
         swap(sub).wait()
-    total = mine[...] + precv[...]
-    out_ref[0] = (total[0:Q_BLK, 0:P_BLK] * dd[...]).T
-    out_ref[1] = (total[0:Q_BLK, P_PAD:P_PAD + P_BLK] * dd[...]).T
+        row0, rows = SUBS[sub]
+        rows = min(rows, Q_BLK - row0)
+        s = slice(row0, row0 + rows)
+        total = mine[s] + precv[s]
+        for i in range(2):
+            out_ref[i, :, s] = (total[:, P_PAD * i:P_PAD * i + P_BLK] * dd[s]).T
 
 
 def solution(mesh):
@@ -442,27 +449,28 @@
         *samples, = pl.pallas_call(
             exchange_kernel,
             out_shape=[sds((2, 8, n), F32), sds((2, 4, n), F32), sds((2, 4, n), F32), sds((2, 16, LANES), jnp.int32),
-                       sds((2, 16, LANES), jnp.int32), sds((N_CHUNK, WIDE, P_TWO), BF16)] + acc_shape,
+                       sds((N_CHUNK, WIDE, P_TWO), BF16)] + acc_shape,
             in_specs=[hbm] * 6,
-            out_specs=[vmem] * (6 + N_ACC),
+            out_specs=[vmem] * (5 + N_ACC),
             scratch_shapes=[pltpu.VMEM((KV, P_TWO), BF16), pltpu.VMEM((2, 8, n), F32), pltpu.VMEM((16, LANES), jnp.int32), pltpu.VMEM((16, LANES), jnp.int32),
-                            pltpu.VMEM((8, n), F32), pltpu.SemaphoreType.DMA((6,)), pltpu.SemaphoreType.DMA((5,)),
-                            pltpu.SemaphoreType.DMA((5,))],
+                            pltpu.VMEM((8, n), F32), pltpu.SemaphoreType.DMA((6,)), pltpu.SemaphoreType.DMA((4,)),
+                            pltpu.SemaphoreType.DMA((4,))],
             compiler_params=pltpu.CompilerParams(collective_id=0, has_side_effects=True, vmem_limit_bytes=8 * MIB),
             name='exchange',
         )(*[pltpu.with_memory_space_constraint(x, pltpu.HBM) for x in inputs])
-        y8, wy, wx, addr, roff, e2f = samples[:6]
+        y8, wy, wx, place, e2f = samples[:5]
         accs = pl.pallas_call(
             spread_kernel,
             out_shape=acc_shape,
-            in_specs=[vmem] * (5 + N_ACC),
+            in_specs=[vmem] * (4 + N_ACC),
             out_specs=[vmem] * (N_ACC),
-            scratch_shapes=[pltpu.SMEM((2, 16, LANES), jnp.int32)] + [pltpu.VMEM((WIDE, LANES), F32)] * 4 + [pltpu.SemaphoreType.DMA],
-            input_output_aliases={5 + i: i for i in range(N_ACC)},
+            scratch_shapes=[pltpu.SMEM((2, 16, LANES), jnp.int32), pltpu.VMEM((2, 16, LANES), jnp.int32), pltpu.VMEM((2, 16, LANES), jnp.int32),
+                            pltpu.SemaphoreType.DMA] + [pltpu.VMEM((WIDE, LANES), F32)] * 4,
+            input_output_aliases={4 + i: i for i in range(N_ACC)},
             compiler_params=pltpu.CompilerParams(vmem_limit_bytes=8 * MIB),
             cost_estimate=pl.CostEstimate(flops=2 * 10**9, bytes_accessed=2 * 10**7, transcendentals=0),
             name='spread',
-        )(addr, y8, wy, wx, roff, *samples[6:])
+        )(place, y8, wy, wx, *samples[5:])
         return pl.pallas_call(
             transform_kernel,
             out_shape=sds((2, P_BLK, Q_BLK), F32),

time: 35.3 us -> 35.1 us (level)
  no operation moved by 1% of the time
where the time goes in v10:
time: 35.1 us; the launch traced here: 35 us
  Pallas kernels  34.3 us (98%)
  local copies, waits for them, and re-layouts  0.7 us (2%)
    pallas_call x1, Pallas kernels, local_fn(): pl.pallas_call(transform_kernel, out_shape=sds((2, P_BLK, Q_BLK), F32), i...  20.8 us
    pallas_call x1, Pallas kernels, local_fn(): pl.pallas_call(exchange_kernel, out_shape=[sds((2, 8, n), F32), sds((2, 4...  8.03 us
    pallas_call x1, Pallas kernels, local_fn(): pl.pallas_call(spread_kernel, out_shape=acc_shape, in_specs=[vmem] * (4 +...  5.43 us

profile of v10, /device:TPU:0, one launch (start us, length us, event | category | flops | bytes accessed | tf_op | source)
XLA Modules:
  0.0 35.0 jit_solution(7155564772301184929)
XLA Ops:
  0.0 8.0 %exchange.1 = (f32[2,8,2048]{2,1,0:T(8,128)S(1)}, f32[2,4,2048]{2,1,0:T(4,128)S(1)}, f32[2,4,2048]{2,1,0:T(4,128)S(1)}, s32[2,16,128]{2,1,0:T(8,128)S(1)}, bf16[...) custom-call(f32[2,8,2048]{2,1,0:T(8,128)} %y_hbm.1, ...), custom_call_target="tpu_custom_call" | custom-call | tf_op jit(solution)/shard_map/exchange/pallas_call | solution.py:449
  8.0 0.0 copy-start
  8.1 0.0 copy-start.1
  8.1 0.0 copy-start.2
  8.1 5.4 %spread.1 = (f32[5880,128]{1,0:T(8,128)S(1)}, f32[5880,128]{1,0:T(8,128)S(1)}, f32[5880,128]{1,0:T(8,128)S(1)}, f32[5880,128]{1,0:T(8,128)S(1)}, f32[5880,128]{1,0:T(8,128)S(1)}, /*index=5*/f32[5880,128]{1,0:T(8,128)S(1)}) custom-call(s32[2,16,128]{2,1,0:T(8,128)S(1)} %get-tuple-element.22., ...), custom_call_target="tpu_custom_call", output_to_operand_aliasing={{0}: (4, {}), {1}: (5, {}), {2}: (6, {}), {3}: (7, {}), {4}... | custom-call | flops 2000000000 | bytes 20000000 | tf_op jit(solution)/shard_map/spread/pallas_call | solution.py:462
  13.5 0.0 copy-done
  13.5 0.0 copy-done.1
  13.5 0.0 copy-done.2
  13.5 20.8 %transform.1 = f32[2,184,92]{2,1,0:T(8,128)S(1)} custom-call(f32[5880,128]{1,0:T(8,128)S(1)} %get-tuple-element.32.refs_0_, f32[5880,128]{1,0:T(8,128)S(1)} %get-tuple-element.33.refs_1_, f32[5880,128]{1,0:T(8,128)S(1)} %get-tuple-element.34.refs_2_, f32[5880,128]{1,0:T(8,128)S(1)} %get-tuple-element.35.refs_3_, f32[5880,128]{1,0:T(8,128)S(1)} %get-tuple-element.36.refs_4_, ...), custom_call_target="tpu_custom_call" | custom-call | tf_op jit(solution)/shard_map/transform/pallas_call | solution.py:474
  34.4 0.7 %copy.23 = f32[2,184,92]{2,1,0:T(8,128)} copy(f32[2,184,92]{2,1,0:T(8,128)S(1)} %transform.1) | data formatting | bytes 270848
Async XLA Ops:
  8.0 5.5 %copy-start = (bf16[768,768]{1,0:T(8,128)(2,1)S(1)}, bf16[768,768]{1,0:T(8,128)(2,1)}, u32[]{:S(2)}) copy-start(bf16[768,768]{1,0:T(8,128)(2,1)} %constant.7.refs_6_) | copy-start | bytes 3538948
  8.1 5.5 %copy-start.1 = (f32[2,4,368,92]{2,1,3,0:T(4,128)S(1)}, f32[2,4,368,92]{2,1,3,0:T(4,128)}, u32[]{:S(2)}) copy-start(f32[2,4,368,92]{2,1,3,0:T(4,128)} %param.14) | copy-start | bytes 3250180
  8.1 5.5 %copy-start.2 = (f32[368]{0:T(512)S(1)}, f32[368]{0:T(512)}, u32[]{:S(2)}) copy-start(f32[368]{0:T(512)} %refs_9_.1) | copy-start | bytes 4420

commit v11 on v10

--- a/solution.py
+++ b/solution.py
@@ -68,9 +68,9 @@
     return isinstance(j, int) and j == LAST
 
 
-def exchange_kernel(y_hbm, wy_hbm, wx_hbm, iy_hbm, ix_hbm, e2_hbm, y_ref, wy_ref, wx_ref, place_ref, e2f, *refs):
+def exchange_kernel(y_hbm, wy_hbm, wx_hbm, iy_hbm, ix_hbm, e2_hbm, y_ref, wy_ref, wx_ref, place_ref, e2f, q_own, *refs):
     accs = refs[:N_ACC]
-    e2_ref, y_in, iy, ix, y_send, in_sem, send_sem, recv_sem = refs[N_ACC:]
+    e2_ref, y_in, iy, ix, roff, y_send, in_sem, send_sem, recv_sem = refs[N_ACC:]
     k = lax.axis_index('cols')
     r = lax.axis_index('rows')
     other = {'cols': 1 - k}
@@ -97,7 +97,8 @@
     tile = jnp.zeros_like(row)
     for t in range(1, N_SRC):
         tile = tile + jnp.where(row >= STRIDE_U * t, 1, 0)
-    place_ref[0] = (tile * VS + (ix[...] - k * COL_BLK)) * ROWS + ((row + 14) & 15)
+    roff[0] = (row + 14) & 15
+    place_ref[0] = (tile * VS + (ix[...] - k * COL_BLK)) * ROWS + roff[0]
     loads[2].wait()
     y_re, y_im = y_in[0], y_in[1]
     low = jnp.concatenate([y_re[0:4], y_im[0:4]], axis=0)
@@ -111,6 +112,12 @@
             a[pl.ds(pl.multiple_of(i * VS, 8), VS), :] = jnp.zeros((VS, LANES), F32)
         return 0
     lax.fori_loop(0, N_SRC, zero, 0)
+    expand = expansion()
+
+    def own_rows(i, _):
+        q_own[pl.ds(pl.multiple_of(i * WIDE, WIDE), WIDE), :] = sample_rows(expand, i, 0, y_ref, wy_ref, roff)
+        return 0
+    lax.fori_loop(0, y_ref.shape[2] // WIDE, own_rows, 0)
     loads[-1].wait()
     for j in range(N_CHUNK):
         for h in range(2):
@@ -129,7 +136,30 @@
     return [hi, mid, rest - mid]
 
 
-def spread_kernel(place_ref, y_ref, wy_ref, wx_ref, *refs):
+def expansion():
+    r0 = lax.broadcasted_iota(jnp.int32, (80, WIDE), 0)
+    l0 = lax.broadcasted_iota(jnp.int32, (80, WIDE), 1)
+    ry = (r0 < 24) & (l0 < LANES) & ((r0 & 7) == (l0 >> 4))
+    rw = (r0 >= 24) & (r0 < 72) & (l0 >= LANES) & (((r0 - 24) & 15) == (l0 & 15))
+    return jnp.where(ry | rw, 1.0, 0.0).astype(BF16)
+
+
+def sample_rows(expand, i, slot, y_ref, wy_ref, roff):
+    n_blk = y_ref.shape[2] // WIDE
+    rr = lax.broadcasted_iota(jnp.int32, (ROWS, WIDE), 0)
+    ds = [pl.ds(pl.multiple_of((i + n_blk * h) * LANES, LANES), LANES) for h in range(2)]
+    y = jnp.concatenate([y_ref[slot, :, s] for s in ds], axis=1)
+    wy = jnp.concatenate([wy_ref[slot, :, s] for s in ds], axis=1)
+    d = (rr - jnp.concatenate([roff[slot, pl.ds(i + n_blk * h, 1), :] for h in range(2)], axis=1)) & 15
+    w16 = jnp.zeros((ROWS, WIDE), F32)
+    for a in range(4):
+        w16 = jnp.where(d == a, wy[a:a + 1], w16)
+    lhs = jnp.concatenate(split3(y) + split3(w16) + [jnp.zeros((8, WIDE), F32)], axis=0).astype(BF16)
+    o = lax.dot_general(lhs, expand, (((0,), (0,)), ((), ())), preferred_element_type=F32)
+    return o[:, :LANES] * o[:, LANES:]
+
+
+def spread_kernel(place_ref, y_ref, wy_ref, wx_ref, q_own, *refs):
     accs = refs[N_ACC:4 * N_COPY]
     addr, addr_v, roff, sem, *q_refs = refs[4 * N_COPY:]
     place = place_ref[...]
@@ -139,29 +169,17 @@
     to_smem.start()
     n = y_ref.shape[2]
 
-    r0 = lax.broadcasted_iota(jnp.int32, (80, WIDE), 0)
-    l0 = lax.broadcasted_iota(jnp.int32, (80, WIDE), 1)
-    ry = (r0 < 24) & (l0 < LANES) & ((r0 & 7) == (l0 >> 4))
-    rw = (r0 >= 24) & (r0 < 72) & (l0 >= LANES) & (((r0 - 24) & 15) == (l0 & 15))
-    expand = jnp.where(ry | rw, 1.0, 0.0).astype(BF16)
-    rr = lax.broadcasted_iota(jnp.int32, (ROWS, WIDE), 0)
     n_blk = n // WIDE
 
+    expand = expansion()
+
     def prep(i, slot, q_ref):
-        ds = [pl.ds(pl.multiple_of((i + n_blk * h) * LANES, LANES), LANES) for h in range(2)]
-        y = jnp.concatenate([y_ref[slot, :, s] for s in ds], axis=1)
-        wy = jnp.concatenate([wy_ref[slot, :, s] for s in ds], axis=1)
-        d = (rr - jnp.concatenate([roff[slot, pl.ds(i + n_blk * h, 1), :] for h in range(2)], axis=1)) & 15
-        w16 = jnp.zeros((ROWS, WIDE), F32)
-        for a in range(4):
-            w16 = jnp.where(d == a, wy[a:a + 1], w16)
-        lhs = jnp.concatenate(split3(y) + split3(w16) + [jnp.zeros((8, WIDE), F32)], axis=0).astype(BF16)
-        o = lax.dot_general(lhs, expand, (((0,), (0,)), ((), ())), preferred_element_type=F32)
-        q_ref[...] = o[:, :LANES] * o[:, LANES:]
+        q_ref[...] = sample_rows(expand, i, slot, y_ref, wy_ref, roff)
 
     top = lax.broadcasted_iota(jnp.int32, (8, LANES), 0) < 4
 
-    def scatter(i, qs):
+    def scatter(i, q_nbr):
+        first = pl.multiple_of(i * WIDE, WIDE)
         ds = [pl.ds(pl.multiple_of((i + n_blk * h) * LANES, LANES), LANES) for h in range(2)]
         wx = [jnp.concatenate([wx_ref[slot, :, s] for s in ds], axis=0) for slot in range(2)]
         for j in range(LANES):
@@ -170,7 +188,8 @@
                 for slot in range(2):
                     acc = accs[slot * N_COPY + (2 * j + h) % N_COPY]
                     base = addr[slot, i + n_blk * h, j] + (0 if h else 4)
-                    q = jnp.broadcast_to(qs[slot][j + LANES * h:j + LANES * h + 1, :], (8, LANES))
+                    at = j + LANES * h
+                    q = jnp.broadcast_to(q_nbr[at:at + 1, :] if slot else q_own[pl.ds(first + at, 1), :], (8, LANES))
                     if h:
                         s = pl.ds(base, 8)
                         acc[s, :] = acc[s, :] + jnp.where(top, 0.0, cols[slot]) * q
@@ -178,15 +197,13 @@
                         s = pl.ds(base, 4)
                         acc[s, :] = acc[s, :] + cols[slot][0:4] * q[0:4]
 
-    qa, qb = q_refs[:2], q_refs[2:]
-    for slot in range(2):
-        prep(0, slot, qa[slot])
+    qa, qb = q_refs
+    prep(0, 1, qa)
     to_smem.wait()
 
     def two_blocks(i, _):
         for step, now, then in ((0, qa, qb), (1, qb, qa)):
-            for slot in range(2):
-                prep(lax.rem(2 * i + step + 1, n_blk), slot, then[slot])
+            prep(lax.rem(2 * i + step + 1, n_blk), 1, then)
             scatter(2 * i + step, now)
         return 0
     lax.fori_loop(0, n_blk // 2, two_blocks, 0)
@@ -449,28 +466,29 @@
         *samples, = pl.pallas_call(
             exchange_kernel,
             out_shape=[sds((2, 8, n), F32), sds((2, 4, n), F32), sds((2, 4, n), F32), sds((2, 16, LANES), jnp.int32),
-                       sds((N_CHUNK, WIDE, P_TWO), BF16)] + acc_shape,
+                       sds((N_CHUNK, WIDE, P_TWO), BF16), sds((n, LANES), F32)] + acc_shape,
             in_specs=[hbm] * 6,
-            out_specs=[vmem] * (5 + N_ACC),
+            out_specs=[vmem] * (6 + N_ACC),
             scratch_shapes=[pltpu.VMEM((KV, P_TWO), BF16), pltpu.VMEM((2, 8, n), F32), pltpu.VMEM((16, LANES), jnp.int32), pltpu.VMEM((16, LANES), jnp.int32),
+                            pltpu.VMEM((1, 16, LANES), jnp.int32),
                             pltpu.VMEM((8, n), F32), pltpu.SemaphoreType.DMA((6,)), pltpu.SemaphoreType.DMA((4,)),
                             pltpu.SemaphoreType.DMA((4,))],
             compiler_params=pltpu.CompilerParams(collective_id=0, has_side_effects=True, vmem_limit_bytes=8 * MIB),
             name='exchange',
         )(*[pltpu.with_memory_space_constraint(x, pltpu.HBM) for x in inputs])
-        y8, wy, wx, place, e2f = samples[:5]
+        y8, wy, wx, place, e2f, q_own = samples[:6]
         accs = pl.pallas_call(
             spread_kernel,
             out_shape=acc_shape,
-            in_specs=[vmem] * (4 + N_ACC),
+            in_specs=[vmem] * (5 + N_ACC),
             out_specs=[vmem] * (N_ACC),
             scratch_shapes=[pltpu.SMEM((2, 16, LANES), jnp.int32), pltpu.VMEM((2, 16, LANES), jnp.int32), pltpu.VMEM((2, 16, LANES), jnp.int32),
-                            pltpu.SemaphoreType.DMA] + [pltpu.VMEM((WIDE, LANES), F32)] * 4,
-            input_output_aliases={4 + i: i for i in range(N_ACC)},
+                            pltpu.SemaphoreType.DMA] + [pltpu.VMEM((WIDE, LANES), F32)] * 2,
+            input_output_aliases={5 + i: i for i in range(N_ACC)},
             compiler_params=pltpu.CompilerParams(vmem_limit_bytes=8 * MIB),
             cost_estimate=pl.CostEstimate(flops=2 * 10**9, bytes_accessed=2 * 10**7, transcendentals=0),
             name='spread',
-        )(place, y8, wy, wx, *samples[5:])
+        )(place, y8, wy, wx, q_own, *samples[6:])
         return pl.pallas_call(
             transform_kernel,
             out_shape=sds((2, P_BLK, Q_BLK), F32),

time: 35.1 us -> 35.1 us (level)
  no operation moved by 1% of the time
where the time goes in v11:
time: 35.1 us; the launch traced here: 35 us
  Pallas kernels  34.2 us (97%)
  local copies, waits for them, and re-layouts  0.7 us (2%)
    pallas_call x1, Pallas kernels, local_fn(): pl.pallas_call(transform_kernel, out_shape=sds((2, P_BLK, Q_BLK), F32), i...  20.8 us
    pallas_call x1, Pallas kernels, local_fn(): pl.pallas_call(exchange_kernel, out_shape=[sds((2, 8, n), F32), sds((2, 4...  8.03 us
    pallas_call x1, Pallas kernels, local_fn(): pl.pallas_call(spread_kernel, out_shape=acc_shape, in_specs=[vmem] * (5 +...  5.38 us

profile of v11, /device:TPU:0, one launch (start us, length us, event | category | flops | bytes accessed | tf_op | source)
XLA Modules:
  0.0 35.0 jit_solution(14163190543682435604)
XLA Ops:
  0.0 8.0 %exchange.1 = (f32[2,8,2048]{2,1,0:T(8,128)S(1)}, f32[2,4,2048]{2,1,0:T(4,128)S(1)}, f32[2,4,2048]{2,1,0:T(4,128)S(1)}, s32[2,16,128]{2,1,0:T(8,128)S(1)}, bf16[...) custom-call(f32[2,8,2048]{2,1,0:T(8,128)} %y_hbm.1, ...), custom_call_target="tpu_custom_call" | custom-call | tf_op jit(solution)/shard_map/exchange/pallas_call | solution.py:466
  8.0 0.0 copy-start
  8.1 0.0 copy-start.1
  8.1 0.0 copy-start.2
  8.1 5.4 %spread.1 = (f32[5880,128]{1,0:T(8,128)S(1)}, f32[5880,128]{1,0:T(8,128)S(1)}, f32[5880,128]{1,0:T(8,128)S(1)}, f32[5880,128]{1,0:T(8,128)S(1)}, f32[5880,128]{1,0:T(8,128)S(1)}, /*index=5*/f32[5880,128]{1,0:T(8,128)S(1)}) custom-call(s32[2,16,128]{2,1,0:T(8,128)S(1)} %get-tuple-element.23., ...), custom_call_target="tpu_custom_call", output_to_operand_aliasing={{0}: (5, {}), {1}: (6, {}), {2}: (7, {}), {3}: (8, {}), {4}... | custom-call | flops 2000000000 | bytes 20000000 | tf_op jit(solution)/shard_map/spread/pallas_call | solution.py:480
  13.5 0.0 copy-done
  13.5 0.0 copy-done.1
  13.5 0.0 copy-done.2
  13.5 20.8 %transform.1 = f32[2,184,92]{2,1,0:T(8,128)S(1)} custom-call(f32[5880,128]{1,0:T(8,128)S(1)} %get-tuple-element.34.refs_0_, f32[5880,128]{1,0:T(8,128)S(1)} %get-tuple-element.35.refs_1_, f32[5880,128]{1,0:T(8,128)S(1)} %get-tuple-element.36.refs_2_, f32[5880,128]{1,0:T(8,128)S(1)} %get-tuple-element.37.refs_3_, f32[5880,128]{1,0:T(8,128)S(1)} %get-tuple-element.38.refs_4_, ...), custom_call_target="tpu_custom_call" | custom-call | tf_op jit(solution)/shard_map/transform/pallas_call | solution.py:492
  34.3 0.7 %copy.23 = f32[2,184,92]{2,1,0:T(8,128)} copy(f32[2,184,92]{2,1,0:T(8,128)S(1)} %transform.1) | data formatting | bytes 270848
Async XLA Ops:
  8.0 5.4 %copy-start = (bf16[768,768]{1,0:T(8,128)(2,1)S(1)}, bf16[768,768]{1,0:T(8,128)(2,1)}, u32[]{:S(2)}) copy-start(bf16[768,768]{1,0:T(8,128)(2,1)} %constant.7.refs_6_) | copy-start | bytes 3538948
  8.1 5.4 %copy-start.1 = (f32[2,4,368,92]{2,1,3,0:T(4,128)S(1)}, f32[2,4,368,92]{2,1,3,0:T(4,128)}, u32[]{:S(2)}) copy-start(f32[2,4,368,92]{2,1,3,0:T(4,128)} %param.14) | copy-start | bytes 3250180
  8.1 5.4 %copy-start.2 = (f32[368]{0:T(512)S(1)}, f32[368]{0:T(512)}, u32[]{:S(2)}) copy-start(f32[368]{0:T(512)} %refs_9_.1) | copy-start | bytes 4420

commit v12 on v11

--- a/solution.py
+++ b/solution.py
@@ -283,6 +283,15 @@
         return pltpu.make_async_remote_copy(src_ref=psend.at[rows], dst_ref=precv.at[rows], send_sem=psend_sem.at[sub],
                                             recv_sem=precv_sem.at[sub], device_id={'cols': 1 - k}, device_id_type=MESH)
 
+    def first_dft_of(j, g, which):
+        rows = pl.ds(pl.multiple_of(P_ALL * which, P_ALL), P_ALL)
+        ab = jnp.dot(e1_ref[rows, :], g, preferred_element_type=F32)
+        for d in range(2):
+            a = ab[P_PAD * d:P_PAD * d + Q_PAD]
+            b = ab[P_PAD * d + Q_PAD:P_PAD * (d + 1)]
+            b = jnp.concatenate([pltpu.roll(b[:, :LANES], 64, 1), pltpu.roll(b[:, LANES:], 64, 1)], axis=1)
+            msg[j, 2 * which + d] = jnp.where(lane < 64, a - b, a + b).astype(BF16)
+
     def first_dft(j, g):
         ab = jnp.dot(e1_ref[...], g, preferred_element_type=F32)
         for d in range(4):
@@ -322,9 +331,13 @@
             recv_last[r] = msg_last[r]
 
     merge_all(CHUNK_TILES[0], put_chunk)
-    first_dft(0, gch[...])
+    first_dft_of(0, gch[...], 1 - chip)
     pl.semaphore_wait(barrier, 4)
-    post(0)
+    for i in range(2):
+        copy_of(0, FULL, i, r).start()
+    first_dft_of(0, gch[...], chip)
+    copy_of(0, FULL, 2, r).start()
+    recv[0, r] = msg[0, r]
 
     merge_all((None, 0, N_TGT - 1), put_edges)
     la = lax.broadcasted_iota(jnp.int32, (Q_PAD, LANES), 1) & 15

time: 35.1 us -> 35.1 us (level)
  no operation moved by 1% of the time
where the time goes in v12:
time: 35.1 us; the launch traced here: 35 us
  Pallas kernels  34.3 us (98%)
  local copies, waits for them, and re-layouts  0.7 us (2%)
    pallas_call x1, Pallas kernels, local_fn(): pl.pallas_call(transform_kernel, out_shape=sds((2, P_BLK, Q_BLK), F32), i...  20.9 us
    pallas_call x1, Pallas kernels, local_fn(): pl.pallas_call(exchange_kernel, out_shape=[sds((2, 8, n), F32), sds((2, 4...  8.03 us
    pallas_call x1, Pallas kernels, local_fn(): pl.pallas_call(spread_kernel, out_shape=acc_shape, in_specs=[vmem] * (5 +...  5.38 us

profile of v12, /device:TPU:0, one launch (start us, length us, event | category | flops | bytes accessed | tf_op | source)
XLA Modules:
  0.0 35.0 jit_solution(15575343929599410648)
XLA Ops:
  0.0 8.0 %exchange.1 = (f32[2,8,2048]{2,1,0:T(8,128)S(1)}, f32[2,4,2048]{2,1,0:T(4,128)S(1)}, f32[2,4,2048]{2,1,0:T(4,128)S(1)}, s32[2,16,128]{2,1,0:T(8,128)S(1)}, bf16[...) custom-call(f32[2,8,2048]{2,1,0:T(8,128)} %y_hbm.1, ...), custom_call_target="tpu_custom_call" | custom-call | tf_op jit(solution)/shard_map/exchange/pallas_call | solution.py:479
  8.0 0.0 copy-start
  8.1 0.0 copy-start.1
  8.1 0.0 copy-start.2
  8.1 5.4 %spread.1 = (f32[5880,128]{1,0:T(8,128)S(1)}, f32[5880,128]{1,0:T(8,128)S(1)}, f32[5880,128]{1,0:T(8,128)S(1)}, f32[5880,128]{1,0:T(8,128)S(1)}, f32[5880,128]{1,0:T(8,128)S(1)}, /*index=5*/f32[5880,128]{1,0:T(8,128)S(1)}) custom-call(s32[2,16,128]{2,1,0:T(8,128)S(1)} %get-tuple-element.23., ...), custom_call_target="tpu_custom_call", output_to_operand_aliasing={{0}: (5, {}), {1}: (6, {}), {2}: (7, {}), {3}: (8, {}), {4}... | custom-call | flops 2000000000 | bytes 20000000 | tf_op jit(solution)/shard_map/spread/pallas_call | solution.py:493
  13.5 0.0 copy-done
  13.5 0.0 copy-done.1
  13.5 0.0 copy-done.2
  13.5 20.9 %transform.1 = f32[2,184,92]{2,1,0:T(8,128)S(1)} custom-call(f32[5880,128]{1,0:T(8,128)S(1)} %get-tuple-element.34.refs_0_, f32[5880,128]{1,0:T(8,128)S(1)} %get-tuple-element.35.refs_1_, f32[5880,128]{1,0:T(8,128)S(1)} %get-tuple-element.36.refs_2_, f32[5880,128]{1,0:T(8,128)S(1)} %get-tuple-element.37.refs_3_, f32[5880,128]{1,0:T(8,128)S(1)} %get-tuple-element.38.refs_4_, ...), custom_call_target="tpu_custom_call" | custom-call | tf_op jit(solution)/shard_map/transform/pallas_call | solution.py:505
  34.4 0.7 %copy.23 = f32[2,184,92]{2,1,0:T(8,128)} copy(f32[2,184,92]{2,1,0:T(8,128)S(1)} %transform.1) | data formatting | bytes 270848
Async XLA Ops:
  8.0 5.4 %copy-start = (bf16[768,768]{1,0:T(8,128)(2,1)S(1)}, bf16[768,768]{1,0:T(8,128)(2,1)}, u32[]{:S(2)}) copy-start(bf16[768,768]{1,0:T(8,128)(2,1)} %constant.7.refs_6_) | copy-start | bytes 3538948
  8.1 5.4 %copy-start.1 = (f32[2,4,368,92]{2,1,3,0:T(4,128)S(1)}, f32[2,4,368,92]{2,1,3,0:T(4,128)}, u32[]{:S(2)}) copy-start(f32[2,4,368,92]{2,1,3,0:T(4,128)} %param.14) | copy-start | bytes 3250180
  8.1 5.4 %copy-start.2 = (f32[368]{0:T(512)S(1)}, f32[368]{0:T(512)}, u32[]{:S(2)}) copy-start(f32[368]{0:T(512)} %refs_9_.1) | copy-start | bytes 4420

commit v13 on v11

--- a/solution.py
+++ b/solution.py
@@ -78,8 +78,8 @@
     pl.semaphore_signal(barrier, inc=1, device_id=other, device_id_type=MESH)
     loads = [(iy_hbm, iy), (ix_hbm, ix), (y_hbm, y_in), (wy_hbm, wy_ref.at[0]), (wx_hbm, wx_ref.at[0]), (e2_hbm, e2_ref)]
     loads = [pltpu.make_async_copy(a, b, in_sem.at[i]) for i, (a, b) in enumerate(loads)]
-    for c in loads:
-        c.start()
+    for i in (3, 4, 0, 1, 2):
+        loads[i].start()
 
     def send(i, src, dst):
         c = pltpu.make_async_remote_copy(src_ref=src, dst_ref=dst, send_sem=send_sem.at[i], recv_sem=recv_sem.at[i],
@@ -106,6 +106,7 @@
     y_ref[0] = jnp.where(k == 0, low, high)
     y_send[...] = jnp.where(k == 0, high, low)
     copies += [send(2, place_ref.at[0], place_ref.at[1]), send(3, y_send, y_ref.at[1])]
+    loads[-1].start()
 
     def zero(i, _):
         for a in accs:

time: 35.1 us -> 35.1 us (level)
  no operation moved by 1% of the time
where the time goes in v13:
time: 35.1 us; the launch traced here: 35 us
  Pallas kernels  34.2 us (97%)
  local copies, waits for them, and re-layouts  0.7 us (2%)
    pallas_call x1, Pallas kernels, local_fn(): pl.pallas_call(transform_kernel, out_shape=sds((2, P_BLK, Q_BLK), F32), i...  20.9 us
    pallas_call x1, Pallas kernels, local_fn(): pl.pallas_call(exchange_kernel, out_shape=[sds((2, 8, n), F32), sds((2, 4...  7.94 us
    pallas_call x1, Pallas kernels, local_fn(): pl.pallas_call(spread_kernel, out_shape=acc_shape, in_specs=[vmem] * (5 +...  5.38 us

profile of v13, /device:TPU:0, one launch (start us, length us, event | category | flops | bytes accessed | tf_op | source)
XLA Modules:
  0.0 35.0 jit_solution(2780211922235245563)
XLA Ops:
  0.0 7.9 %exchange.1 = (f32[2,8,2048]{2,1,0:T(8,128)S(1)}, f32[2,4,2048]{2,1,0:T(4,128)S(1)}, f32[2,4,2048]{2,1,0:T(4,128)S(1)}, s32[2,16,128]{2,1,0:T(8,128)S(1)}, bf16[...) custom-call(f32[2,8,2048]{2,1,0:T(8,128)} %y_hbm.1, ...), custom_call_target="tpu_custom_call" | custom-call | tf_op jit(solution)/shard_map/exchange/pallas_call | solution.py:467
  7.9 0.0 copy-start
  8.0 0.0 copy-start.1
  8.0 0.0 copy-start.2
  8.0 5.4 %spread.1 = (f32[5880,128]{1,0:T(8,128)S(1)}, f32[5880,128]{1,0:T(8,128)S(1)}, f32[5880,128]{1,0:T(8,128)S(1)}, f32[5880,128]{1,0:T(8,128)S(1)}, f32[5880,128]{1,0:T(8,128)S(1)}, /*index=5*/f32[5880,128]{1,0:T(8,128)S(1)}) custom-call(s32[2,16,128]{2,1,0:T(8,128)S(1)} %get-tuple-element.23., ...), custom_call_target="tpu_custom_call", output_to_operand_aliasing={{0}: (5, {}), {1}: (6, {}), {2}: (7, {}), {3}: (8, {}), {4}... | custom-call | flops 2000000000 | bytes 20000000 | tf_op jit(solution)/shard_map/spread/pallas_call | solution.py:481
  13.4 0.0 copy-done
  13.4 0.0 copy-done.1
  13.4 0.0 copy-done.2
  13.4 20.9 %transform.1 = f32[2,184,92]{2,1,0:T(8,128)S(1)} custom-call(f32[5880,128]{1,0:T(8,128)S(1)} %get-tuple-element.34.refs_0_, f32[5880,128]{1,0:T(8,128)S(1)} %get-tuple-element.35.refs_1_, f32[5880,128]{1,0:T(8,128)S(1)} %get-tuple-element.36.refs_2_, f32[5880,128]{1,0:T(8,128)S(1)} %get-tuple-element.37.refs_3_, f32[5880,128]{1,0:T(8,128)S(1)} %get-tuple-element.38.refs_4_, ...), custom_call_target="tpu_custom_call" | custom-call | tf_op jit(solution)/shard_map/transform/pallas_call | solution.py:493
  34.3 0.7 %copy.23 = f32[2,184,92]{2,1,0:T(8,128)} copy(f32[2,184,92]{2,1,0:T(8,128)S(1)} %transform.1) | data formatting | bytes 270848
Async XLA Ops:
  7.9 5.4 %copy-start = (bf16[768,768]{1,0:T(8,128)(2,1)S(1)}, bf16[768,768]{1,0:T(8,128)(2,1)}, u32[]{:S(2)}) copy-start(bf16[768,768]{1,0:T(8,128)(2,1)} %constant.7.refs_6_) | copy-start | bytes 3538948
  8.0 5.4 %copy-start.1 = (f32[2,4,368,92]{2,1,3,0:T(4,128)S(1)}, f32[2,4,368,92]{2,1,3,0:T(4,128)}, u32[]{:S(2)}) copy-start(f32[2,4,368,92]{2,1,3,0:T(4,128)} %param.14) | copy-start | bytes 3250180
  8.0 5.4 %copy-start.2 = (f32[368]{0:T(512)S(1)}, f32[368]{0:T(512)}, u32[]{:S(2)}) copy-start(f32[368]{0:T(512)} %refs_9_.1) | copy-start | bytes 4420

commit v14 on v13

--- a/solution.py
+++ b/solution.py
@@ -217,7 +217,7 @@
     k = lax.axis_index('cols')
     r = lax.axis_index('rows')
     chip, core = r // 2, r % 2
-    dests = [2 * (1 - chip) + core, 2 * (1 - chip) + (1 - core), 2 * chip + (1 - core)]
+    dests = [2 * (1 - chip) + (1 - core), 2 * (1 - chip) + core, 2 * chip + (1 - core)]
     nxt, prv = lax.rem(r + 1, 4), lax.rem(r + 3, 4)
     barrier = pltpu.get_barrier_semaphore()
     for d in dests:

time: 35.1 us -> 35.3 us (level)
  no operation moved by 1% of the time
where the time goes in v14:
time: 35.3 us; the launch traced here: 35.2 us
  Pallas kernels  34.4 us (97%)
  local copies, waits for them, and re-layouts  0.7 us (2%)
    pallas_call x1, Pallas kernels, local_fn(): pl.pallas_call(transform_kernel, out_shape=sds((2, P_BLK, Q_BLK), F32), i...  21.1 us
    pallas_call x1, Pallas kernels, local_fn(): pl.pallas_call(exchange_kernel, out_shape=[sds((2, 8, n), F32), sds((2, 4...  7.94 us
    pallas_call x1, Pallas kernels, local_fn(): pl.pallas_call(spread_kernel, out_shape=acc_shape, in_specs=[vmem] * (5 +...  5.39 us

profile of v14, /device:TPU:0, one launch (start us, length us, event | category | flops | bytes accessed | tf_op | source)
XLA Modules:
  0.0 35.2 jit_solution(1107058416472922244)
XLA Ops:
  0.0 7.9 %exchange.1 = (f32[2,8,2048]{2,1,0:T(8,128)S(1)}, f32[2,4,2048]{2,1,0:T(4,128)S(1)}, f32[2,4,2048]{2,1,0:T(4,128)S(1)}, s32[2,16,128]{2,1,0:T(8,128)S(1)}, bf16[...) custom-call(f32[2,8,2048]{2,1,0:T(8,128)} %y_hbm.1, ...), custom_call_target="tpu_custom_call" | custom-call | tf_op jit(solution)/shard_map/exchange/pallas_call | solution.py:467
  7.9 0.0 copy-start
  8.0 0.0 copy-start.1
  8.0 0.0 copy-start.2
  8.0 5.4 %spread.1 = (f32[5880,128]{1,0:T(8,128)S(1)}, f32[5880,128]{1,0:T(8,128)S(1)}, f32[5880,128]{1,0:T(8,128)S(1)}, f32[5880,128]{1,0:T(8,128)S(1)}, f32[5880,128]{1,0:T(8,128)S(1)}, /*index=5*/f32[5880,128]{1,0:T(8,128)S(1)}) custom-call(s32[2,16,128]{2,1,0:T(8,128)S(1)} %get-tuple-element.23., ...), custom_call_target="tpu_custom_call", output_to_operand_aliasing={{0}: (5, {}), {1}: (6, {}), {2}: (7, {}), {3}: (8, {}), {4}... | custom-call | flops 2000000000 | bytes 20000000 | tf_op jit(solution)/shard_map/spread/pallas_call | solution.py:481
  13.4 0.0 copy-done
  13.4 0.0 copy-done.1
  13.4 0.0 copy-done.2
  13.4 21.1 %transform.1 = f32[2,184,92]{2,1,0:T(8,128)S(1)} custom-call(f32[5880,128]{1,0:T(8,128)S(1)} %get-tuple-element.34.refs_0_, f32[5880,128]{1,0:T(8,128)S(1)} %get-tuple-element.35.refs_1_, f32[5880,128]{1,0:T(8,128)S(1)} %get-tuple-element.36.refs_2_, f32[5880,128]{1,0:T(8,128)S(1)} %get-tuple-element.37.refs_3_, f32[5880,128]{1,0:T(8,128)S(1)} %get-tuple-element.38.refs_4_, ...), custom_call_target="tpu_custom_call" | custom-call | tf_op jit(solution)/shard_map/transform/pallas_call | solution.py:493
  34.5 0.7 %copy.23 = f32[2,184,92]{2,1,0:T(8,128)} copy(f32[2,184,92]{2,1,0:T(8,128)S(1)} %transform.1) | data formatting | bytes 270848
Async XLA Ops:
  7.9 5.4 %copy-start = (bf16[768,768]{1,0:T(8,128)(2,1)S(1)}, bf16[768,768]{1,0:T(8,128)(2,1)}, u32[]{:S(2)}) copy-start(bf16[768,768]{1,0:T(8,128)(2,1)} %constant.7.refs_6_) | copy-start | bytes 3538948
  8.0 5.4 %copy-start.1 = (f32[2,4,368,92]{2,1,3,0:T(4,128)S(1)}, f32[2,4,368,92]{2,1,3,0:T(4,128)}, u32[]{:S(2)}) copy-start(f32[2,4,368,92]{2,1,3,0:T(4,128)} %param.14) | copy-start | bytes 3250180
  8.0 5.4 %copy-start.2 = (f32[368]{0:T(512)S(1)}, f32[368]{0:T(512)}, u32[]{:S(2)}) copy-start(f32[368]{0:T(512)} %refs_9_.1) | copy-start | bytes 4420
